TPU v7x, 32 devices: a whole 2x2x4 slice. The times are simulated.
32 devices in a mesh: queue: 8 (over z, y), batch: 4 (over x, core).
Axes of the slice: x: 2, y: 2, z: 4, core: 2. Of those that a mesh axis runs over, the one named last changes fastest.
Arguments:
- queries: bfloat16 [4096, 256], P(('queue', 'batch')), may hold values from -160 to 160
- keys: bfloat16 [4096, 256], P(('queue', 'batch')), may hold values from -0.5 to 0.5
- queue_keys: bfloat16 [32768, 256], P('queue'), may hold values from -2 to 2
- log_scale: float32 [1], replicated, may hold values from 0 to 1
- write_pointer: int32 [1], replicated, may hold values from 0 to 255
- block_order: int32 [32], replicated, may hold values from 0 to 31, each once
- pos_index: int32 [4096], P(('queue', 'batch')), may hold values from 0 to 127
Outputs:
- loss: float32 [4096], P(('queue', 'batch'))
- temp_grad: float32 [1], replicated
- new_queue: bfloat16 [32768, 256], P('queue')
Inputs may be any that keep to these rules, and one draw needn't show every extreme that they name: `block_order`: each number of 0 to 31 appears once.
All inputs are finite; a program needn't handle non-finite values.
Results may differ from a plain program's by a relative error of at most 0.0004.
Values may be sent and summed in bfloat16 or wider, within the bound.
No kernel may reach another device: no remote copies, remote signals or barrier semaphores. Data moves between devices by JAX's collectives and lax.ppermute only.
A program may use at most 64 MiB of HBM per device.

v0:
```python
import jax
import jax.numpy as jnp
from jax import lax
from jax.sharding import PartitionSpec as P

BLOCK = 128


def block_stats(query_block, shard_keys, scale):
    logits = scale * lax.dot_general(
        query_block, shard_keys, (((1,), (1,)), ((), ())), preferred_element_type=jnp.float32
    )
    highest = jnp.max(logits, axis=1)
    weights = jnp.exp(logits - highest[:, None])
    return (highest, jnp.sum(weights, axis=1), jnp.sum(weights * logits, axis=1))


def per_device(queries, keys, queue_keys, log_scale, write_pointer, block_order, pos_index):
    scale = jnp.exp(log_scale[0])
    tok_rows = queries.shape[0]
    width = queries.shape[1]
    group_size = lax.axis_size("queue")
    my_index = lax.axis_index("queue")
    gathered_rows = tok_rows * group_size

    def absorb(piece):
        count = piece.shape[0]
        blocks = piece.reshape(count // 512, 512, width)
        stats = lax.map(lambda block_rows: block_stats(block_rows, queue_keys, scale), blocks)
        stats = tuple((item.reshape(count) for item in stats))
        return tuple((fresh for fresh in stats))

    peak, total, weighted = absorb(lax.all_gather(queries, "queue", axis=0, tiled=True))
    parts = tuple((item.reshape(group_size, tok_rows) for item in (peak, total, weighted)))
    got_peak, got_total, got_weighted = lax.all_to_all(
        parts, "queue", split_axis=0, concat_axis=0, tiled=True
    )
    peak = jnp.max(got_peak, axis=0)
    factor = jnp.exp(got_peak - peak[None, :])
    total = jnp.sum(got_total * factor, axis=0)
    weighted = jnp.sum(got_weighted * factor, axis=0)
    local_scores = lax.dot_general(
        queries, keys, (((1,), (1,)), ((), ())), preferred_element_type=jnp.float32
    )
    columns = lax.broadcasted_iota(jnp.int32, local_scores.shape, 1)
    pos = scale * jnp.sum(jnp.where(columns == pos_index[:, None], local_scores, 0.0), axis=1)
    highest = jnp.maximum(peak, pos)
    factor = jnp.exp(peak - highest)
    own_weight = jnp.exp(pos - highest)
    final_total = total * factor + own_weight
    final_weighted = weighted * factor + pos * own_weight
    lse = highest + jnp.log(final_total)
    loss = lse - pos
    terms = final_weighted / final_total - pos
    summed = lax.psum(jnp.sum(terms), ("queue", "batch"))
    temp_grad = (summed / (gathered_rows * lax.axis_size("batch"))).reshape(1)
    per_dev = queue_keys.shape[0] // BLOCK
    total_blocks = per_dev * group_size
    pointer = write_pointer[0]
    initial = queue_keys.reshape(per_dev, BLOCK, width)
    piece = lax.all_gather(keys, ("queue", "batch"), axis=0, tiled=True)
    count = piece.shape[0] // BLOCK
    local = (pointer + block_order) % total_blocks - my_index * per_dev
    hits = local[:, None] == jnp.arange(per_dev, dtype=jnp.int32)[None, :]
    moved = jnp.einsum(
        "cs,crd->srd",
        hits.astype(jnp.bfloat16),
        piece.reshape(count, BLOCK, width),
        preferred_element_type=jnp.float32,
    ).astype(jnp.bfloat16)
    updated = jnp.where(jnp.any(hits, axis=0)[:, None, None], moved, initial)
    new_queue = updated.reshape(per_dev * BLOCK, width)
    return (loss, temp_grad, new_queue)


def solution(mesh):
    placed = (
        P(("queue", "batch"), None),
        P(("queue", "batch"), None),
        P("queue", None),
        P(),
        P(),
        P(),
        P(("queue", "batch")),
    )
    return jax.shard_map(
        per_device,
        mesh=mesh,
        in_specs=placed,
        out_specs=(P(("queue", "batch")), P(), P("queue", None)),
        check_vma=False,
    )
```

profile of v0, /device:TPU:0, one launch (start us, length us, event | category | flops | bytes accessed | tf_op | source)
XLA Modules:
  0.0 140.9 jit_solution(15826687093977612357)
XLA Ops:
  7.2 0.0 all-gather.2.cloned.1.call-start
  7.2 0.7 all-gather.2.cloned.1.call-update
  8.6 33.6 %all_gather.6 = bf16[1024,256]{1,0:T(8,128)(2,1)S(1)} all-gather(bf16[128,256]{1,0:T(8,128)(2,1)} %param.9), channel_id=1, replica_groups=mesh['queue'=8,'batch'=4] {'queue'}, dimensions={0}, use_global_device_ids=true | all-gather | bytes 589824 | tf_op jit(solution)/shard_map/all_gather | solution.py:33
  42.2 0.0 copy-start.2
  42.3 0.0 copy-start
  42.3 0.0 copy-start.1
  42.3 0.0 copy-start.3
  42.3 11.1 %while.14 = (s32[]{:T(128)}, f32[2,512]{1,0:T(2,128)S(1)}, f32[2,512]{1,0:T(2,128)S(1)}, f32[2,512]{1,0:T(2,128)S(1)}, f32[]{:T(128)}, /*index=5*/bf16[2,512,256...) while((s32[]{:T(128)}, f32[2,512]{1,0:T(2,128)S(1)}, f32[2,512]{1,0:T(2,128)S(1)}, ...), condition=%wide.region_4.5_spmd, body=%wide.region_0.4_spmd.sunk | while | flops 1088420352 | bytes 19157108 | solution.py:29
  42.3 3.0 %multiply_reduce_fusion.6 = (f32[512]{0:T(512)S(1)}, f32[512,4096]{1,0:T(8,128)S(1)}) fusion(f32[]{:T(128)} %get-tuple-element.140, bf16[4096,256]{1,0:T(8,128)(2,1)} %get-tuple-element.142, bf16[2,512,256]{2,1,0:T(8,128)(2,1)S(1)} %get-tuple-element.141, s32[]{:T(128)} %get-tuple-element.127), kind=kOutput, calls=%fused_computation.3.clone.1 | convolution fusion | flops 1077935616 | bytes 10749960 | tf_op jit(solution)/shard_map/while/body/eval_jaxpr/dot_general | solution.py:10
  45.3 2.4 %multiply_reduce_fusion.7 = (f32[512]{0:T(512)S(1)}, f32[512]{0:T(512)S(1)}) fusion(f32[512,4096]{1,0:T(8,128)S(1)} %get-tuple-element.115, f32[512]{0:T(512)S(1)} %get-tuple-element.114, f32[]{:T(128)} %get-tuple-element.140), kind=kLoop, calls=%fused_computation.clone.1 | loop fusion | flops 10484736 | bytes 8394756 | tf_op jit(solution)/shard_map/while/body/eval_jaxpr/reduce_sum | solution.py:15
  47.9 3.0 %multiply_reduce_fusion.6 = (f32[512]{0:T(512)S(1)}, f32[512,4096]{1,0:T(8,128)S(1)}) fusion(f32[]{:T(128)} %get-tuple-element.140, bf16[4096,256]{1,0:T(8,128)(2,1)} %get-tuple-element.142, bf16[2,512,256]{2,1,0:T(8,128)(2,1)S(1)} %get-tuple-element.141, s32[]{:T(128)} %get-tuple-element.127), kind=kOutput, calls=%fused_computation.3.clone.1 | convolution fusion | flops 1077935616 | bytes 10749960 | tf_op jit(solution)/shard_map/while/body/eval_jaxpr/dot_general | solution.py:10
  50.9 2.4 %multiply_reduce_fusion.7 = (f32[512]{0:T(512)S(1)}, f32[512]{0:T(512)S(1)}) fusion(f32[512,4096]{1,0:T(8,128)S(1)} %get-tuple-element.115, f32[512]{0:T(512)S(1)} %get-tuple-element.114, f32[]{:T(128)} %get-tuple-element.140), kind=kLoop, calls=%fused_computation.clone.1 | loop fusion | flops 10484736 | bytes 8394756 | tf_op jit(solution)/shard_map/while/body/eval_jaxpr/reduce_sum | solution.py:15
  53.4 0.6 all_to_all.24
  54.0 5.3 %all-to-all-start = ((f32[8,1,128]{2,1,0:T(1,128)}), f32[8,1,128]{2,1,0:T(1,128)S(1)}, u32[]{:S(2)}, u32[]{:S(2)}) async-start(f32[8,1,128]{2,1,0:T(1,128)} %all_to_all.24), calls=%async_computation | async-start | bytes 8192 | tf_op jit(solution)/shard_map/all_to_all | solution.py:35
  60.0 0.0 copy-done.2
  60.0 0.6 all_to_all.26
  60.6 5.1 %all-to-all-done = f32[8,1,128]{2,1,0:T(1,128)S(1)} async-done(((f32[8,1,128]{2,1,0:T(1,128)}), f32[8,1,128]{2,1,0:T(1,128)S(1)}, u32[]{:S(2)}, u32[]{:S(2)}) %all-to-all-start) | async-done | bytes 4128 | tf_op jit(solution)/shard_map/all_to_all | solution.py:35
  65.7 3.3 %all-to-all-start.1 = ((f32[8,1,128]{2,1,0:T(1,128)}), f32[8,1,128]{2,1,0:T(1,128)S(1)}, u32[]{:S(2)}, u32[]{:S(2)}) async-start(f32[8,1,128]{2,1,0:T(1,128)} %all_to_all.26), calls=%async_computation.1 | async-start | bytes 8192 | tf_op jit(solution)/shard_map/all_to_all | solution.py:35
  69.0 0.0 copy-done
  69.0 0.0 copy-done.1
  69.0 0.0 copy-done.3
  69.0 0.2 fusion.9
  69.2 0.6 all_to_all.30
  69.8 5.6 %all-to-all-done.1 = f32[8,1,128]{2,1,0:T(1,128)S(1)} async-done(((f32[8,1,128]{2,1,0:T(1,128)}), f32[8,1,128]{2,1,0:T(1,128)S(1)}, u32[]{:S(2)}, u32[]{:S(2)}) %all-to-all-start.1) | async-done | bytes 4128 | tf_op jit(solution)/shard_map/all_to_all | solution.py:35
  75.4 3.3 %all-to-all-start.2 = ((f32[8,1,128]{2,1,0:T(1,128)}), f32[8,1,128]{2,1,0:T(1,128)S(1)}, u32[]{:S(2)}, u32[]{:S(2)}) async-start(f32[8,1,128]{2,1,0:T(1,128)} %all_to_all.30), calls=%async_computation.2 | async-start | bytes 8192 | tf_op jit(solution)/shard_map/all_to_all | solution.py:35
  78.8 0.1 fusion.11
  78.9 6.2 %all-to-all-done.2 = f32[8,1,128]{2,1,0:T(1,128)S(1)} async-done(((f32[8,1,128]{2,1,0:T(1,128)}), f32[8,1,128]{2,1,0:T(1,128)S(1)}, u32[]{:S(2)}, u32[]{:S(2)}) %all-to-all-start.2) | async-done | bytes 4128 | tf_op jit(solution)/shard_map/all_to_all | solution.py:35
  85.1 1.1 subtract_reduce_fusion
  86.3 38.4 %psum.7 = f32[]{:T(128)} all-reduce(f32[]{:T(128)} %get-tuple-element.65), channel_id=1, replica_groups=mesh['queue'=8,'batch'=4] {'queue','batch'}, use_global_device_ids=true, to_apply=%region_10.11 | all-reduce | flops 1 | bytes 8 | tf_op jit(solution)/shard_map/psum | solution.py:55
  125.3 0.0 all-gather.2.cloned.1.call-done
  125.4 5.0 %copy_select_fusion = bf16[32,128,256]{2,0,1:T(8,128)(2,1)S(1)} fusion(bf16[32,128,256]{2,1,0:T(8,128)(2,1)} %bitcast.35, pred[32]{0:T(512)(128)(4,1)S(1)} %fusion.11, bf16[32,128,256]{2,1,0:T(8,128)(2,1)} %bitcast.44, s32[32]{0:T(128)S(1)} %fusion.14), kind=kOutput, calls=%fused_computation.8 | convolution fusion | flops 69207040 | bytes 6291616 | tf_op jit(solution)/shard_map/cs,crd->srd/dot_general | solution.py:65
  130.4 2.5 %copy.15 = bf16[32,128,256]{2,1,0:T(8,128)(2,1)} copy(bf16[32,128,256]{2,0,1:T(8,128)(2,1)S(1)} %copy_select_fusion) | data formatting | bytes 4194304 | tf_op jit(solution)/shard_map/jit(_where)/select_n | solution.py:71
  (12 shorter events, 0.3 us)
Async XLA Ops:
  7.2 118.2 %all-gather.2.cloned.1.call-start = ((), (), s32[]{:S(2)}) async-start(), calls=%async_computation.3 | async-start | bytes 2162688 | tf_op jit(solution)/shard_map/all_gather | solution.py:61
  42.2 17.7 %copy-start.2 = (s32[32]{0:T(128)S(1)}, s32[32]{0:T(128)}, u32[]{:S(2)}) copy-start(s32[32]{0:T(128)} %param.14) | copy-start | bytes 388
  42.3 26.8 %copy-start = (bf16[128,256]{1,0:T(8,128)(2,1)S(1)}, bf16[128,256]{1,0:T(8,128)(2,1)}, u32[]{:S(2)}) copy-start(bf16[128,256]{1,0:T(8,128)(2,1)} %param.9) | copy-start | bytes 196612
  42.3 26.8 %copy-start.1 = (bf16[128,256]{1,0:T(8,128)(2,1)S(1)}, bf16[128,256]{1,0:T(8,128)(2,1)}, u32[]{:S(2)}) copy-start(bf16[128,256]{1,0:T(8,128)(2,1)} %param.10) | copy-start | bytes 196612
  42.3 26.8 %copy-start.3 = (s32[128]{0:T(128)S(1)}, s32[128]{0:T(128)}, u32[]{:S(2)}) copy-start(s32[128]{0:T(128)} %param.15) | copy-start | bytes 1540
  54.0 11.7 %all-to-all-start = ((f32[8,1,128]{2,1,0:T(1,128)}), f32[8,1,128]{2,1,0:T(1,128)S(1)}, u32[]{:S(2)}, u32[]{:S(2)}) async-start(f32[8,1,128]{2,1,0:T(1,128)} %all_to_all.24), calls=%async_computation | async-start | bytes 8192 | tf_op jit(solution)/shard_map/all_to_all | solution.py:35
  65.7 9.7 %all-to-all-start.1 = ((f32[8,1,128]{2,1,0:T(1,128)}), f32[8,1,128]{2,1,0:T(1,128)S(1)}, u32[]{:S(2)}, u32[]{:S(2)}) async-start(f32[8,1,128]{2,1,0:T(1,128)} %all_to_all.26), calls=%async_computation.1 | async-start | bytes 8192 | tf_op jit(solution)/shard_map/all_to_all | solution.py:35
  75.4 9.7 %all-to-all-start.2 = ((f32[8,1,128]{2,1,0:T(1,128)}), f32[8,1,128]{2,1,0:T(1,128)S(1)}, u32[]{:S(2)}, u32[]{:S(2)}) async-start(f32[8,1,128]{2,1,0:T(1,128)} %all_to_all.30), calls=%async_computation.2 | async-start | bytes 8192 | tf_op jit(solution)/shard_map/all_to_all | solution.py:35
Sparse Core Ops, SparseCore 0:
  10.8 58.9 all-gather.1
where the time goes:
time: 141 us
  blocking collectives  72.1 us (51%)
  waiting for transfers between devices  17.6 us (12%)
  between operations  17.3 us (12%)
  starting transfers between devices  11.9 us (8%)
  matrix products  11.2 us (8%)
  other arithmetic  6.15 us (4%)
  local copies, waits for them, and re-layouts  4.62 us (3%)
    psum x1, blocking collectives, per_device(): summed = lax.psum(jnp.sum(terms), ('queue', 'batch'))  38.4 us
    all_gather x1, blocking collectives, per_device(): lax.all_gather(queries, 'queue', axis=0, tiled=True)  33.6 us
    all_to_all x3, waiting for transfers between devices, per_device(): lax.all_to_all(parts, 'queue', split_axis=0, concat_axis=0, tiled=True)  16.9 us
    all_to_all x3, starting transfers between devices, per_device(): lax.all_to_all(parts, 'queue', split_axis=0, concat_axis=0, tiled=True)  11.9 us
    dot_general x2, matrix products, block_stats(): lax.dot_general(query_block, shard_keys, (((1,), (1,)), ((), ())), prefer...  6.01 us
    dot_general x1, matrix products, per_device(): jnp.einsum('cs,crd->srd', hits.astype(jnp.bfloat16), piece.reshape(count,...  5.03 us
    reduce_sum x2, other arithmetic, block_stats(): jnp.sum(weights * logits, axis=1)  4.84 us
  transfers between devices with their start and end apart: 4, of which 3 were waited for; matrix products, arithmetic and copies ran while one was open for 9% of the time, Pallas kernels for 0%

commit v1 on v0

v1 whole, which is shorter than its diff:
```python
import functools

import jax
import jax.numpy as jnp
from jax import lax
from jax.experimental import pallas as pl
from jax.experimental.pallas import tpu as pltpu
from jax.sharding import PartitionSpec as P


BLOCK = 128
TILE = 256
LOG2E = 1.4426950408889634
VMEM = pl.BlockSpec(memory_space=pltpu.VMEM)
SMEM = pl.BlockSpec(memory_space=pltpu.SMEM)
HBM = pl.BlockSpec(memory_space=pltpu.HBM)


def accumulate(log_scale, q, k_ref):
    count, rows = q.shape[0], k_ref.shape[0]
    c = jnp.exp(jnp.full((8, count), log_scale, jnp.float32)) * LOG2E
    m = jnp.full((8, count), -jnp.inf, jnp.float32)
    s = jnp.zeros((8, count), jnp.float32)
    w = jnp.zeros((8, count), jnp.float32)
    for t in range(rows // TILE):
        d = lax.dot_general(
            k_ref[pl.ds(t * TILE, TILE), :], q, (((1,), (1,)), ((), ())), preferred_element_type=jnp.float32
        ).reshape(TILE // 8, 8, count)
        higher = jnp.maximum(m, jnp.max(d, axis=0))
        a = jnp.exp2((m - higher) * c)
        e = jnp.exp2((d - higher[None]) * c[None])
        s = s * a + jnp.sum(e, axis=0)
        w = w * a + jnp.sum(e * d, axis=0)
        m = higher
    top = jnp.max(m, axis=0, keepdims=True)
    a = jnp.exp2((m - top) * c)
    return top, jnp.sum(s * a, axis=0, keepdims=True), jnp.sum(w * a, axis=0, keepdims=True)


def first_kernel(ls_ref, qa_ref, qb_ref, k_ref, o_ref, base_ref, sem):
    copy = pltpu.make_async_copy(k_ref, base_ref, sem)
    copy.start()
    for i, row in enumerate(accumulate(ls_ref[0], jnp.concatenate([qa_ref[...], qb_ref[...]], axis=0), k_ref)):
        o_ref[i : i + 1, :] = row
    copy.wait()


def middle_kernel(ls_ref, qa_ref, qb_ref, k_ref, o_ref):
    for i, row in enumerate(accumulate(ls_ref[0], jnp.concatenate([qa_ref[...], qb_ref[...]], axis=0), k_ref)):
        o_ref[i : i + 1, :] = row


def last_kernel(ls_ref, qa_ref, qb_ref, k_ref, pos_ref, *refs):
    *parts, o_ref = refs
    n, tok = o_ref.shape[0], o_ref.shape[2]
    me = lax.axis_index("queue")
    rows = accumulate(ls_ref[0], jnp.concatenate([qa_ref[...], qb_ref[...]], axis=0), k_ref)
    for k in range(n):
        at = jnp.bitwise_xor(me, k)
        for i in range(3):
            lanes = pl.ds((k % 2) * tok, tok)
            row = rows[i][:, (k % 2) * tok : (k % 2 + 1) * tok] if k // 2 == n // 2 - 1 else parts[k // 2][i : i + 1, lanes]
            o_ref[:, pl.ds(i * n + at, 1), :] = jnp.broadcast_to(row[None], (n, 1, tok))
    o_ref[:, 3 * n : 3 * n + 1, :] = jnp.broadcast_to(pos_ref[...][None], (n, 1, tok))


def final_kernel(ls_ref, back_ref, loss_ref, term_ref, hold_ref):
    n, tok = back_ref.shape[0], back_ref.shape[2]
    scale = jnp.exp(jnp.full((n, tok), ls_ref[0], jnp.float32))
    pos = scale * back_ref[:, 3 * n, :]
    peak = back_ref[0, 0:n, :]
    for i in range(1, n):
        peak = jnp.maximum(peak, back_ref[i, 0:n, :])
    total = jnp.zeros((n, tok), jnp.float32)
    weighted = jnp.zeros((n, tok), jnp.float32)
    for i in range(n):
        factor = jnp.exp(scale * (back_ref[i, 0:n, :] - peak))
        total += back_ref[i, n : 2 * n, :] * factor
        weighted += back_ref[i, 2 * n : 3 * n, :] * factor
    peak = scale * peak
    highest = jnp.maximum(peak, pos)
    factor = jnp.exp(peak - highest)
    own = jnp.exp(pos - highest)
    final_total = total * factor + own
    final_weighted = scale * weighted * factor + pos * own
    hold_ref[...] = highest + jnp.log(final_total) - pos
    loss_ref[...] = hold_ref[pl.ds(lax.axis_index("queue"), 1), :]
    terms = final_weighted / final_total - pos
    term_ref[...] = jnp.broadcast_to(jnp.sum(terms, keepdims=True), term_ref.shape)


def enqueue_kernel(n_queue, n_batch, ptr_ref, order_ref, base_ref, *refs):
    *pieces, out_ref, sem = refs
    per_dev = out_ref.shape[0] // BLOCK
    total = per_dev * n_queue
    me_q, me_b = lax.axis_index("queue"), lax.axis_index("batch")
    each = order_ref.shape[0] // (n_queue * n_batch)

    def rows(i):
        return pl.ds(pl.multiple_of(i * BLOCK, BLOCK), BLOCK)

    def slot_of(c):
        at = ptr_ref[0] + order_ref[c]
        at = jnp.where(at >= total, at - total, at) - me_q * per_dev
        return at, (at >= 0) & (at < per_dev)

    def start(c, _):
        slot, mine = slot_of(c)

        @pl.when(mine)
        def _():
            dev, rest = c // each, c % each
            dq, db = jnp.bitwise_xor(dev // n_batch, me_q), jnp.bitwise_xor(dev % n_batch, me_b)
            at = ((dq // 2) * (n_batch // 2) + db // 2) * each + rest
            for j, piece in enumerate(pieces):
                @pl.when(dq % 2 + 2 * (db % 2) == j)
                def _():
                    pltpu.make_async_copy(piece.at[rows(at)], out_ref.at[rows(slot)], sem.at[slot]).start()

        return 0

    def finish(c, _):
        slot, mine = slot_of(c)

        @pl.when(mine)
        def _():
            pltpu.make_async_copy(pieces[0].at[rows(0)], out_ref.at[rows(slot)], sem.at[slot]).wait()

        return 0

    lax.fori_loop(0, order_ref.shape[0], start, 0)
    lax.fori_loop(0, order_ref.shape[0], finish, 0)


def kernel_call(kernel, operands, specs, shapes, out_specs, scratch=(), cost=None, **more):
    return pl.pallas_call(
        kernel,
        out_shape=shapes,
        in_specs=specs,
        out_specs=out_specs,
        scratch_shapes=list(scratch),
        compiler_params=pltpu.CompilerParams(vmem_limit_bytes=12 << 20),
        cost_estimate=cost,
        **more,
    )(*operands)


def per_device(n_queue, n_batch, queries, keys, queue_keys, log_scale, write_pointer, block_order, pos_index):
    tok_rows, width = queries.shape

    def hop(x, axis, n, k):
        return lax.ppermute(x, axis, [(i, i ^ k) for i in range(n)])

    def across(x, k):
        return hop(x, "queue", n_queue, k)

    def beside(x, k):
        return hop(x, "batch", n_batch, k)

    got = [None] * n_queue
    got[0] = queries
    for k in range(2, n_queue, 2):
        got[k] = across(queries, k)
    got[1] = across(queries, 1)
    for k in range(3, n_queue, 2):
        got[k] = across(got[k - 1], 1)

    half = [keys]
    step = n_batch // 2
    while step > 1:
        half = half + [beside(x, step) for x in half]
        step //= 2
    order = [0]
    step = n_batch // 2
    while step > 1:
        order = order + [o ^ step for o in order]
        step //= 2
    half = jnp.concatenate([half[order.index(2 * j)] for j in range(n_batch // 2)], axis=0)
    even = jnp.concatenate([half] + [across(half, k) for k in range(2, n_queue, 2)], axis=0)
    odd = across(even, 1)
    pieces = (even, odd, beside(even, 1), beside(odd, 1))

    local_scores = lax.dot_general(keys, queries, (((1,), (1,)), ((), ())), preferred_element_type=jnp.float32)
    rows = lax.broadcasted_iota(jnp.int32, local_scores.shape, 0)
    pos = jnp.sum(jnp.where(rows == pos_index[None, :], local_scores, 0.0), axis=0, keepdims=True)

    cost = pl.CostEstimate(
        flops=4 * tok_rows * queue_keys.shape[0] * width,
        bytes_accessed=queue_keys.size * 2,
        transcendentals=2 * tok_rows * queue_keys.shape[0],
    )
    part_shape = jax.ShapeDtypeStruct((3, 2 * tok_rows), jnp.float32)
    first, base = kernel_call(
        first_kernel,
        (log_scale, got[0], got[1], queue_keys),
        [SMEM, VMEM, VMEM, VMEM],
        (part_shape, jax.ShapeDtypeStruct(queue_keys.shape, queue_keys.dtype)),
        (VMEM, HBM),
        [pltpu.SemaphoreType.DMA],
        cost,
    )
    parts = [first]
    for k in range(2, n_queue - 2, 2):
        parts.append(
            kernel_call(
                middle_kernel,
                (log_scale, got[k], got[k + 1], queue_keys),
                [SMEM, VMEM, VMEM, VMEM],
                part_shape,
                VMEM,
                cost=cost,
            )
        )
    sent = kernel_call(
        last_kernel,
        (log_scale, got[n_queue - 2], got[n_queue - 1], queue_keys, pos, *parts),
        [SMEM, VMEM, VMEM, VMEM, VMEM] + [VMEM] * len(parts),
        jax.ShapeDtypeStruct((n_queue, 3 * n_queue + 8, tok_rows), jnp.float32),
        VMEM,
        cost=cost,
    )
    back = lax.all_to_all(sent, "queue", split_axis=0, concat_axis=0, tiled=True)
    loss, term = kernel_call(
        final_kernel,
        (log_scale, back),
        [SMEM, VMEM],
        (jax.ShapeDtypeStruct((1, tok_rows), jnp.float32), jax.ShapeDtypeStruct((1, 128), jnp.float32)),
        (VMEM, VMEM),
        [pltpu.VMEM((n_queue, tok_rows), jnp.float32)],
    )
    step = n_batch // 2
    while step:
        term = term + beside(term, step)
        step //= 2
    temp_grad = term[0, :1] / (tok_rows * n_queue * n_batch)

    new_queue = kernel_call(
        functools.partial(enqueue_kernel, n_queue, n_batch),
        (write_pointer, block_order, base, *pieces),
        [SMEM, SMEM, HBM] + [VMEM] * len(pieces),
        jax.ShapeDtypeStruct(queue_keys.shape, queue_keys.dtype),
        HBM,
        [pltpu.SemaphoreType.DMA((queue_keys.shape[0] // BLOCK,))],
        input_output_aliases={2: 0},
    )
    return (loss.reshape(tok_rows), temp_grad, new_queue)


def solution(mesh):
    n_queue, n_batch = mesh.shape["queue"], mesh.shape["batch"]
    placed = (
        P(("queue", "batch"), None),
        P(("queue", "batch"), None),
        P("queue", None),
        P(),
        P(),
        P(),
        P(("queue", "batch")),
    )
    return jax.shard_map(
        functools.partial(per_device, n_queue, n_batch),
        mesh=mesh,
        in_specs=placed,
        out_specs=(P(("queue", "batch")), P(), P("queue", None)),
        check_vma=False,
    )
```

time: 141 us -> 68.8 us (0.49)
  blocking collectives: 72.1 us -> 14.5 us
  between operations: 17.3 us -> 3.27 us
  matrix products: 11.2 us -> 1.05 us
  Pallas kernels: 0 us -> 9.71 us
  starting transfers between devices: 11.9 us -> 19.2 us
  other arithmetic: 6.15 us -> 0.01 us
    psum x1 -> x0, blocking collectives: 38.4 us -> none  [per_device(): summed = lax.psum(jnp.sum(terms), ('queue', 'batch'))]
    all_gather x1 -> x0, blocking collectives: 33.6 us -> none  [per_device(): lax.all_gather(queries, 'queue', axis=0, tiled=True)]
    ppermute x0 -> x16, starting transfers between devices: none -> 19.2 us  [hop(): return lax.ppermute(x, axis, [(i, i ^ k) for i in range(n)])]
    all_to_all x3 -> x0, waiting for transfers between devices: 16.9 us -> none  [per_device(): lax.all_to_all(parts, 'queue', split_axis=0, concat_axis=0, tiled=True)]
    ppermute x0 -> x16, waiting for transfers between devices: none -> 16.7 us  [hop(): return lax.ppermute(x, axis, [(i, i ^ k) for i in range(n)])]
    all_to_all x0 -> x1, blocking collectives: none -> 14.5 us  [per_device(): lax.all_to_all(sent, 'queue', split_axis=0, concat_axis=0, tiled=True)]
    all_to_all x3 -> x0, starting transfers between devices: 11.9 us -> none  [per_device(): lax.all_to_all(parts, 'queue', split_axis=0, concat_axis=0, tiled=True)]
    dot_general x4 -> x1, matrix products: 11.2 us -> 1.05 us  [per_device(): lax.dot_general(keys, queries, (((1,), (1,)), ((), ())), preferred_elemen...]
  transfers between devices with their start and end apart: 4 -> 16, of which waited for: 3 -> 8; matrix products, arithmetic and copies ran while one was open for 9% -> 3% of each run, Pallas kernels for 0% -> 11%
where the time goes in v1:
time: 68.8 us; the launch traced here: 68.4 us
  starting transfers between devices  19.2 us (28%)
  waiting for transfers between devices  16.7 us (24%)
  blocking collectives  14.5 us (21%)
  Pallas kernels  9.71 us (14%)
  local copies, waits for them, and re-layouts  3.98 us (6%)
  between operations  3.27 us (5%)
  matrix products  1.05 us (2%)
    ppermute x16, starting transfers between devices, hop(): return lax.ppermute(x, axis, [(i, i ^ k) for i in range(n)])  19.2 us
    ppermute x16, waiting for transfers between devices, hop(): return lax.ppermute(x, axis, [(i, i ^ k) for i in range(n)])  16.7 us
    all_to_all x1, blocking collectives, per_device(): lax.all_to_all(sent, 'queue', split_axis=0, concat_axis=0, tiled=True)  14.5 us
    pallas_call x6, Pallas kernels, kernel_call(): pl.pallas_call(kernel, out_shape=shapes, in_specs=specs, out_specs=out_sp...  9.71 us
    unnamed x11, local copies, waits for them, and re-layouts  3.96 us
  transfers between devices with their start and end apart: 16, of which 8 were waited for; matrix products, arithmetic and copies ran while one was open for 3% of the time, Pallas kernels for 11%

profile of v1, /device:TPU:0, one launch (start us, length us, event | category | flops | bytes accessed | tf_op | source)
XLA Modules:
  0.0 68.4 jit_solution(4063277727724108753)
XLA Ops:
  0.6 3.0 %collective-permute-start.9 = (bf16[128,256]{1,0:T(8,128)(2,1)}, bf16[128,256]{1,0:T(8,128)(2,1)S(1)}, u32[]{:S(2)}, u32[]{:S(2)}) collective-permute-start(bf16[128,256]{1,0:T(8,128)(2,1)} %param.8), channel_id=1, source_target_pairs={{0,2},{1,3},{2,0},{3,1},{4,6},{5,7},{6,4},{7,5},{8,10},{9,11},{10,... | collective-permute-start | bytes 196616 | tf_op jit(solution)/shard_map/ppermute | solution.py:152
  3.7 0.9 %constant_dynamic-update-slice_fusion.1 = (bf16[256,256]{1,0:T(8,128)(2,1)S(1)}, bf16[1024,256]{1,0:T(8,128)(2,1)S(1)}) fusion(bf16[128,256]{1,0:T(8,128)(2,1)} %param.8), kind=kLoop, calls=%fused_computation.4 | loop fusion | bytes 196608
  4.5 1.6 %collective-permute-done.9 = bf16[128,256]{1,0:T(8,128)(2,1)S(1)} collective-permute-done((bf16[128,256]{1,0:T(8,128)(2,1)}, bf16[128,256]{1,0:T(8,128)(2,1)S(1)}, u32[]{:S(2)}, u32[]{:S(2)}) %collective-permute-start.9) | collective-permute-done | bytes 65568 | tf_op jit(solution)/shard_map/ppermute | solution.py:152
  6.1 2.2 %collective-permute-start.10 = (bf16[256,256]{1,0:T(8,128)(2,1)S(1)}, bf16[256,256]{1,0:T(8,128)(2,1)S(1)}, u32[]{:S(2)}, u32[]{:S(2)}) collective-permute-start(bf16[256,256]{1,0:T(8,128)(2,1)S(1)} %get-tuple-element.11), channel_id=1, source_target_pairs={{0,8},{4,12},{8,0},{12,4},{16,24},{20,28},{24,16},{28,20},{1,9},{5... | collective-permute-start | bytes 393224 | tf_op jit(solution)/shard_map/ppermute | solution.py:152
  8.3 2.6 %collective-permute-start.11 = (bf16[256,256]{1,0:T(8,128)(2,1)S(1)}, bf16[256,256]{1,0:T(8,128)(2,1)S(1)}, u32[]{:S(2)}, u32[]{:S(2)}) collective-permute-start(bf16[256,256]{1,0:T(8,128)(2,1)S(1)} %get-tuple-element.11), channel_id=1, source_target_pairs={{0,16},{4,20},{8,24},{12,28},{16,0},{20,4},{24,8},{28,12},{1,17},{... | collective-permute-start | bytes 393224 | tf_op jit(solution)/shard_map/ppermute | solution.py:152
  10.9 1.7 %collective-permute-done.10 = bf16[256,256]{1,0:T(8,128)(2,1)S(1)} collective-permute-done((bf16[256,256]{1,0:T(8,128)(2,1)S(1)}, bf16[256,256]{1,0:T(8,128)(2,1)S(1)}, u32[]{:S(2)}, u32[]{:S(2)}) %collective-permute-start.10) | collective-permute-done | bytes 131104 | tf_op jit(solution)/shard_map/ppermute | solution.py:152
  12.6 7.5 %collective-permute-done.11 = bf16[256,256]{1,0:T(8,128)(2,1)S(1)} collective-permute-done((bf16[256,256]{1,0:T(8,128)(2,1)S(1)}, bf16[256,256]{1,0:T(8,128)(2,1)S(1)}, u32[]{:S(2)}, u32[]{:S(2)}) %collective-permute-start.11) | collective-permute-done | bytes 131104 | tf_op jit(solution)/shard_map/ppermute | solution.py:152
  20.1 1.5 %collective-permute-start.13 = (bf16[1024,256]{1,0:T(8,128)(2,1)S(1)}, bf16[1024,256]{1,0:T(8,128)(2,1)S(1)}, u32[]{:S(2)}, u32[]{:S(2)}) collective-permute-start(bf16[1024,256]{1,0:T(8,128)(2,1)S(1)} %constant_dynamic-update-slice_fusion.2.refs_0_), channel_id=1, source_target_pairs={{0,4},{4,0},{8,12},{12,8},{16,20},{20,16},{24,28},{28,24},{1,5},{5... | collective-permute-start | bytes 1572872 | tf_op jit(solution)/shard_map/ppermute | solution.py:152
  21.7 1.9 %collective-permute-start.3 = (bf16[128,256]{1,0:T(8,128)(2,1)}, bf16[128,256]{1,0:T(8,128)(2,1)S(1)}, u32[]{:S(2)}, u32[]{:S(2)}) collective-permute-start(bf16[128,256]{1,0:T(8,128)(2,1)} %qa_ref.1), channel_id=1, source_target_pairs={{0,8},{4,12},{8,0},{12,4},{16,24},{20,28},{24,16},{28,20},{1,9},{5... | collective-permute-start | bytes 196616 | tf_op jit(solution)/shard_map/ppermute | solution.py:152
  23.6 2.5 %collective-permute-start = (bf16[128,256]{1,0:T(8,128)(2,1)}, bf16[128,256]{1,0:T(8,128)(2,1)S(1)}, u32[]{:S(2)}, u32[]{:S(2)}) collective-permute-start(bf16[128,256]{1,0:T(8,128)(2,1)} %qa_ref.1), channel_id=1, source_target_pairs={{0,24},{4,28},{8,16},{12,20},{16,8},{20,12},{24,0},{28,4},{1,25},{... | collective-permute-start | bytes 196616 | tf_op jit(solution)/shard_map/ppermute | solution.py:152
  26.1 0.5 collective-permute-start.2
  26.6 0.2 collective-permute-done.3.qa_ref
  26.8 1.3 %collective-permute-start.4 = (bf16[128,256]{1,0:T(8,128)(2,1)S(1)}, bf16[128,256]{1,0:T(8,128)(2,1)S(1)}, u32[]{:S(2)}, u32[]{:S(2)}) collective-permute-start(bf16[128,256]{1,0:T(8,128)(2,1)S(1)} %collective-permute-done.3.qa_ref), channel_id=1, source_target_pairs={{0,4},{4,0},{8,12},{12,8},{16,20},{20,16},{24,28},{28,24},{1,5},{5... | collective-permute-start | bytes 196616 | tf_op jit(solution)/shard_map/ppermute | solution.py:152
  28.2 1.7 %collective-permute-done.qa_ref = bf16[128,256]{1,0:T(8,128)(2,1)S(1)} collective-permute-done((bf16[128,256]{1,0:T(8,128)(2,1)}, bf16[128,256]{1,0:T(8,128)(2,1)S(1)}, u32[]{:S(2)}, u32[]{:S(2)}) %collective-permute-start) | collective-permute-done | bytes 65568 | tf_op jit(solution)/shard_map/ppermute | solution.py:152
  29.9 1.5 %collective-permute-done.13.refs_1_ = bf16[1024,256]{1,0:T(8,128)(2,1)S(1)} collective-permute-done((bf16[1024,256]{1,0:T(8,128)(2,1)S(1)}, bf16[1024,256]{1,0:T(8,128)(2,1)S(1)}, u32[]{:S(2)}, u32[]{:S(2)}) %collective-permute-start.13) | collective-permute-done | bytes 524320 | tf_op jit(solution)/shard_map/ppermute | solution.py:152
  31.3 1.1 %fusion = f32[128]{0:T(128)S(1)} fusion(bf16[128,256]{1,0:T(8,128)(2,1)} %param.8, bf16[128,256]{1,0:T(8,128)(2,1)} %qa_ref.1, s32[128]{0:T(128)} %param.13), kind=kOutput, calls=%fused_computation.1 | convolution fusion | flops 8437632 | bytes 132096 | tf_op jit(solution)/shard_map/dot_general | solution.py:183
  33.1 1.6 %collective-permute-start.1 = (bf16[128,256]{1,0:T(8,128)(2,1)S(1)}, bf16[128,256]{1,0:T(8,128)(2,1)S(1)}, u32[]{:S(2)}, u32[]{:S(2)}) collective-permute-start(bf16[128,256]{1,0:T(8,128)(2,1)S(1)} %collective-permute-done.qa_ref), channel_id=1, source_target_pairs={{0,4},{4,0},{8,12},{12,8},{16,20},{20,16},{24,28},{28,24},{1,5},{5... | collective-permute-start | bytes 196616 | tf_op jit(solution)/shard_map/ppermute | solution.py:152
  34.7 0.5 collective-permute-start.6
  35.2 1.6 %copy-done = bf16[4096,256]{1,0:T(8,128)(2,1)S(1)} copy-done((bf16[4096,256]{1,0:T(8,128)(2,1)S(1)}, bf16[4096,256]{1,0:T(8,128)(2,1)}, u32[]{:S(2)}) %copy-start) | copy-done | bytes 2097176
  36.8 0.8 %copy-done.2 = bf16[128,256]{1,0:T(8,128)(2,1)S(1)} copy-done((bf16[128,256]{1,0:T(8,128)(2,1)S(1)}, bf16[128,256]{1,0:T(8,128)(2,1)}, u32[]{:S(2)}) %copy-start.2) | copy-done | bytes 65560
  37.6 1.7 %shard_map.94 = (f32[3,256]{1,0:T(4,128)S(1)}, bf16[4096,256]{1,0:T(8,128)(2,1)}) custom-call(f32[1]{0:T(128)S(6)} %copy.17.ls_ref, bf16[128,256]{1,0:T(8,128)(2,1)S(1)} %copy-done.2, bf16[128,256]{1,0:T(8,128)(2,1)S(1)} %collective-permute-done.2.qb_ref, bf16[4096,256]{1,0:T(8,128)(2,1)S(1)} %copy-done), custom_call_target="tpu_custom_call" | custom-call | flops 536870912 | bytes 2097152 | tf_op jit(solution)/shard_map/pallas_call | solution.py:136
  39.3 0.6 copy-done.1
  40.0 1.7 %shard_map.95.refs_1_ = f32[3,256]{1,0:T(4,128)S(1)} custom-call(f32[1]{0:T(128)S(6)} %copy.17.ls_ref, bf16[128,256]{1,0:T(8,128)(2,1)S(1)} %collective-permute-done.3.qa_ref, bf16[128,256]{1,0:T(8,128)(2,1)S(1)} %collective-permute-done.4.qb_ref, bf16[4096,256]{1,0:T(8,128)(2,1)S(1)} %copy-done.1), custom_call_target="tpu_custom_call" | custom-call | flops 536870912 | bytes 2097152 | tf_op jit(solution)/shard_map/pallas_call | solution.py:136
  41.7 0.0 copy-start.3
  41.7 1.7 %shard_map.96.refs_2_ = f32[3,256]{1,0:T(4,128)S(1)} custom-call(f32[1]{0:T(128)S(6)} %copy.17.ls_ref, bf16[128,256]{1,0:T(8,128)(2,1)S(1)} %collective-permute-done.5.qa_ref, bf16[128,256]{1,0:T(8,128)(2,1)S(1)} %collective-permute-done.6.qb_ref, bf16[4096,256]{1,0:T(8,128)(2,1)S(1)} %copy-done.1), custom_call_target="tpu_custom_call" | custom-call | flops 536870912 | bytes 2097152 | tf_op jit(solution)/shard_map/pallas_call | solution.py:136
  43.4 1.7 %shard_map.97 = f32[8,32,128]{2,1,0:T(8,128)S(1)} custom-call(f32[1]{0:T(128)S(6)} %copy.17.ls_ref, bf16[128,256]{1,0:T(8,128)(2,1)S(1)} %collective-permute-done.qa_ref, bf16[128,256]{1,0:T(8,128)(2,1)S(1)} %collective-permute-done.1.qb_ref, bf16[4096,256]{1,0:T(8,128)(2,1)S(1)} %copy-done.1, f32[1,128]{1,0:T(1,128)S(1)} %bitcast.6, ...), custom_call_target="tpu_custom_call" | custom-call | flops 536870912 | bytes 2097152 | tf_op jit(solution)/shard_map/pallas_call | solution.py:136
  45.1 14.5 %all_to_all.5.back_ref = f32[8,32,128]{2,1,0:T(8,128)S(1)} all-to-all(f32[8,32,128]{2,1,0:T(8,128)S(1)} %shard_map.97), channel_id=1, replica_groups=mesh['queue'=8,'batch'=4] {'queue'}, dimensions={0} | all-to-all | bytes 262144 | tf_op jit(solution)/shard_map/all_to_all | solution.py:222
  59.6 0.6 shard_map.98
  60.1 1.5 %collective-permute-start.7 = (f32[1,128]{1,0:T(1,128)S(1)}, f32[1,128]{1,0:T(1,128)S(1)}, u32[]{:S(2)}, u32[]{:S(2)}) collective-permute-start(f32[1,128]{1,0:T(1,128)S(1)} %get-tuple-element.9), channel_id=1, source_target_pairs={{0,2},{1,3},{2,0},{3,1},{4,6},{5,7},{6,4},{7,5},{8,10},{9,11},{10,... | collective-permute-start | bytes 1544 | tf_op jit(solution)/shard_map/ppermute | solution.py:152
  61.6 2.1 %collective-permute-done.7 = f32[1,128]{1,0:T(1,128)S(1)} collective-permute-done((f32[1,128]{1,0:T(1,128)S(1)}, f32[1,128]{1,0:T(1,128)S(1)}, u32[]{:S(2)}, u32[]{:S(2)}) %collective-permute-start.7) | collective-permute-done | bytes 544 | tf_op jit(solution)/shard_map/ppermute | solution.py:152
  64.4 0.5 collective-permute-done.8
  65.0 2.3 %shard_map.99 = bf16[4096,256]{1,0:T(8,128)(2,1)} custom-call(s32[1]{0:T(128)S(6)} %copy.18.ptr_ref, s32[32]{0:T(128)S(1)} %copy-done.3, bf16[4096,256]{1,0:T(8,128)(2,1)} %get-tuple-element.10.base_ref, bf16[1024,256]{1,0:T(8,128)(2,1)S(1)} %constant_dynamic-update-slice_fusion.2.refs_0_, ...), custom_call_target="tpu_custom_call", output_to_operand_aliasing={{}: (2, {})} | custom-call | tf_op jit(solution)/shard_map/pallas_call | solution.py:136
  (23 shorter events, 0.1 us)
Async XLA Ops:
  0.6 5.5 %collective-permute-start.9 = (bf16[128,256]{1,0:T(8,128)(2,1)}, bf16[128,256]{1,0:T(8,128)(2,1)S(1)}, u32[]{:S(2)}, u32[]{:S(2)}) collective-permute-start(bf16[128,256]{1,0:T(8,128)(2,1)} %param.8), channel_id=1, source_target_pairs={{0,2},{1,3},{2,0},{3,1},{4,6},{5,7},{6,4},{7,5},{8,10},{9,11},{10,... | collective-permute-start | bytes 196616 | tf_op jit(solution)/shard_map/ppermute | solution.py:152
  6.1 6.4 %collective-permute-start.10 = (bf16[256,256]{1,0:T(8,128)(2,1)S(1)}, bf16[256,256]{1,0:T(8,128)(2,1)S(1)}, u32[]{:S(2)}, u32[]{:S(2)}) collective-permute-start(bf16[256,256]{1,0:T(8,128)(2,1)S(1)} %get-tuple-element.11), channel_id=1, source_target_pairs={{0,8},{4,12},{8,0},{12,4},{16,24},{20,28},{24,16},{28,20},{1,9},{5... | collective-permute-start | bytes 393224 | tf_op jit(solution)/shard_map/ppermute | solution.py:152
  8.3 11.8 %collective-permute-start.11 = (bf16[256,256]{1,0:T(8,128)(2,1)S(1)}, bf16[256,256]{1,0:T(8,128)(2,1)S(1)}, u32[]{:S(2)}, u32[]{:S(2)}) collective-permute-start(bf16[256,256]{1,0:T(8,128)(2,1)S(1)} %get-tuple-element.11), channel_id=1, source_target_pairs={{0,16},{4,20},{8,24},{12,28},{16,0},{20,4},{24,8},{28,12},{1,17},{... | collective-permute-start | bytes 393224 | tf_op jit(solution)/shard_map/ppermute | solution.py:152
  10.9 9.2 %collective-permute-start.12 = (bf16[256,256]{1,0:T(8,128)(2,1)S(1)}, bf16[256,256]{1,0:T(8,128)(2,1)S(1)}, u32[]{:S(2)}, u32[]{:S(2)}) collective-permute-start(bf16[256,256]{1,0:T(8,128)(2,1)S(1)} %get-tuple-element.11), channel_id=1, source_target_pairs={{0,24},{4,28},{8,16},{12,20},{16,8},{20,12},{24,0},{28,4},{1,25},{... | collective-permute-start | bytes 393224 | tf_op jit(solution)/shard_map/ppermute | solution.py:152
  20.1 11.2 %collective-permute-start.13 = (bf16[1024,256]{1,0:T(8,128)(2,1)S(1)}, bf16[1024,256]{1,0:T(8,128)(2,1)S(1)}, u32[]{:S(2)}, u32[]{:S(2)}) collective-permute-start(bf16[1024,256]{1,0:T(8,128)(2,1)S(1)} %constant_dynamic-update-slice_fusion.2.refs_0_), channel_id=1, source_target_pairs={{0,4},{4,0},{8,12},{12,8},{16,20},{20,16},{24,28},{28,24},{1,5},{5... | collective-permute-start | bytes 1572872 | tf_op jit(solution)/shard_map/ppermute | solution.py:152
  21.7 5.2 %collective-permute-start.3 = (bf16[128,256]{1,0:T(8,128)(2,1)}, bf16[128,256]{1,0:T(8,128)(2,1)S(1)}, u32[]{:S(2)}, u32[]{:S(2)}) collective-permute-start(bf16[128,256]{1,0:T(8,128)(2,1)} %qa_ref.1), channel_id=1, source_target_pairs={{0,8},{4,12},{8,0},{12,4},{16,24},{20,28},{24,16},{28,20},{1,9},{5... | collective-permute-start | bytes 196616 | tf_op jit(solution)/shard_map/ppermute | solution.py:152
  23.6 6.3 %collective-permute-start = (bf16[128,256]{1,0:T(8,128)(2,1)}, bf16[128,256]{1,0:T(8,128)(2,1)S(1)}, u32[]{:S(2)}, u32[]{:S(2)}) collective-permute-start(bf16[128,256]{1,0:T(8,128)(2,1)} %qa_ref.1), channel_id=1, source_target_pairs={{0,24},{4,28},{8,16},{12,20},{16,8},{20,12},{24,0},{28,4},{1,25},{... | collective-permute-start | bytes 196616 | tf_op jit(solution)/shard_map/ppermute | solution.py:152
  26.1 7.0 %collective-permute-start.2 = (bf16[128,256]{1,0:T(8,128)(2,1)}, bf16[128,256]{1,0:T(8,128)(2,1)S(1)}, u32[]{:S(2)}, u32[]{:S(2)}) collective-permute-start(bf16[128,256]{1,0:T(8,128)(2,1)} %qa_ref.1), channel_id=1, source_target_pairs={{0,4},{4,0},{8,12},{12,8},{16,20},{20,16},{24,28},{28,24},{1,5},{5... | collective-permute-start | bytes 196616 | tf_op jit(solution)/shard_map/ppermute | solution.py:152
  26.6 8.0 %collective-permute-start.5 = (bf16[128,256]{1,0:T(8,128)(2,1)}, bf16[128,256]{1,0:T(8,128)(2,1)S(1)}, u32[]{:S(2)}, u32[]{:S(2)}) collective-permute-start(bf16[128,256]{1,0:T(8,128)(2,1)} %qa_ref.1), channel_id=1, source_target_pairs={{0,16},{4,20},{8,24},{12,28},{16,0},{20,4},{24,8},{28,12},{1,17},{... | collective-permute-start | bytes 196616 | tf_op jit(solution)/shard_map/ppermute | solution.py:152
  26.8 12.5 %collective-permute-start.4 = (bf16[128,256]{1,0:T(8,128)(2,1)S(1)}, bf16[128,256]{1,0:T(8,128)(2,1)S(1)}, u32[]{:S(2)}, u32[]{:S(2)}) collective-permute-start(bf16[128,256]{1,0:T(8,128)(2,1)S(1)} %collective-permute-done.3.qa_ref), channel_id=1, source_target_pairs={{0,4},{4,0},{8,12},{12,8},{16,20},{20,16},{24,28},{28,24},{1,5},{5... | collective-permute-start | bytes 196616 | tf_op jit(solution)/shard_map/ppermute | solution.py:152
  29.9 35.1 %collective-permute-start.14 = (bf16[1024,256]{1,0:T(8,128)(2,1)S(1)}, bf16[1024,256]{1,0:T(8,128)(2,1)S(1)}, u32[]{:S(2)}, u32[]{:S(2)}) collective-permute-start(bf16[1024,256]{1,0:T(8,128)(2,1)S(1)} %constant_dynamic-update-slice_fusion.2.refs_0_), channel_id=1, source_target_pairs={{0,1},{1,0},{2,3},{3,2},{4,5},{5,4},{6,7},{7,6},{8,9},{9,8},{10,11... | collective-permute-start | bytes 1572872 | tf_op jit(solution)/shard_map/ppermute | solution.py:152
  31.3 33.6 %collective-permute-start.15 = (bf16[1024,256]{1,0:T(8,128)(2,1)S(1)}, bf16[1024,256]{1,0:T(8,128)(2,1)S(1)}, u32[]{:S(2)}, u32[]{:S(2)}) collective-permute-start(bf16[1024,256]{1,0:T(8,128)(2,1)S(1)} %collective-permute-done.13.refs_1_), channel_id=1, source_target_pairs={{0,1},{1,0},{2,3},{3,2},{4,5},{5,4},{6,7},{7,6},{8,9},{9,8},{10,11... | collective-permute-start | bytes 1572872 | tf_op jit(solution)/shard_map/ppermute | solution.py:152
  33.1 10.3 %collective-permute-start.1 = (bf16[128,256]{1,0:T(8,128)(2,1)S(1)}, bf16[128,256]{1,0:T(8,128)(2,1)S(1)}, u32[]{:S(2)}, u32[]{:S(2)}) collective-permute-start(bf16[128,256]{1,0:T(8,128)(2,1)S(1)} %collective-permute-done.qa_ref), channel_id=1, source_target_pairs={{0,4},{4,0},{8,12},{12,8},{16,20},{20,16},{24,28},{28,24},{1,5},{5... | collective-permute-start | bytes 196616 | tf_op jit(solution)/shard_map/ppermute | solution.py:152
  34.7 7.0 %collective-permute-start.6 = (bf16[128,256]{1,0:T(8,128)(2,1)S(1)}, bf16[128,256]{1,0:T(8,128)(2,1)S(1)}, u32[]{:S(2)}, u32[]{:S(2)}) collective-permute-start(bf16[128,256]{1,0:T(8,128)(2,1)S(1)} %collective-permute-done.5.qa_ref), channel_id=1, source_target_pairs={{0,4},{4,0},{8,12},{12,8},{16,20},{20,16},{24,28},{28,24},{1,5},{5... | collective-permute-start | bytes 196616 | tf_op jit(solution)/shard_map/ppermute | solution.py:152
  35.2 1.6 %copy-start = (bf16[4096,256]{1,0:T(8,128)(2,1)S(1)}, bf16[4096,256]{1,0:T(8,128)(2,1)}, u32[]{:S(2)}) copy-start(bf16[4096,256]{1,0:T(8,128)(2,1)} %k_ref.7) | copy-start | bytes 6291460
  36.8 0.8 %copy-start.2 = (bf16[128,256]{1,0:T(8,128)(2,1)S(1)}, bf16[128,256]{1,0:T(8,128)(2,1)}, u32[]{:S(2)}) copy-start(bf16[128,256]{1,0:T(8,128)(2,1)} %qa_ref.1) | copy-start | bytes 196612
  37.6 2.3 %copy-start.1 = (bf16[4096,256]{1,0:T(8,128)(2,1)S(1)}, bf16[4096,256]{1,0:T(8,128)(2,1)}, u32[]{:S(2)}) copy-start(bf16[4096,256]{1,0:T(8,128)(2,1)} %k_ref.7) | copy-start | bytes 6291460
  41.7 23.3 %copy-start.3 = (s32[32]{0:T(128)S(1)}, s32[32]{0:T(128)}, u32[]{:S(2)}) copy-start(s32[32]{0:T(128)} %order_ref.1) | copy-start | bytes 388
  60.1 3.6 %collective-permute-start.7 = (f32[1,128]{1,0:T(1,128)S(1)}, f32[1,128]{1,0:T(1,128)S(1)}, u32[]{:S(2)}, u32[]{:S(2)}) collective-permute-start(f32[1,128]{1,0:T(1,128)S(1)} %get-tuple-element.9), channel_id=1, source_target_pairs={{0,2},{1,3},{2,0},{3,1},{4,6},{5,7},{6,4},{7,5},{8,10},{9,11},{10,... | collective-permute-start | bytes 1544 | tf_op jit(solution)/shard_map/ppermute | solution.py:152
  63.7 1.2 %collective-permute-start.8 = (f32[1,128]{1,0:T(1,128)S(1)}, f32[1,128]{1,0:T(1,128)S(1)}, u32[]{:S(2)}, u32[]{:S(2)}) collective-permute-start(f32[1,128]{1,0:T(1,128)S(1)} %add.6), channel_id=1, source_target_pairs={{0,1},{1,0},{2,3},{3,2},{4,5},{5,4},{6,7},{7,6},{8,9},{9,8},{10,11... | collective-permute-start | bytes 1544 | tf_op jit(solution)/shard_map/ppermute | solution.py:152

commit v2 on v1

v2 whole, which is shorter than its diff:
```python
import functools

import jax
import jax.numpy as jnp
from jax import lax
from jax.experimental import pallas as pl
from jax.experimental.pallas import tpu as pltpu
from jax.sharding import PartitionSpec as P


BLOCK = 128
TILE = 256
LOG2E = 1.4426950408889634
LARGE = 2.0**60
VMEM = pl.BlockSpec(memory_space=pltpu.VMEM)
HBM = pl.BlockSpec(memory_space=pltpu.HBM)
SMEM = pl.BlockSpec(memory_space=pltpu.SMEM)


def dot_t(a, b):
    return lax.dot_general(a, b, (((1,), (1,)), ((), ())), preferred_element_type=jnp.float32)


def scores_of(k_ref, q, t):
    return dot_t(k_ref[pl.ds(t * TILE, TILE), :], q).reshape(TILE // 8, 8, q.shape[0])


def settle(m, s, w, c, o_ref):
    top = jnp.max(m, axis=0, keepdims=True)
    a = jnp.exp2((m - top) * c)
    o_ref[0:1, :] = top
    o_ref[1:2, :] = jnp.sum(s * a, axis=0, keepdims=True)
    o_ref[2:3, :] = jnp.sum(w * a, axis=0, keepdims=True)


def accumulate(log_scale, q, k_ref, o_ref):
    count, tiles = q.shape[0], k_ref.shape[0] // TILE
    c = jnp.exp(jnp.broadcast_to(log_scale, (8, count))) * LOG2E
    d = scores_of(k_ref, q, 0)
    m = jnp.max(d, axis=0)
    e = jnp.exp2((d - m[None]) * c[None])
    s = jnp.sum(e, axis=0)
    w = jnp.sum(e * d, axis=0)
    for t in range(1, tiles):
        d = scores_of(k_ref, q, t)
        e = jnp.exp2((d - m[None]) * c[None])
        s = s + jnp.sum(e, axis=0)
        w = w + jnp.sum(e * d, axis=0)
    settle(m, s, w, c, o_ref)

    @pl.when(jnp.logical_not(jnp.max(s) < LARGE))
    def _():
        def step(t, carry):
            m, s, w = carry
            d = scores_of(k_ref, q, t)
            higher = jnp.maximum(m, jnp.max(d, axis=0))
            a = jnp.exp2((m - higher) * c)
            e = jnp.exp2((d - higher[None]) * c[None])
            return higher, s * a + jnp.sum(e, axis=0), w * a + jnp.sum(e * d, axis=0)

        zero = jnp.zeros((8, count), jnp.float32)
        settle(*lax.fori_loop(0, tiles, step, (m, zero, zero)), c, o_ref)


def both(a_ref, b_ref, tok):
    return jnp.concatenate([a_ref[:tok, :], b_ref[:tok, :]], axis=0)


def open_kernel(o_ref):
    o_ref[...] = jnp.zeros_like(o_ref)


def first_kernel(_, ls_ref, index_ref, qa_ref, qb_ref, k_ref, o_ref, pos_ref):
    tok = qa_ref.shape[0] // 2
    scores = dot_t(qa_ref[tok:, :], qa_ref[:tok, :])
    rows = lax.broadcasted_iota(jnp.int32, scores.shape, 0)
    pos_ref[...] = jnp.sum(jnp.where(rows == index_ref[...], scores, 0.0), axis=0, keepdims=True)
    accumulate(ls_ref[...], both(qa_ref, qb_ref, tok), k_ref, o_ref)


def middle_kernel(ls_ref, qa_ref, qb_ref, k_ref, o_ref):
    accumulate(ls_ref[...], both(qa_ref, qb_ref, o_ref.shape[1] // 2), k_ref, o_ref)


def last_kernel(ls_ref, qa_ref, qb_ref, k_ref, pos_ref, *refs):
    *parts, o_ref, hold, own = refs
    n, tok = o_ref.shape[0], o_ref.shape[2]
    me = lax.axis_index("queue")
    hold[3 * n : 3 * n + 1, :] = pos_ref[...]
    for k in range(n - 2):
        at = jnp.bitwise_xor(me, k)
        for i in range(3):
            hold[pl.ds(i * n + at, 1), :] = parts[k // 2][i : i + 1, (k % 2) * tok : (k % 2 + 1) * tok]
    accumulate(ls_ref[...], both(qa_ref, qb_ref, tok), k_ref, own)
    for k in range(n - 2, n):
        at = jnp.bitwise_xor(me, k)
        for i in range(3):
            hold[pl.ds(i * n + at, 1), :] = own[i : i + 1, (k % 2) * tok : (k % 2 + 1) * tok]
    sent = hold[...]
    for i in range(n):
        o_ref[i] = sent


def base_kernel(_, ptr_ref, order_ref, k_ref, base_ref, sem):
    copy = pltpu.make_async_copy(k_ref, base_ref, sem)
    copy.start()
    copy.wait()


def final_kernel(ls_ref, back_ref, loss_ref, term_ref, hold_ref):
    n, tok = back_ref.shape[0], back_ref.shape[2]
    scale = jnp.exp(jnp.broadcast_to(ls_ref[...], (n, tok)))
    pos = scale * back_ref[:, 3 * n, :]
    peak = back_ref[0, 0:n, :]
    for i in range(1, n):
        peak = jnp.maximum(peak, back_ref[i, 0:n, :])
    total = jnp.zeros((n, tok), jnp.float32)
    weighted = jnp.zeros((n, tok), jnp.float32)
    for i in range(n):
        factor = jnp.exp(scale * (back_ref[i, 0:n, :] - peak))
        total += back_ref[i, n : 2 * n, :] * factor
        weighted += back_ref[i, 2 * n : 3 * n, :] * factor
    peak = scale * peak
    highest = jnp.maximum(peak, pos)
    factor = jnp.exp(peak - highest)
    own = jnp.exp(pos - highest)
    final_total = total * factor + own
    final_weighted = scale * weighted * factor + pos * own
    hold_ref[...] = highest + jnp.log(final_total) - pos
    loss_ref[...] = hold_ref[pl.ds(lax.axis_index("queue"), 1), :]
    terms = final_weighted / final_total - pos
    mean = jnp.sum(terms, keepdims=True) / (n * tok * lax.axis_size("batch"))
    term_ref[...] = jnp.broadcast_to(mean, term_ref.shape)


def grad_kernel(*refs):
    *terms, o_ref = refs
    o_ref[...] = sum((x[0:1, 0:1] for x in terms[1:]), terms[0][0:1, 0:1])


def enqueue_kernel(n_queue, n_batch, order, ptr, block_order, base_ref, *refs):
    *pieces, out_ref, sem = refs
    per_dev = out_ref.shape[0] // BLOCK
    total = per_dev * n_queue
    count = block_order.shape[0]
    each = count // (n_queue * n_batch)
    me_q, me_b = lax.axis_index("queue"), lax.axis_index("batch")
    offset = ptr[0] - me_q * per_dev
    offset = jnp.where(offset < 0, offset + total, offset)

    def rows(i):
        return pl.ds(pl.multiple_of(i * BLOCK, BLOCK), BLOCK)

    def slot_of(c):
        at = offset + block_order[c]
        return jnp.where(at >= total, at - total, at)

    def start(c, _):
        slot = slot_of(c)

        @pl.when(slot < per_dev)
        def _():
            dev = c // each
            dq, db = jnp.bitwise_xor(dev // n_batch, me_q), jnp.bitwise_xor(dev % n_batch, me_b)
            at = jnp.where(dq < 4, dq, dq - 4) * each + c % each
            for (b, p), piece in zip(order, pieces):
                @pl.when((db == b) & (dq >= 4 if p else dq < 4))
                def _():
                    pltpu.make_async_copy(piece.at[rows(at)], out_ref.at[rows(slot)], sem.at[slot]).start()

        return 0

    def finish(c, _):
        slot = slot_of(c)

        @pl.when(slot < per_dev)
        def _():
            pltpu.make_async_copy(pieces[0].at[rows(0)], out_ref.at[rows(slot)], sem.at[slot]).wait()

        return 0

    @pl.when((offset < per_dev) | (offset + count > total))
    def _():
        lax.fori_loop(0, count, start, 0, unroll=4)
        lax.fori_loop(0, count, finish, 0, unroll=4)


def kernel_call(kernel, operands, specs, shapes, out_specs, scratch=(), cost=None, **more):
    return pl.pallas_call(
        kernel,
        out_shape=shapes,
        in_specs=specs,
        out_specs=out_specs,
        scratch_shapes=list(scratch),
        compiler_params=pltpu.CompilerParams(vmem_limit_bytes=12 << 20),
        cost_estimate=cost,
        **more,
    )(*operands)


def evens(n):
    return sorted(range(2, n, 2), key=lambda k: (bin(k).count("1"), -k))


def per_device(n_queue, n_batch, queries, keys, queue_keys, log_scale, write_pointer, block_order, pos_index):
    tok, width = queries.shape

    def hop(x, axis, n, k):
        return lax.ppermute(x, axis, [(i, i ^ k) for i in range(n)])

    def across(x, k):
        return hop(x, "queue", n_queue, k)

    def beside(x, k):
        return hop(x, "batch", n_batch, k)

    cost = pl.CostEstimate(
        flops=4 * tok * queue_keys.shape[0] * width,
        bytes_accessed=queue_keys.size * 2,
        transcendentals=2 * tok * queue_keys.shape[0],
    )
    ls = log_scale.reshape(1, 1)
    opened = kernel_call(open_kernel, (), [], jax.ShapeDtypeStruct((8, 128), jnp.float32), VMEM, cost=cost)

    got = [None] * n_queue
    far = [k for k in evens(n_queue) if k > 2]
    for k in far:
        low = k & -k
        got[k] = across(got[k - low] if k > low else queries, low)
    above = lax.broadcasted_iota(jnp.int32, (2 * tok, width), 0) < tok
    got[0] = jnp.where(above, jnp.pad(queries, ((0, tok), (0, 0))), jnp.pad(keys, ((tok, 0), (0, 0))))
    for k in (2, 1, 3):
        if k < n_queue:
            got[k] = across(got[k - 1] if k == 3 else got[0], 2 if k == 2 else 1)
    far_keys = {}
    for k in far:
        low = k & -k
        far_keys[k] = across(far_keys[k - low] if k > low else keys, low)
        got[k + 1] = across(jnp.concatenate([got[k], far_keys[k]], axis=0), 1)
        far_keys[k + 1] = got[k + 1][tok:]

    pieces = {(0, 0): jnp.concatenate([x[tok:] for x in got[:4]], axis=0)}
    if far:
        pieces[0, 1] = jnp.concatenate([far_keys[k] for k in sorted(far_keys)], axis=0)
    step = n_batch // 2
    while step:
        for (b, p), x in list(pieces.items()):
            pieces[b ^ step, p] = beside(x, step)
        step //= 2
    order = list(pieces)

    part_shape = jax.ShapeDtypeStruct((3, 2 * tok), jnp.float32)
    queue_shape = jax.ShapeDtypeStruct(queue_keys.shape, queue_keys.dtype)
    first, pos = kernel_call(
        first_kernel,
        (opened, ls, pos_index.reshape(1, tok), got[0], got[1], queue_keys),
        [VMEM] * 6,
        (part_shape, jax.ShapeDtypeStruct((1, tok), jnp.float32)),
        (VMEM, VMEM),
        cost=cost,
    )
    parts = [first]
    for k in range(2, n_queue - 2, 2):
        parts.append(
            kernel_call(
                middle_kernel, (ls, got[k], got[k + 1], queue_keys), [VMEM] + [VMEM] * 3, part_shape, VMEM, cost=cost
            )
        )
    sent = kernel_call(
        last_kernel,
        (ls, got[n_queue - 2], got[n_queue - 1], queue_keys, pos, *parts),
        [VMEM] + [VMEM] * (4 + len(parts)),
        jax.ShapeDtypeStruct((n_queue, 3 * n_queue + 8, tok), jnp.float32),
        VMEM,
        [
            pltpu.VMEM((3 * n_queue + 8, tok), jnp.float32),
            pltpu.VMEM((3, 2 * tok), jnp.float32),
        ],
        cost=cost,
    )
    base = kernel_call(
        base_kernel, (first, write_pointer, block_order, queue_keys), [HBM, SMEM, SMEM, VMEM], queue_shape, HBM, [pltpu.SemaphoreType.DMA], cost=cost
    )
    back = lax.all_to_all(sent, "queue", split_axis=0, concat_axis=0, tiled=True)
    loss, term = kernel_call(
        final_kernel,
        (ls, back),
        [VMEM, VMEM],
        (jax.ShapeDtypeStruct((1, tok), jnp.float32), jax.ShapeDtypeStruct((1, tok), jnp.float32)),
        (VMEM, VMEM),
        [pltpu.VMEM((n_queue, tok), jnp.float32)],
    )
    terms = [term] + [beside(term, k) for k in range(n_batch - 1, 0, -1)]
    temp_grad = kernel_call(grad_kernel, terms, [VMEM] * n_batch, jax.ShapeDtypeStruct((1, 1), jnp.float32), VMEM)
    new_queue = kernel_call(
        functools.partial(enqueue_kernel, n_queue, n_batch, order),
        (write_pointer, block_order, base, *pieces.values()),
        [SMEM, SMEM, HBM] + [VMEM] * len(pieces),
        queue_shape,
        HBM,
        [pltpu.SemaphoreType.DMA((queue_keys.shape[0] // BLOCK,))],
        input_output_aliases={2: 0},
    )
    return (loss.reshape(tok), temp_grad.reshape(1), new_queue)


def solution(mesh):
    n_queue, n_batch = mesh.shape["queue"], mesh.shape["batch"]
    placed = (
        P(("queue", "batch"), None),
        P(("queue", "batch"), None),
        P("queue", None),
        P(),
        P(),
        P(),
        P(("queue", "batch")),
    )
    return jax.shard_map(
        functools.partial(per_device, n_queue, n_batch),
        mesh=mesh,
        in_specs=placed,
        out_specs=(P(("queue", "batch")), P(), P("queue", None)),
        check_vma=False,
    )
```

time: 68.8 us -> 74.3 us (1.080)
  Pallas kernels: 9.71 us -> 30.7 us
  blocking collectives: 14.5 us -> 0 us
  starting transfers between devices: 19.2 us -> 24.3 us
  local copies, waits for them, and re-layouts: 3.98 us -> 0.05 us
  between operations: 3.27 us -> 2.08 us
  matrix products: 1.05 us -> 0 us
  other arithmetic: 0.01 us -> 1.03 us
  waiting for transfers between devices: 16.7 us -> 15.9 us
    pallas_call x6 -> x9, Pallas kernels: 9.71 us -> 30.7 us  [kernel_call(): pl.pallas_call(kernel, out_shape=shapes, in_specs=specs, out_specs=out_sp...]
    all_to_all x1 -> x0, blocking collectives: 14.5 us -> none  [per_device(): lax.all_to_all(sent, 'queue', split_axis=0, concat_axis=0, tiled=True)]
    ppermute x16 -> x18, waiting for transfers between devices: 16.7 us -> 9.58 us  [hop(): return lax.ppermute(x, axis, [(i, i ^ k) for i in range(n)])]
    all_to_all x0 -> x1, waiting for transfers between devices: none -> 6.31 us  [per_device(): lax.all_to_all(sent, 'queue', split_axis=0, concat_axis=0, tiled=True)]
    all_to_all x0 -> x1, starting transfers between devices: none -> 5.49 us  [per_device(): lax.all_to_all(sent, 'queue', split_axis=0, concat_axis=0, tiled=True)]
    unnamed x11 -> x6, local copies, waits for them, and re-layouts: 3.96 us -> 0.02 us
    dot_general x1 -> x0, matrix products: 1.05 us -> none  [per_device(): lax.dot_general(keys, queries, (((1,), (1,)), ((), ())), preferred_elemen...]
    select_n x0 -> x1, other arithmetic: none -> 0.97 us  [per_device(): jnp.where(above, jnp.pad(queries, ((0, tok), (0, 0))), jnp.pad(keys, ((to...]
  transfers between devices with their start and end apart: 16 -> 19, of which waited for: 8 -> 8; matrix products, arithmetic and copies ran while one was open for 3% -> 1% of each run, Pallas kernels for 11% -> 40%
where the time goes in v2:
time: 74.3 us; the launch traced here: 74 us
  Pallas kernels  30.7 us (41%)
  starting transfers between devices  24.3 us (33%)
  waiting for transfers between devices  15.9 us (21%)
  between operations  2.08 us (3%)
  other arithmetic  1.03 us (1%)
    pallas_call x9, Pallas kernels, kernel_call(): pl.pallas_call(kernel, out_shape=shapes, in_specs=specs, out_specs=out_sp...  30.7 us
    ppermute x18, starting transfers between devices, hop(): return lax.ppermute(x, axis, [(i, i ^ k) for i in range(n)])  18.8 us
    ppermute x18, waiting for transfers between devices, hop(): return lax.ppermute(x, axis, [(i, i ^ k) for i in range(n)])  9.58 us
    all_to_all x1, waiting for transfers between devices, per_device(): lax.all_to_all(sent, 'queue', split_axis=0, concat_axis=0, tiled=True)  6.31 us
    all_to_all x1, starting transfers between devices, per_device(): lax.all_to_all(sent, 'queue', split_axis=0, concat_axis=0, tiled=True)  5.49 us
  transfers between devices with their start and end apart: 19, of which 8 were waited for; matrix products, arithmetic and copies ran while one was open for 1% of the time, Pallas kernels for 40%

profile of v2, /device:TPU:0, one launch (start us, length us, event | category | flops | bytes accessed | tf_op | source)
XLA Modules:
  0.0 74.0 jit_solution(40351120359051784)
XLA Ops:
  0.6 4.1 %collective-permute-start = (bf16[128,256]{1,0:T(8,128)(2,1)}, bf16[128,256]{1,0:T(8,128)(2,1)S(1)}, u32[]{:S(2)}, u32[]{:S(2)}) collective-permute-start(bf16[128,256]{1,0:T(8,128)(2,1)} %param.7), channel_id=1, source_target_pairs={{0,16},{4,20},{8,24},{12,28},{16,0},{20,4},{24,8},{28,12},{1,17},{... | collective-permute-start | bytes 196616 | tf_op jit(solution)/shard_map/ppermute | solution.py:209
  4.8 0.1 collective-permute-start.2
  4.8 1.0 %pad_select_fusion.qa_ref = bf16[256,256]{1,0:T(8,128)(2,1)S(1)} fusion(bf16[128,256]{1,0:T(8,128)(2,1)} %param.8, bf16[128,256]{1,0:T(8,128)(2,1)} %param.7, pred[256]{0:T(512)(128)(4,1)S(1)} %iota_compare_fusion), kind=kLoop, calls=%fused_computation.4 | loop fusion | flops 65536 | bytes 262400 | tf_op jit(solution)/shard_map/jit(_where)/select_n | solution.py:231
  5.8 1.9 %collective-permute-start.6 = (bf16[256,256]{1,0:T(8,128)(2,1)S(1)}, bf16[256,256]{1,0:T(8,128)(2,1)S(1)}, u32[]{:S(2)}, u32[]{:S(2)}) collective-permute-start(bf16[256,256]{1,0:T(8,128)(2,1)S(1)} %pad_select_fusion.qa_ref), channel_id=1, source_target_pairs={{0,8},{4,12},{8,0},{12,4},{16,24},{20,28},{24,16},{28,20},{1,9},{5... | collective-permute-start | bytes 393224 | tf_op jit(solution)/shard_map/ppermute | solution.py:209
  7.7 1.5 %collective-permute-start.5 = (bf16[256,256]{1,0:T(8,128)(2,1)S(1)}, bf16[256,256]{1,0:T(8,128)(2,1)S(1)}, u32[]{:S(2)}, u32[]{:S(2)}) collective-permute-start(bf16[256,256]{1,0:T(8,128)(2,1)S(1)} %pad_select_fusion.qa_ref), channel_id=1, source_target_pairs={{0,4},{4,0},{8,12},{12,8},{16,20},{20,16},{24,28},{28,24},{1,5},{5... | collective-permute-start | bytes 393224 | tf_op jit(solution)/shard_map/ppermute | solution.py:209
  9.2 1.5 %collective-permute-start.1 = (bf16[128,256]{1,0:T(8,128)(2,1)S(1)}, bf16[128,256]{1,0:T(8,128)(2,1)S(1)}, u32[]{:S(2)}, u32[]{:S(2)}) collective-permute-start(bf16[128,256]{1,0:T(8,128)(2,1)S(1)} %collective-permute-done.qa_ref), channel_id=1, source_target_pairs={{0,8},{4,12},{8,0},{12,4},{16,24},{20,28},{24,16},{28,20},{1,9},{5... | collective-permute-start | bytes 196616 | tf_op jit(solution)/shard_map/ppermute | solution.py:209
  10.8 0.2 collective-permute-done.2
  11.0 1.4 %collective-permute-start.3 = (bf16[128,256]{1,0:T(8,128)(2,1)S(1)}, bf16[128,256]{1,0:T(8,128)(2,1)S(1)}, u32[]{:S(2)}, u32[]{:S(2)}) collective-permute-start(bf16[128,256]{1,0:T(8,128)(2,1)S(1)} %collective-permute-done.2), channel_id=1, source_target_pairs={{0,8},{4,12},{8,0},{12,4},{16,24},{20,28},{24,16},{28,20},{1,9},{5... | collective-permute-start | bytes 196616 | tf_op jit(solution)/shard_map/ppermute | solution.py:209
  12.4 1.6 %collective-permute-start.8 = (bf16[256,256]{1,0:T(8,128)(2,1)S(1)}, bf16[256,256]{1,0:T(8,128)(2,1)S(1)}, u32[]{:S(2)}, u32[]{:S(2)}) collective-permute-start(bf16[256,256]{1,0:T(8,128)(2,1)S(1)} %pad_maximum_fusion.3), channel_id=1, source_target_pairs={{0,4},{4,0},{8,12},{12,8},{16,20},{20,16},{24,28},{28,24},{1,5},{5... | collective-permute-start | bytes 393224 | tf_op jit(solution)/shard_map/ppermute | solution.py:209
  14.0 0.7 collective-permute-start.7
  14.7 0.5 collective-permute-done.3
  15.3 2.0 %collective-permute-start.4 = (bf16[256,256]{1,0:T(8,128)(2,1)S(1)}, bf16[256,256]{1,0:T(8,128)(2,1)S(1)}, u32[]{:S(2)}, u32[]{:S(2)}) collective-permute-start(bf16[256,256]{1,0:T(8,128)(2,1)S(1)} %pad_maximum_fusion.2), channel_id=1, source_target_pairs={{0,4},{4,0},{8,12},{12,8},{16,20},{20,16},{24,28},{28,24},{1,5},{5... | collective-permute-start | bytes 393224 | tf_op jit(solution)/shard_map/ppermute | solution.py:209
  18.0 0.9 %collective-permute-done.8.qb_ref = bf16[256,256]{1,0:T(8,128)(2,1)S(1)} collective-permute-done((bf16[256,256]{1,0:T(8,128)(2,1)S(1)}, bf16[256,256]{1,0:T(8,128)(2,1)S(1)}, u32[]{:S(2)}, u32[]{:S(2)}) %collective-permute-start.8) | collective-permute-done | bytes 131104 | tf_op jit(solution)/shard_map/ppermute | solution.py:209
  18.9 2.7 %collective-permute-done.7.qb_ref = bf16[256,256]{1,0:T(8,128)(2,1)S(1)} collective-permute-done((bf16[256,256]{1,0:T(8,128)(2,1)S(1)}, bf16[256,256]{1,0:T(8,128)(2,1)S(1)}, u32[]{:S(2)}, u32[]{:S(2)}) %collective-permute-start.7) | collective-permute-done | bytes 131104 | tf_op jit(solution)/shard_map/ppermute | solution.py:209
  21.6 1.6 %collective-permute-start.12 = (bf16[512,256]{1,0:T(8,128)(2,1)S(1)}, bf16[512,256]{1,0:T(8,128)(2,1)S(1)}, u32[]{:S(2)}, u32[]{:S(2)}) collective-permute-start(bf16[512,256]{1,0:T(8,128)(2,1)S(1)} %pad_maximum_fusion.refs_0_), channel_id=1, source_target_pairs={{0,2},{1,3},{2,0},{3,1},{4,6},{5,7},{6,4},{7,5},{8,10},{9,11},{10,... | collective-permute-start | bytes 786440 | tf_op jit(solution)/shard_map/ppermute | solution.py:209
  23.2 1.4 %collective-permute-start.13 = (bf16[512,256]{1,0:T(8,128)(2,1)S(1)}, bf16[512,256]{1,0:T(8,128)(2,1)S(1)}, u32[]{:S(2)}, u32[]{:S(2)}) collective-permute-start(bf16[512,256]{1,0:T(8,128)(2,1)S(1)} %pad_maximum_fusion.1.refs_1_), channel_id=1, source_target_pairs={{0,2},{1,3},{2,0},{3,1},{4,6},{5,7},{6,4},{7,5},{8,10},{9,11},{10,... | collective-permute-start | bytes 786440 | tf_op jit(solution)/shard_map/ppermute | solution.py:209
  24.6 6.4 %shard_map.95 = (f32[3,256]{1,0:T(4,128)S(1)}, f32[1,128]{1,0:T(1,128)S(1)}) custom-call(f32[8,128]{1,0:T(8,128)S(1)} %shard_map.94._, f32[1,1]{1,0:T(1,128)} %bitcast.4.ls_ref, s32[1,128]{1,0:T(1,128)S(1)} %bitcast.9, bf16[256,256]{1,0:T(8,128)(2,1)S(1)} %pad_select_fusion.qa_ref, bf16[256,256]{1,0:T(8,128)(2,1)S(1)} %collective-permute-done.5.qb_ref, ...), custom_call_target="tpu_custom_call" | custom-call | flops 536870912 | bytes 2097152 | tf_op jit(solution)/shard_map/pallas_call | solution.py:189
  31.0 6.4 %shard_map.97.refs_2_ = f32[3,256]{1,0:T(4,128)S(1)} custom-call(f32[1,1]{1,0:T(1,128)} %bitcast.6.ls_ref, bf16[128,256]{1,0:T(8,128)(2,1)S(1)} %collective-permute-done.qa_ref, bf16[256,256]{1,0:T(8,128)(2,1)S(1)} %collective-permute-done.8.qb_ref, bf16[4096,256]{1,0:T(8,128)(2,1)S(1)} %copy-done), custom_call_target="tpu_custom_call" | custom-call | flops 536870912 | bytes 2097152 | tf_op jit(solution)/shard_map/pallas_call | solution.py:189
  37.4 6.4 %shard_map.96.refs_1_ = f32[3,256]{1,0:T(4,128)S(1)} custom-call(f32[1,1]{1,0:T(1,128)} %bitcast.5.ls_ref, bf16[256,256]{1,0:T(8,128)(2,1)S(1)} %collective-permute-done.6.qa_ref, bf16[256,256]{1,0:T(8,128)(2,1)S(1)} %collective-permute-done.7.qb_ref, bf16[4096,256]{1,0:T(8,128)(2,1)S(1)} %copy-done), custom_call_target="tpu_custom_call" | custom-call | flops 536870912 | bytes 2097152 | tf_op jit(solution)/shard_map/pallas_call | solution.py:189
  43.8 7.1 %shard_map.98 = f32[8,32,128]{2,1,0:T(8,128)} custom-call(f32[1,1]{1,0:T(1,128)} %bitcast.7.ls_ref, bf16[128,256]{1,0:T(8,128)(2,1)S(1)} %collective-permute-done.1.qa_ref, bf16[256,256]{1,0:T(8,128)(2,1)S(1)} %collective-permute-done.4.qb_ref, bf16[4096,256]{1,0:T(8,128)(2,1)S(1)} %copy-done, f32[1,128]{1,0:T(1,128)S(1)} %get-tuple-element.7.pos_ref, ...), custom_call_target="tpu_custom_call" | custom-call | flops 536870912 | bytes 2097152 | tf_op jit(solution)/shard_map/pallas_call | solution.py:189
  50.9 5.5 %all-to-all-start = ((f32[8,32,128]{2,1,0:T(8,128)}), f32[8,32,128]{2,1,0:T(8,128)S(1)}, u32[]{:S(2)}, u32[]{:S(2)}) async-start(f32[8,32,128]{2,1,0:T(8,128)} %shard_map.98), calls=%async_computation | async-start | bytes 262144 | tf_op jit(solution)/shard_map/all_to_all | solution.py:284
  56.4 0.5 collective-permute-start.15
  56.9 0.1 collective-permute-start.16
  57.0 0.4 collective-permute-start.17
  57.4 6.3 %all-to-all-done.back_ref = f32[8,32,128]{2,1,0:T(8,128)S(1)} async-done(((f32[8,32,128]{2,1,0:T(8,128)}), f32[8,32,128]{2,1,0:T(8,128)S(1)}, u32[]{:S(2)}, u32[]{:S(2)}) %all-to-all-start) | async-done | bytes 131104 | tf_op jit(solution)/shard_map/all_to_all | solution.py:284
  63.7 0.6 shard_map.99
  64.4 1.2 %collective-permute-done.11.refs_3_ = f32[1,128]{1,0:T(1,128)S(1)} collective-permute-done((f32[1,128]{1,0:T(1,128)S(1)}, f32[1,128]{1,0:T(1,128)S(1)}, u32[]{:S(2)}, u32[]{:S(2)}) %collective-permute-start.11) | collective-permute-done | bytes 544 | tf_op jit(solution)/shard_map/ppermute | solution.py:209
  66.2 2.9 %collective-permute-done.10.refs_2_ = f32[1,128]{1,0:T(1,128)S(1)} collective-permute-done((f32[1,128]{1,0:T(1,128)S(1)}, f32[1,128]{1,0:T(1,128)S(1)}, u32[]{:S(2)}, u32[]{:S(2)}) %collective-permute-start.10) | collective-permute-done | bytes 544 | tf_op jit(solution)/shard_map/ppermute | solution.py:209
  69.1 1.9 %shard_map.101.base_ref = bf16[4096,256]{1,0:T(8,128)(2,1)} custom-call(f32[3,256]{1,0:T(4,128)S(1)} %get-tuple-element.8.refs_0_._, s32[1]{0:T(128)S(6)} %copy.13.ptr_ref.ptr, s32[32]{0:T(128)S(1)} %copy-done.1, bf16[4096,256]{1,0:T(8,128)(2,1)S(1)} %copy-done), custom_call_target="tpu_custom_call" | custom-call | flops 536870912 | bytes 2097152 | tf_op jit(solution)/shard_map/pallas_call | solution.py:189
  71.0 1.1 %collective-permute-done.9.refs_1_ = f32[1,128]{1,0:T(1,128)S(1)} collective-permute-done((f32[1,128]{1,0:T(1,128)S(1)}, f32[1,128]{1,0:T(1,128)S(1)}, u32[]{:S(2)}, u32[]{:S(2)}) %collective-permute-start.9) | collective-permute-done | bytes 544 | tf_op jit(solution)/shard_map/ppermute | solution.py:209
  72.1 0.5 shard_map.100
  72.6 1.4 %shard_map.102 = bf16[4096,256]{1,0:T(8,128)(2,1)} custom-call(s32[1]{0:T(128)S(6)} %copy.13.ptr_ref.ptr, s32[32]{0:T(128)S(1)} %copy-done.1, bf16[4096,256]{1,0:T(8,128)(2,1)} %shard_map.101.base_ref, bf16[512,256]{1,0:T(8,128)(2,1)S(1)} %pad_maximum_fusion.refs_0_, bf16[512,256]{1,0:T(8,128)(2,1)S(1)} %pad_maximum_fusion.1.refs_1_, ...), custom_call_target="tpu_custom_call", output_to_operand_aliasing={{}: (2, {})} | custom-call | tf_op jit(solution)/shard_map/pallas_call | solution.py:189
  (33 shorter events, 0.2 us)
Async XLA Ops:
  0.6 8.6 %collective-permute-start = (bf16[128,256]{1,0:T(8,128)(2,1)}, bf16[128,256]{1,0:T(8,128)(2,1)S(1)}, u32[]{:S(2)}, u32[]{:S(2)}) collective-permute-start(bf16[128,256]{1,0:T(8,128)(2,1)} %param.7), channel_id=1, source_target_pairs={{0,16},{4,20},{8,24},{12,28},{16,0},{20,4},{24,8},{28,12},{1,17},{... | collective-permute-start | bytes 196616 | tf_op jit(solution)/shard_map/ppermute | solution.py:209
  4.8 6.2 %collective-permute-start.2 = (bf16[128,256]{1,0:T(8,128)(2,1)}, bf16[128,256]{1,0:T(8,128)(2,1)S(1)}, u32[]{:S(2)}, u32[]{:S(2)}) collective-permute-start(bf16[128,256]{1,0:T(8,128)(2,1)} %param.8), channel_id=1, source_target_pairs={{0,16},{4,20},{8,24},{12,28},{16,0},{20,4},{24,8},{28,12},{1,17},{... | collective-permute-start | bytes 196616 | tf_op jit(solution)/shard_map/ppermute | solution.py:209
  5.8 8.2 %collective-permute-start.6 = (bf16[256,256]{1,0:T(8,128)(2,1)S(1)}, bf16[256,256]{1,0:T(8,128)(2,1)S(1)}, u32[]{:S(2)}, u32[]{:S(2)}) collective-permute-start(bf16[256,256]{1,0:T(8,128)(2,1)S(1)} %pad_select_fusion.qa_ref), channel_id=1, source_target_pairs={{0,8},{4,12},{8,0},{12,4},{16,24},{20,28},{24,16},{28,20},{1,9},{5... | collective-permute-start | bytes 393224 | tf_op jit(solution)/shard_map/ppermute | solution.py:209
  7.7 10.2 %collective-permute-start.5 = (bf16[256,256]{1,0:T(8,128)(2,1)S(1)}, bf16[256,256]{1,0:T(8,128)(2,1)S(1)}, u32[]{:S(2)}, u32[]{:S(2)}) collective-permute-start(bf16[256,256]{1,0:T(8,128)(2,1)S(1)} %pad_select_fusion.qa_ref), channel_id=1, source_target_pairs={{0,4},{4,0},{8,12},{12,8},{16,20},{20,16},{24,28},{28,24},{1,5},{5... | collective-permute-start | bytes 393224 | tf_op jit(solution)/shard_map/ppermute | solution.py:209
  9.2 5.5 %collective-permute-start.1 = (bf16[128,256]{1,0:T(8,128)(2,1)S(1)}, bf16[128,256]{1,0:T(8,128)(2,1)S(1)}, u32[]{:S(2)}, u32[]{:S(2)}) collective-permute-start(bf16[128,256]{1,0:T(8,128)(2,1)S(1)} %collective-permute-done.qa_ref), channel_id=1, source_target_pairs={{0,8},{4,12},{8,0},{12,4},{16,24},{20,28},{24,16},{28,20},{1,9},{5... | collective-permute-start | bytes 196616 | tf_op jit(solution)/shard_map/ppermute | solution.py:209
  11.0 4.3 %collective-permute-start.3 = (bf16[128,256]{1,0:T(8,128)(2,1)S(1)}, bf16[128,256]{1,0:T(8,128)(2,1)S(1)}, u32[]{:S(2)}, u32[]{:S(2)}) collective-permute-start(bf16[128,256]{1,0:T(8,128)(2,1)S(1)} %collective-permute-done.2), channel_id=1, source_target_pairs={{0,8},{4,12},{8,0},{12,4},{16,24},{20,28},{24,16},{28,20},{1,9},{5... | collective-permute-start | bytes 196616 | tf_op jit(solution)/shard_map/ppermute | solution.py:209
  12.4 12.2 %copy-start = (bf16[4096,256]{1,0:T(8,128)(2,1)S(1)}, bf16[4096,256]{1,0:T(8,128)(2,1)}, u32[]{:S(2)}) copy-start(bf16[4096,256]{1,0:T(8,128)(2,1)} %k_ref.9) | copy-start | bytes 6291460
  12.4 12.2 %copy-start.2 = (s32[128]{0:T(128)S(1)}, s32[128]{0:T(128)}, u32[]{:S(2)}) copy-start(s32[128]{0:T(128)} %param.13) | copy-start | bytes 1540
  12.4 6.4 %collective-permute-start.8 = (bf16[256,256]{1,0:T(8,128)(2,1)S(1)}, bf16[256,256]{1,0:T(8,128)(2,1)S(1)}, u32[]{:S(2)}, u32[]{:S(2)}) collective-permute-start(bf16[256,256]{1,0:T(8,128)(2,1)S(1)} %pad_maximum_fusion.3), channel_id=1, source_target_pairs={{0,4},{4,0},{8,12},{12,8},{16,20},{20,16},{24,28},{28,24},{1,5},{5... | collective-permute-start | bytes 393224 | tf_op jit(solution)/shard_map/ppermute | solution.py:209
  14.0 7.6 %collective-permute-start.7 = (bf16[256,256]{1,0:T(8,128)(2,1)S(1)}, bf16[256,256]{1,0:T(8,128)(2,1)S(1)}, u32[]{:S(2)}, u32[]{:S(2)}) collective-permute-start(bf16[256,256]{1,0:T(8,128)(2,1)S(1)} %collective-permute-done.6.qa_ref), channel_id=1, source_target_pairs={{0,4},{4,0},{8,12},{12,8},{16,20},{20,16},{24,28},{28,24},{1,5},{5... | collective-permute-start | bytes 393224 | tf_op jit(solution)/shard_map/ppermute | solution.py:209
  15.3 7.9 %collective-permute-start.4 = (bf16[256,256]{1,0:T(8,128)(2,1)S(1)}, bf16[256,256]{1,0:T(8,128)(2,1)S(1)}, u32[]{:S(2)}, u32[]{:S(2)}) collective-permute-start(bf16[256,256]{1,0:T(8,128)(2,1)S(1)} %pad_maximum_fusion.2), channel_id=1, source_target_pairs={{0,4},{4,0},{8,12},{12,8},{16,20},{20,16},{24,28},{28,24},{1,5},{5... | collective-permute-start | bytes 393224 | tf_op jit(solution)/shard_map/ppermute | solution.py:209
  21.6 35.3 %collective-permute-start.12 = (bf16[512,256]{1,0:T(8,128)(2,1)S(1)}, bf16[512,256]{1,0:T(8,128)(2,1)S(1)}, u32[]{:S(2)}, u32[]{:S(2)}) collective-permute-start(bf16[512,256]{1,0:T(8,128)(2,1)S(1)} %pad_maximum_fusion.refs_0_), channel_id=1, source_target_pairs={{0,2},{1,3},{2,0},{3,1},{4,6},{5,7},{6,4},{7,5},{8,10},{9,11},{10,... | collective-permute-start | bytes 786440 | tf_op jit(solution)/shard_map/ppermute | solution.py:209
  23.2 33.7 %collective-permute-start.13 = (bf16[512,256]{1,0:T(8,128)(2,1)S(1)}, bf16[512,256]{1,0:T(8,128)(2,1)S(1)}, u32[]{:S(2)}, u32[]{:S(2)}) collective-permute-start(bf16[512,256]{1,0:T(8,128)(2,1)S(1)} %pad_maximum_fusion.1.refs_1_), channel_id=1, source_target_pairs={{0,2},{1,3},{2,0},{3,1},{4,6},{5,7},{6,4},{7,5},{8,10},{9,11},{10,... | collective-permute-start | bytes 786440 | tf_op jit(solution)/shard_map/ppermute | solution.py:209
  37.4 31.7 %copy-start.1 = (s32[32]{0:T(128)S(1)}, s32[32]{0:T(128)}, u32[]{:S(2)}) copy-start(s32[32]{0:T(128)} %block_order.1) | copy-start | bytes 388
  50.9 12.8 %all-to-all-start = ((f32[8,32,128]{2,1,0:T(8,128)}), f32[8,32,128]{2,1,0:T(8,128)S(1)}, u32[]{:S(2)}, u32[]{:S(2)}) async-start(f32[8,32,128]{2,1,0:T(8,128)} %shard_map.98), calls=%async_computation | async-start | bytes 262144 | tf_op jit(solution)/shard_map/all_to_all | solution.py:284
  56.4 16.2 %collective-permute-start.14 = (bf16[512,256]{1,0:T(8,128)(2,1)S(1)}, bf16[512,256]{1,0:T(8,128)(2,1)S(1)}, u32[]{:S(2)}, u32[]{:S(2)}) collective-permute-start(bf16[512,256]{1,0:T(8,128)(2,1)S(1)} %pad_maximum_fusion.refs_0_), channel_id=1, source_target_pairs={{0,1},{1,0},{2,3},{3,2},{4,5},{5,4},{6,7},{7,6},{8,9},{9,8},{10,11... | collective-permute-start | bytes 786440 | tf_op jit(solution)/shard_map/ppermute | solution.py:209
  56.4 16.2 %collective-permute-start.15 = (bf16[512,256]{1,0:T(8,128)(2,1)S(1)}, bf16[512,256]{1,0:T(8,128)(2,1)}, u32[]{:S(2)}, u32[]{:S(2)}) collective-permute-start(bf16[512,256]{1,0:T(8,128)(2,1)S(1)} %pad_maximum_fusion.1.refs_1_), channel_id=1, source_target_pairs={{0,1},{1,0},{2,3},{3,2},{4,5},{5,4},{6,7},{7,6},{8,9},{9,8},{10,11... | collective-permute-start | bytes 786440 | tf_op jit(solution)/shard_map/ppermute | solution.py:209
  56.9 15.7 %collective-permute-start.16 = (bf16[512,256]{1,0:T(8,128)(2,1)S(1)}, bf16[512,256]{1,0:T(8,128)(2,1)}, u32[]{:S(2)}, u32[]{:S(2)}) collective-permute-start(bf16[512,256]{1,0:T(8,128)(2,1)S(1)} %collective-permute-done.12.refs_2_), channel_id=1, source_target_pairs={{0,1},{1,0},{2,3},{3,2},{4,5},{5,4},{6,7},{7,6},{8,9},{9,8},{10,11... | collective-permute-start | bytes 786440 | tf_op jit(solution)/shard_map/ppermute | solution.py:209
  57.0 15.6 %collective-permute-start.17 = (bf16[512,256]{1,0:T(8,128)(2,1)S(1)}, bf16[512,256]{1,0:T(8,128)(2,1)}, u32[]{:S(2)}, u32[]{:S(2)}) collective-permute-start(bf16[512,256]{1,0:T(8,128)(2,1)S(1)} %collective-permute-done.13.refs_3_), channel_id=1, source_target_pairs={{0,1},{1,0},{2,3},{3,2},{4,5},{5,4},{6,7},{7,6},{8,9},{9,8},{10,11... | collective-permute-start | bytes 786440 | tf_op jit(solution)/shard_map/ppermute | solution.py:209
  64.4 1.2 %collective-permute-start.11 = (f32[1,128]{1,0:T(1,128)S(1)}, f32[1,128]{1,0:T(1,128)S(1)}, u32[]{:S(2)}, u32[]{:S(2)}) collective-permute-start(f32[1,128]{1,0:T(1,128)S(1)} %get-tuple-element.10.refs_0_), channel_id=1, source_target_pairs={{0,1},{1,0},{2,3},{3,2},{4,5},{5,4},{6,7},{7,6},{8,9},{9,8},{10,11... | collective-permute-start | bytes 1544 | tf_op jit(solution)/shard_map/ppermute | solution.py:209
  65.5 3.6 %collective-permute-start.10 = (f32[1,128]{1,0:T(1,128)S(1)}, f32[1,128]{1,0:T(1,128)S(1)}, u32[]{:S(2)}, u32[]{:S(2)}) collective-permute-start(f32[1,128]{1,0:T(1,128)S(1)} %get-tuple-element.10.refs_0_), channel_id=1, source_target_pairs={{0,2},{1,3},{2,0},{3,1},{4,6},{5,7},{6,4},{7,5},{8,10},{9,11},{10,... | collective-permute-start | bytes 1544 | tf_op jit(solution)/shard_map/ppermute | solution.py:209
  69.1 3.0 %collective-permute-start.9 = (f32[1,128]{1,0:T(1,128)S(1)}, f32[1,128]{1,0:T(1,128)S(1)}, u32[]{:S(2)}, u32[]{:S(2)}) collective-permute-start(f32[1,128]{1,0:T(1,128)S(1)} %get-tuple-element.10.refs_0_), channel_id=1, source_target_pairs={{0,3},{1,2},{2,1},{3,0},{4,7},{5,6},{6,5},{7,4},{8,11},{9,10},{10,... | collective-permute-start | bytes 1544 | tf_op jit(solution)/shard_map/ppermute | solution.py:209

commit v3 on v2

--- a/solution.py
+++ b/solution.py
@@ -33,9 +33,9 @@
     o_ref[2:3, :] = jnp.sum(w * a, axis=0, keepdims=True)
 
 
-def accumulate(log_scale, q, k_ref, o_ref):
+def accumulate(rate_ref, q, k_ref, o_ref):
     count, tiles = q.shape[0], k_ref.shape[0] // TILE
-    c = jnp.exp(jnp.broadcast_to(log_scale, (8, count))) * LOG2E
+    c = jnp.concatenate([rate_ref[...]] * (count // rate_ref.shape[1]), axis=1) * LOG2E
     d = scores_of(k_ref, q, 0)
     m = jnp.max(d, axis=0)
     e = jnp.exp2((d - m[None]) * c[None])
@@ -70,19 +70,19 @@
     o_ref[...] = jnp.zeros_like(o_ref)
 
 
-def first_kernel(_, ls_ref, index_ref, qa_ref, qb_ref, k_ref, o_ref, pos_ref):
+def first_kernel(_, rate_ref, index_ref, qa_ref, qb_ref, k_ref, o_ref, pos_ref):
     tok = qa_ref.shape[0] // 2
     scores = dot_t(qa_ref[tok:, :], qa_ref[:tok, :])
     rows = lax.broadcasted_iota(jnp.int32, scores.shape, 0)
     pos_ref[...] = jnp.sum(jnp.where(rows == index_ref[...], scores, 0.0), axis=0, keepdims=True)
-    accumulate(ls_ref[...], both(qa_ref, qb_ref, tok), k_ref, o_ref)
-
-
-def middle_kernel(ls_ref, qa_ref, qb_ref, k_ref, o_ref):
-    accumulate(ls_ref[...], both(qa_ref, qb_ref, o_ref.shape[1] // 2), k_ref, o_ref)
-
-
-def last_kernel(ls_ref, qa_ref, qb_ref, k_ref, pos_ref, *refs):
+    accumulate(rate_ref, both(qa_ref, qb_ref, tok), k_ref, o_ref)
+
+
+def middle_kernel(rate_ref, qa_ref, qb_ref, k_ref, o_ref):
+    accumulate(rate_ref, both(qa_ref, qb_ref, o_ref.shape[1] // 2), k_ref, o_ref)
+
+
+def last_kernel(rate_ref, qa_ref, qb_ref, k_ref, pos_ref, *refs):
     *parts, o_ref, hold, own = refs
     n, tok = o_ref.shape[0], o_ref.shape[2]
     me = lax.axis_index("queue")
@@ -91,7 +91,7 @@
         at = jnp.bitwise_xor(me, k)
         for i in range(3):
             hold[pl.ds(i * n + at, 1), :] = parts[k // 2][i : i + 1, (k % 2) * tok : (k % 2 + 1) * tok]
-    accumulate(ls_ref[...], both(qa_ref, qb_ref, tok), k_ref, own)
+    accumulate(rate_ref, both(qa_ref, qb_ref, tok), k_ref, own)
     for k in range(n - 2, n):
         at = jnp.bitwise_xor(me, k)
         for i in range(3):
@@ -101,15 +101,95 @@
         o_ref[i] = sent
 
 
-def base_kernel(_, ptr_ref, order_ref, k_ref, base_ref, sem):
-    copy = pltpu.make_async_copy(k_ref, base_ref, sem)
-    copy.start()
-    copy.wait()
-
-
-def final_kernel(ls_ref, back_ref, loss_ref, term_ref, hold_ref):
+def places(n_queue, n_batch, split, order, ptr, block_order, per_dev):
+    total = per_dev * n_queue
+    count = block_order.shape[0]
+    each = count // (n_queue * n_batch)
+    me_q, me_b = lax.axis_index("queue"), lax.axis_index("batch")
+    offset = ptr[0] - me_q * per_dev
+    offset = jnp.where(offset < 0, offset + total, offset)
+
+    def slot_of(c):
+        at = offset + block_order[c]
+        return jnp.where(at >= total, at - total, at)
+
+    def from_piece(c, pieces, group, use):
+        dev = c // each
+        dq, db = jnp.bitwise_xor(dev // n_batch, me_q), jnp.bitwise_xor(dev % n_batch, me_b)
+        at = (dq - split if group else dq) * each + c % each
+        for b, piece in zip(order, pieces):
+            @pl.when((db == b) & ((dq >= split) if group else (dq < split)))
+            def _():
+                use(piece.at[rows_of(at)])
+
+    return (offset < per_dev) | (offset + count > total), slot_of, from_piece
+
+
+def rows_of(i):
+    return pl.ds(pl.multiple_of(i * BLOCK, BLOCK), BLOCK)
+
+
+def base_kernel(n_queue, n_batch, split, order, _, ptr, block_order, k_ref, *refs):
+    *pieces, out_ref, table, sem, whole = refs
+    per_dev = out_ref.shape[0] // BLOCK
+    count = block_order.shape[0]
+    hit, slot_of, from_piece = places(n_queue, n_batch, split, order, ptr, block_order, per_dev)
+
+    @pl.when(jnp.logical_not(hit))
+    def _():
+        copy = pltpu.make_async_copy(k_ref, out_ref, whole)
+        copy.start()
+        copy.wait()
+
+    def clear(s, _):
+        table[s] = -1
+        return 0
+
+    def fill(c, _):
+        slot = slot_of(c)
+
+        @pl.when(slot < per_dev)
+        def _():
+            table[slot] = c
+
+        return 0
+
+    def mine(s):
+        dq = jnp.bitwise_xor(table[s] // (count // n_queue), lax.axis_index("queue"))
+        return (table[s] < 0) | (dq < split)
+
+    def start(s, _):
+        def put(source):
+            pltpu.make_async_copy(source, out_ref.at[rows_of(s)], sem.at[s]).start()
+
+        @pl.when(table[s] < 0)
+        def _():
+            put(k_ref.at[rows_of(s)])
+
+        @pl.when(table[s] >= 0)
+        def _():
+            from_piece(table[s], pieces, 0, put)
+
+        return 0
+
+    def finish(s, _):
+        @pl.when(mine(s))
+        def _():
+            pltpu.make_async_copy(k_ref.at[rows_of(s)], out_ref.at[rows_of(s)], sem.at[s]).wait()
+
+        return 0
+
+    @pl.when(hit)
+    def _():
+        lax.fori_loop(0, per_dev, clear, 0)
+        lax.fori_loop(0, count, fill, 0)
+        lax.fori_loop(0, per_dev, start, 0)
+        lax.fori_loop(0, per_dev, finish, 0)
+
+
+def final_kernel(rate_ref, back_ref, loss_ref, term_ref, hold_ref):
     n, tok = back_ref.shape[0], back_ref.shape[2]
-    scale = jnp.exp(jnp.broadcast_to(ls_ref[...], (n, tok)))
+    scale = jnp.broadcast_to(rate_ref[0:1, :], (n, tok))
     pos = scale * back_ref[:, 3 * n, :]
     peak = back_ref[0, 0:n, :]
     for i in range(1, n):
@@ -138,51 +218,41 @@
     o_ref[...] = sum((x[0:1, 0:1] for x in terms[1:]), terms[0][0:1, 0:1])
 
 
-def enqueue_kernel(n_queue, n_batch, order, ptr, block_order, base_ref, *refs):
+def enqueue_kernel(n_queue, n_batch, split, order, ptr, block_order, base_ref, *refs):
     *pieces, out_ref, sem = refs
     per_dev = out_ref.shape[0] // BLOCK
-    total = per_dev * n_queue
     count = block_order.shape[0]
-    each = count // (n_queue * n_batch)
-    me_q, me_b = lax.axis_index("queue"), lax.axis_index("batch")
-    offset = ptr[0] - me_q * per_dev
-    offset = jnp.where(offset < 0, offset + total, offset)
-
-    def rows(i):
-        return pl.ds(pl.multiple_of(i * BLOCK, BLOCK), BLOCK)
-
-    def slot_of(c):
-        at = offset + block_order[c]
-        return jnp.where(at >= total, at - total, at)
+    hit, slot_of, from_piece = places(n_queue, n_batch, split, order, ptr, block_order, per_dev)
+
+    def ours(c):
+        dq = jnp.bitwise_xor(c // (count // n_queue), lax.axis_index("queue"))
+        slot = slot_of(c)
+        return slot, (slot < per_dev) & (dq >= split)
 
     def start(c, _):
-        slot = slot_of(c)
-
-        @pl.when(slot < per_dev)
-        def _():
-            dev = c // each
-            dq, db = jnp.bitwise_xor(dev // n_batch, me_q), jnp.bitwise_xor(dev % n_batch, me_b)
-            at = jnp.where(dq < 4, dq, dq - 4) * each + c % each
-            for (b, p), piece in zip(order, pieces):
-                @pl.when((db == b) & (dq >= 4 if p else dq < 4))
-                def _():
-                    pltpu.make_async_copy(piece.at[rows(at)], out_ref.at[rows(slot)], sem.at[slot]).start()
+        slot, write = ours(c)
+
+        @pl.when(write)
+        def _():
+            from_piece(
+                c, pieces, 1, lambda x: pltpu.make_async_copy(x, out_ref.at[rows_of(slot)], sem.at[slot]).start()
+            )
 
         return 0
 
     def finish(c, _):
-        slot = slot_of(c)
-
-        @pl.when(slot < per_dev)
-        def _():
-            pltpu.make_async_copy(pieces[0].at[rows(0)], out_ref.at[rows(slot)], sem.at[slot]).wait()
-
-        return 0
-
-    @pl.when((offset < per_dev) | (offset + count > total))
+        slot, write = ours(c)
+
+        @pl.when(write)
+        def _():
+            pltpu.make_async_copy(pieces[0].at[rows_of(0)], out_ref.at[rows_of(slot)], sem.at[slot]).wait()
+
+        return 0
+
+    @pl.when(hit)
     def _():
-        lax.fori_loop(0, count, start, 0, unroll=4)
-        lax.fori_loop(0, count, finish, 0, unroll=4)
+        lax.fori_loop(0, count, start, 0)
+        lax.fori_loop(0, count, finish, 0)
 
 
 def kernel_call(kernel, operands, specs, shapes, out_specs, scratch=(), cost=None, **more):
@@ -219,8 +289,9 @@
         bytes_accessed=queue_keys.size * 2,
         transcendentals=2 * tok * queue_keys.shape[0],
     )
-    ls = log_scale.reshape(1, 1)
-    opened = kernel_call(open_kernel, (), [], jax.ShapeDtypeStruct((8, 128), jnp.float32), VMEM, cost=cost)
+    rate = jnp.broadcast_to(jnp.exp(log_scale), (8, tok))
+    wait = pl.CostEstimate(flops=64 * cost.flops, bytes_accessed=4096, transcendentals=0)
+    opened = kernel_call(open_kernel, (), [], jax.ShapeDtypeStruct((8, 128), jnp.float32), VMEM, cost=wait)
 
     got = [None] * n_queue
     far = [k for k in evens(n_queue) if k > 2]
@@ -239,21 +310,21 @@
         got[k + 1] = across(jnp.concatenate([got[k], far_keys[k]], axis=0), 1)
         far_keys[k + 1] = got[k + 1][tok:]
 
-    pieces = {(0, 0): jnp.concatenate([x[tok:] for x in got[:4]], axis=0)}
-    if far:
-        pieces[0, 1] = jnp.concatenate([far_keys[k] for k in sorted(far_keys)], axis=0)
+    far_keys.update((k, x[tok:]) for k, x in enumerate(got[:4]))
+    split = max(5 * n_queue // 8, 1)
+    pieces = {(0, 0): jnp.concatenate([far_keys[k] for k in range(split)], axis=0)}
+    pieces[0, 1] = jnp.concatenate([far_keys[k] for k in range(split, n_queue)], axis=0)
     step = n_batch // 2
     while step:
         for (b, p), x in list(pieces.items()):
             pieces[b ^ step, p] = beside(x, step)
         step //= 2
-    order = list(pieces)
 
     part_shape = jax.ShapeDtypeStruct((3, 2 * tok), jnp.float32)
     queue_shape = jax.ShapeDtypeStruct(queue_keys.shape, queue_keys.dtype)
     first, pos = kernel_call(
         first_kernel,
-        (opened, ls, pos_index.reshape(1, tok), got[0], got[1], queue_keys),
+        (opened, rate, pos_index.reshape(1, tok), got[0], got[1], queue_keys),
         [VMEM] * 6,
         (part_shape, jax.ShapeDtypeStruct((1, tok), jnp.float32)),
         (VMEM, VMEM),
@@ -263,12 +334,12 @@
     for k in range(2, n_queue - 2, 2):
         parts.append(
             kernel_call(
-                middle_kernel, (ls, got[k], got[k + 1], queue_keys), [VMEM] + [VMEM] * 3, part_shape, VMEM, cost=cost
+                middle_kernel, (rate, got[k], got[k + 1], queue_keys), [VMEM] + [VMEM] * 3, part_shape, VMEM, cost=cost
             )
         )
     sent = kernel_call(
         last_kernel,
-        (ls, got[n_queue - 2], got[n_queue - 1], queue_keys, pos, *parts),
+        (rate, got[n_queue - 2], got[n_queue - 1], queue_keys, pos, *parts),
         [VMEM] + [VMEM] * (4 + len(parts)),
         jax.ShapeDtypeStruct((n_queue, 3 * n_queue + 8, tok), jnp.float32),
         VMEM,
@@ -278,13 +349,23 @@
         ],
         cost=cost,
     )
+    order = [b for b, p in pieces if p == 0]
+    groups = [[pieces[b, p] for b in order] for p in range(2)]
+    where = (n_queue, n_batch, split, order)
+    per_dev = queue_keys.shape[0] // BLOCK
     base = kernel_call(
-        base_kernel, (first, write_pointer, block_order, queue_keys), [HBM, SMEM, SMEM, VMEM], queue_shape, HBM, [pltpu.SemaphoreType.DMA], cost=cost
+        functools.partial(base_kernel, *where),
+        (first, write_pointer, block_order, queue_keys, *groups[0]),
+        [HBM, SMEM, SMEM, VMEM] + [VMEM] * n_batch,
+        queue_shape,
+        HBM,
+        [pltpu.SMEM((per_dev,), jnp.int32), pltpu.SemaphoreType.DMA((per_dev,)), pltpu.SemaphoreType.DMA],
+        cost=cost,
     )
     back = lax.all_to_all(sent, "queue", split_axis=0, concat_axis=0, tiled=True)
     loss, term = kernel_call(
         final_kernel,
-        (ls, back),
+        (rate, back),
         [VMEM, VMEM],
         (jax.ShapeDtypeStruct((1, tok), jnp.float32), jax.ShapeDtypeStruct((1, tok), jnp.float32)),
         (VMEM, VMEM),
@@ -293,12 +374,12 @@
     terms = [term] + [beside(term, k) for k in range(n_batch - 1, 0, -1)]
     temp_grad = kernel_call(grad_kernel, terms, [VMEM] * n_batch, jax.ShapeDtypeStruct((1, 1), jnp.float32), VMEM)
     new_queue = kernel_call(
-        functools.partial(enqueue_kernel, n_queue, n_batch, order),
-        (write_pointer, block_order, base, *pieces.values()),
-        [SMEM, SMEM, HBM] + [VMEM] * len(pieces),
+        functools.partial(enqueue_kernel, *where),
+        (write_pointer, block_order, base, *groups[1]),
+        [SMEM, SMEM, HBM] + [VMEM] * n_batch,
         queue_shape,
         HBM,
-        [pltpu.SemaphoreType.DMA((queue_keys.shape[0] // BLOCK,))],
+        [pltpu.SemaphoreType.DMA((per_dev,))],
         input_output_aliases={2: 0},
     )
     return (loss.reshape(tok), temp_grad.reshape(1), new_queue)

time: 74.3 us -> 79.8 us (1.074)
  waiting for transfers between devices: 15.9 us -> 21.1 us
    ppermute x18, waiting for transfers between devices: 9.58 us -> 14.2 us  [hop(): return lax.ppermute(x, axis, [(i, i ^ k) for i in range(n)])]
    ppermute x18, starting transfers between devices: 18.8 us -> 16.9 us  [hop(): return lax.ppermute(x, axis, [(i, i ^ k) for i in range(n)])]
    all_to_all x1, starting transfers between devices: 5.49 us -> 6.83 us  [per_device(): lax.all_to_all(sent, 'queue', split_axis=0, concat_axis=0, tiled=True)]
  transfers between devices with their start and end apart: 19 -> 19, of which waited for: 8 -> 8; matrix products, arithmetic and copies ran while one was open for 1% -> 1% of each run, Pallas kernels for 40% -> 38%
where the time goes in v3:
time: 79.8 us; the launch traced here: 79.5 us
  Pallas kernels  31.4 us (39%)
  starting transfers between devices  23.8 us (30%)
  waiting for transfers between devices  21.1 us (26%)
  between operations  2.2 us (3%)
  other arithmetic  1.01 us (1%)
    pallas_call x9, Pallas kernels, kernel_call(): pl.pallas_call(kernel, out_shape=shapes, in_specs=specs, out_specs=out_sp...  31.4 us
    ppermute x18, starting transfers between devices, hop(): return lax.ppermute(x, axis, [(i, i ^ k) for i in range(n)])  16.9 us
    ppermute x18, waiting for transfers between devices, hop(): return lax.ppermute(x, axis, [(i, i ^ k) for i in range(n)])  14.2 us
    all_to_all x1, starting transfers between devices, per_device(): lax.all_to_all(sent, 'queue', split_axis=0, concat_axis=0, tiled=True)  6.83 us
    all_to_all x1, waiting for transfers between devices, per_device(): lax.all_to_all(sent, 'queue', split_axis=0, concat_axis=0, tiled=True)  6.83 us
  transfers between devices with their start and end apart: 19, of which 8 were waited for; matrix products, arithmetic and copies ran while one was open for 1% of the time, Pallas kernels for 38%

profile of v3, /device:TPU:0, one launch (start us, length us, event | category | flops | bytes accessed | tf_op | source)
XLA Modules:
  0.0 79.5 jit_solution(9590070972901785126)
XLA Ops:
  0.6 4.1 %collective-permute-start = (bf16[128,256]{1,0:T(8,128)(2,1)}, bf16[128,256]{1,0:T(8,128)(2,1)S(1)}, u32[]{:S(2)}, u32[]{:S(2)}) collective-permute-start(bf16[128,256]{1,0:T(8,128)(2,1)} %param.7), channel_id=1, source_target_pairs={{0,16},{4,20},{8,24},{12,28},{16,0},{20,4},{24,8},{28,12},{1,17},{... | collective-permute-start | bytes 196616 | tf_op jit(solution)/shard_map/ppermute | solution.py:279
  4.8 0.1 collective-permute-start.2
  4.8 1.0 %pad_select_fusion.qa_ref = bf16[256,256]{1,0:T(8,128)(2,1)S(1)} fusion(bf16[128,256]{1,0:T(8,128)(2,1)} %param.8, bf16[128,256]{1,0:T(8,128)(2,1)} %param.7, pred[256]{0:T(512)(128)(4,1)S(1)} %iota_compare_fusion), kind=kLoop, calls=%fused_computation.3 | loop fusion | flops 65536 | bytes 262400 | tf_op jit(solution)/shard_map/jit(_where)/select_n | solution.py:302
  5.8 1.9 %collective-permute-start.6 = (bf16[256,256]{1,0:T(8,128)(2,1)S(1)}, bf16[256,256]{1,0:T(8,128)(2,1)S(1)}, u32[]{:S(2)}, u32[]{:S(2)}) collective-permute-start(bf16[256,256]{1,0:T(8,128)(2,1)S(1)} %pad_select_fusion.qa_ref), channel_id=1, source_target_pairs={{0,8},{4,12},{8,0},{12,4},{16,24},{20,28},{24,16},{28,20},{1,9},{5... | collective-permute-start | bytes 393224 | tf_op jit(solution)/shard_map/ppermute | solution.py:279
  7.7 1.5 %collective-permute-start.5 = (bf16[256,256]{1,0:T(8,128)(2,1)S(1)}, bf16[256,256]{1,0:T(8,128)(2,1)S(1)}, u32[]{:S(2)}, u32[]{:S(2)}) collective-permute-start(bf16[256,256]{1,0:T(8,128)(2,1)S(1)} %pad_select_fusion.qa_ref), channel_id=1, source_target_pairs={{0,4},{4,0},{8,12},{12,8},{16,20},{20,16},{24,28},{28,24},{1,5},{5... | collective-permute-start | bytes 393224 | tf_op jit(solution)/shard_map/ppermute | solution.py:279
  9.3 1.5 %collective-permute-start.1 = (bf16[128,256]{1,0:T(8,128)(2,1)S(1)}, bf16[128,256]{1,0:T(8,128)(2,1)S(1)}, u32[]{:S(2)}, u32[]{:S(2)}) collective-permute-start(bf16[128,256]{1,0:T(8,128)(2,1)S(1)} %collective-permute-done.qa_ref), channel_id=1, source_target_pairs={{0,8},{4,12},{8,0},{12,4},{16,24},{20,28},{24,16},{28,20},{1,9},{5... | collective-permute-start | bytes 196616 | tf_op jit(solution)/shard_map/ppermute | solution.py:279
  10.8 0.2 collective-permute-done.2
  11.0 1.4 %collective-permute-start.3 = (bf16[128,256]{1,0:T(8,128)(2,1)S(1)}, bf16[128,256]{1,0:T(8,128)(2,1)S(1)}, u32[]{:S(2)}, u32[]{:S(2)}) collective-permute-start(bf16[128,256]{1,0:T(8,128)(2,1)S(1)} %collective-permute-done.2), channel_id=1, source_target_pairs={{0,8},{4,12},{8,0},{12,4},{16,24},{20,28},{24,16},{28,20},{1,9},{5... | collective-permute-start | bytes 196616 | tf_op jit(solution)/shard_map/ppermute | solution.py:279
  12.4 1.6 %collective-permute-start.8 = (bf16[256,256]{1,0:T(8,128)(2,1)S(1)}, bf16[256,256]{1,0:T(8,128)(2,1)S(1)}, u32[]{:S(2)}, u32[]{:S(2)}) collective-permute-start(bf16[256,256]{1,0:T(8,128)(2,1)S(1)} %pad_maximum_fusion.2), channel_id=1, source_target_pairs={{0,4},{4,0},{8,12},{12,8},{16,20},{20,16},{24,28},{28,24},{1,5},{5... | collective-permute-start | bytes 393224 | tf_op jit(solution)/shard_map/ppermute | solution.py:279
  14.0 0.4 collective-permute-done.1.qa_ref
  14.4 0.9 %collective-permute-done.3 = bf16[128,256]{1,0:T(8,128)(2,1)S(1)} collective-permute-done((bf16[128,256]{1,0:T(8,128)(2,1)S(1)}, bf16[128,256]{1,0:T(8,128)(2,1)S(1)}, u32[]{:S(2)}, u32[]{:S(2)}) %collective-permute-start.3) | collective-permute-done | bytes 65568 | tf_op jit(solution)/shard_map/ppermute | solution.py:279
  15.3 2.0 %collective-permute-start.4 = (bf16[256,256]{1,0:T(8,128)(2,1)S(1)}, bf16[256,256]{1,0:T(8,128)(2,1)S(1)}, u32[]{:S(2)}, u32[]{:S(2)}) collective-permute-start(bf16[256,256]{1,0:T(8,128)(2,1)S(1)} %pad_maximum_fusion.1), channel_id=1, source_target_pairs={{0,4},{4,0},{8,12},{12,8},{16,20},{20,16},{24,28},{28,24},{1,5},{5... | collective-permute-start | bytes 393224 | tf_op jit(solution)/shard_map/ppermute | solution.py:279
  17.3 0.1 collective-permute-start.7
  17.4 5.7 %collective-permute-done.7.qb_ref = bf16[256,256]{1,0:T(8,128)(2,1)S(1)} collective-permute-done((bf16[256,256]{1,0:T(8,128)(2,1)S(1)}, bf16[256,256]{1,0:T(8,128)(2,1)S(1)}, u32[]{:S(2)}, u32[]{:S(2)}) %collective-permute-start.7) | collective-permute-done | bytes 131104 | tf_op jit(solution)/shard_map/ppermute | solution.py:279
  23.1 1.6 %collective-permute-start.12 = (bf16[640,256]{1,0:T(8,128)(2,1)S(1)}, bf16[640,256]{1,0:T(8,128)(2,1)S(1)}, u32[]{:S(2)}, u32[]{:S(2)}) collective-permute-start(bf16[640,256]{1,0:T(8,128)(2,1)S(1)} %constant_dynamic-update-slice_fusion.refs_0_), channel_id=1, source_target_pairs={{0,2},{1,3},{2,0},{3,1},{4,6},{5,7},{6,4},{7,5},{8,10},{9,11},{10,... | collective-permute-start | bytes 983048 | tf_op jit(solution)/shard_map/ppermute | solution.py:279
  25.4 6.4 %shard_map.95 = (f32[3,256]{1,0:T(4,128)S(1)}, f32[1,128]{1,0:T(1,128)S(1)}) custom-call(f32[8,128]{1,0:T(8,128)S(1)} %shard_map.94._, f32[8,128]{1,0:T(8,128)S(1)} %broadcast_in_dim.2.rate_ref, s32[1,128]{1,0:T(1,128)S(1)} %bitcast.4, bf16[256,256]{1,0:T(8,128)(2,1)S(1)} %pad_select_fusion.qa_ref, bf16[256,256]{1,0:T(8,128)(2,1)S(1)} %collective-permute-done.5.qb_ref, ...), custom_call_target="tpu_custom_call" | custom-call | flops 536870912 | bytes 2097152 | tf_op jit(solution)/shard_map/pallas_call | solution.py:259
  31.9 0.1 collective-permute-start.15
  31.9 6.4 %shard_map.97.refs_2_ = f32[3,256]{1,0:T(4,128)S(1)} custom-call(f32[8,128]{1,0:T(8,128)S(1)} %broadcast_in_dim.2.rate_ref, bf16[128,256]{1,0:T(8,128)(2,1)S(1)} %collective-permute-done.qa_ref, bf16[256,256]{1,0:T(8,128)(2,1)S(1)} %collective-permute-done.8.qb_ref, bf16[4096,256]{1,0:T(8,128)(2,1)S(1)} %copy-done), custom_call_target="tpu_custom_call" | custom-call | flops 536870912 | bytes 2097152 | tf_op jit(solution)/shard_map/pallas_call | solution.py:259
  38.4 0.1 collective-permute-start.13
  38.4 0.5 collective-permute-start.14
  38.9 6.4 %shard_map.96.refs_1_ = f32[3,256]{1,0:T(4,128)S(1)} custom-call(f32[8,128]{1,0:T(8,128)S(1)} %broadcast_in_dim.2.rate_ref, bf16[256,256]{1,0:T(8,128)(2,1)S(1)} %collective-permute-done.6.qa_ref, bf16[256,256]{1,0:T(8,128)(2,1)S(1)} %collective-permute-done.7.qb_ref, bf16[4096,256]{1,0:T(8,128)(2,1)S(1)} %copy-done), custom_call_target="tpu_custom_call" | custom-call | flops 536870912 | bytes 2097152 | tf_op jit(solution)/shard_map/pallas_call | solution.py:259
  45.3 7.1 %shard_map.98 = f32[8,32,128]{2,1,0:T(8,128)} custom-call(f32[8,128]{1,0:T(8,128)S(1)} %broadcast_in_dim.2.rate_ref, bf16[128,256]{1,0:T(8,128)(2,1)S(1)} %collective-permute-done.1.qa_ref, bf16[256,256]{1,0:T(8,128)(2,1)S(1)} %collective-permute-done.4.qb_ref, bf16[4096,256]{1,0:T(8,128)(2,1)S(1)} %copy-done, f32[1,128]{1,0:T(1,128)S(1)} %get-tuple-element.7.pos_ref, ...), custom_call_target="tpu_custom_call" | custom-call | flops 536870912 | bytes 2097152 | tf_op jit(solution)/shard_map/pallas_call | solution.py:259
  52.4 6.8 %all-to-all-start = ((f32[8,32,128]{2,1,0:T(8,128)}), f32[8,32,128]{2,1,0:T(8,128)S(1)}, u32[]{:S(2)}, u32[]{:S(2)}) async-start(f32[8,32,128]{2,1,0:T(8,128)} %shard_map.98), calls=%async_computation | async-start | bytes 262144 | tf_op jit(solution)/shard_map/all_to_all | solution.py:365
  59.2 0.5 collective-permute-start.17
  59.7 6.8 %all-to-all-done.back_ref = f32[8,32,128]{2,1,0:T(8,128)S(1)} async-done(((f32[8,32,128]{2,1,0:T(8,128)}), f32[8,32,128]{2,1,0:T(8,128)S(1)}, u32[]{:S(2)}, u32[]{:S(2)}) %all-to-all-start) | async-done | bytes 131104 | tf_op jit(solution)/shard_map/all_to_all | solution.py:365
  66.6 0.6 shard_map.99
  67.1 1.2 %collective-permute-done.11.refs_3_ = f32[1,128]{1,0:T(1,128)S(1)} collective-permute-done((f32[1,128]{1,0:T(1,128)S(1)}, f32[1,128]{1,0:T(1,128)S(1)}, u32[]{:S(2)}, u32[]{:S(2)}) %collective-permute-start.11) | collective-permute-done | bytes 544 | tf_op jit(solution)/shard_map/ppermute | solution.py:279
  68.3 3.6 %collective-permute-done.10.refs_2_ = f32[1,128]{1,0:T(1,128)S(1)} collective-permute-done((f32[1,128]{1,0:T(1,128)S(1)}, f32[1,128]{1,0:T(1,128)S(1)}, u32[]{:S(2)}, u32[]{:S(2)}) %collective-permute-start.10) | collective-permute-done | bytes 544 | tf_op jit(solution)/shard_map/ppermute | solution.py:279
  72.5 2.3 %collective-permute-done.9.refs_1_ = f32[1,128]{1,0:T(1,128)S(1)} collective-permute-done((f32[1,128]{1,0:T(1,128)S(1)}, f32[1,128]{1,0:T(1,128)S(1)}, u32[]{:S(2)}, u32[]{:S(2)}) %collective-permute-start.9) | collective-permute-done | bytes 544 | tf_op jit(solution)/shard_map/ppermute | solution.py:279
  74.9 0.5 shard_map.100
  75.4 2.6 %shard_map.101.base_ref = bf16[4096,256]{1,0:T(8,128)(2,1)} custom-call(f32[3,256]{1,0:T(4,128)S(1)} %get-tuple-element.8.refs_0_._, s32[1]{0:T(128)S(6)} %copy.17.ptr, s32[32]{0:T(128)S(1)} %copy-done.1, bf16[4096,256]{1,0:T(8,128)(2,1)S(1)} %copy-done, bf16[640,256]{1,0:T(8,128)(2,1)S(1)} %constant_dynamic-update-slice_fusion.refs_0_, ...), custom_call_target="tpu_custom_call" | custom-call | flops 536870912 | bytes 2097152 | tf_op jit(solution)/shard_map/pallas_call | solution.py:259
  78.0 1.4 %shard_map.102 = bf16[4096,256]{1,0:T(8,128)(2,1)} custom-call(s32[1]{0:T(128)S(6)} %copy.17.ptr, s32[32]{0:T(128)S(1)} %copy-done.1, bf16[4096,256]{1,0:T(8,128)(2,1)} %shard_map.101.base_ref, bf16[384,256]{1,0:T(8,128)(2,1)S(1)} %pad_maximum_fusion.refs_0_, bf16[384,256]{1,0:T(8,128)(2,1)} %collective-permute-done.15.refs_1_, ...), custom_call_target="tpu_custom_call", output_to_operand_aliasing={{}: (2, {})} | custom-call | tf_op jit(solution)/shard_map/pallas_call | solution.py:259
  (34 shorter events, 0.1 us)
Async XLA Ops:
  0.6 8.6 %collective-permute-start = (bf16[128,256]{1,0:T(8,128)(2,1)}, bf16[128,256]{1,0:T(8,128)(2,1)S(1)}, u32[]{:S(2)}, u32[]{:S(2)}) collective-permute-start(bf16[128,256]{1,0:T(8,128)(2,1)} %param.7), channel_id=1, source_target_pairs={{0,16},{4,20},{8,24},{12,28},{16,0},{20,4},{24,8},{28,12},{1,17},{... | collective-permute-start | bytes 196616 | tf_op jit(solution)/shard_map/ppermute | solution.py:279
  4.8 6.2 %collective-permute-start.2 = (bf16[128,256]{1,0:T(8,128)(2,1)}, bf16[128,256]{1,0:T(8,128)(2,1)S(1)}, u32[]{:S(2)}, u32[]{:S(2)}) collective-permute-start(bf16[128,256]{1,0:T(8,128)(2,1)} %param.8), channel_id=1, source_target_pairs={{0,16},{4,20},{8,24},{12,28},{16,0},{20,4},{24,8},{28,12},{1,17},{... | collective-permute-start | bytes 196616 | tf_op jit(solution)/shard_map/ppermute | solution.py:279
  5.8 11.5 %collective-permute-start.6 = (bf16[256,256]{1,0:T(8,128)(2,1)S(1)}, bf16[256,256]{1,0:T(8,128)(2,1)S(1)}, u32[]{:S(2)}, u32[]{:S(2)}) collective-permute-start(bf16[256,256]{1,0:T(8,128)(2,1)S(1)} %pad_select_fusion.qa_ref), channel_id=1, source_target_pairs={{0,8},{4,12},{8,0},{12,4},{16,24},{20,28},{24,16},{28,20},{1,9},{5... | collective-permute-start | bytes 393224 | tf_op jit(solution)/shard_map/ppermute | solution.py:279
  7.7 9.7 %collective-permute-start.5 = (bf16[256,256]{1,0:T(8,128)(2,1)S(1)}, bf16[256,256]{1,0:T(8,128)(2,1)S(1)}, u32[]{:S(2)}, u32[]{:S(2)}) collective-permute-start(bf16[256,256]{1,0:T(8,128)(2,1)S(1)} %pad_select_fusion.qa_ref), channel_id=1, source_target_pairs={{0,4},{4,0},{8,12},{12,8},{16,20},{20,16},{24,28},{28,24},{1,5},{5... | collective-permute-start | bytes 393224 | tf_op jit(solution)/shard_map/ppermute | solution.py:279
  9.3 5.2 %collective-permute-start.1 = (bf16[128,256]{1,0:T(8,128)(2,1)S(1)}, bf16[128,256]{1,0:T(8,128)(2,1)S(1)}, u32[]{:S(2)}, u32[]{:S(2)}) collective-permute-start(bf16[128,256]{1,0:T(8,128)(2,1)S(1)} %collective-permute-done.qa_ref), channel_id=1, source_target_pairs={{0,8},{4,12},{8,0},{12,4},{16,24},{20,28},{24,16},{28,20},{1,9},{5... | collective-permute-start | bytes 196616 | tf_op jit(solution)/shard_map/ppermute | solution.py:279
  11.0 4.3 %collective-permute-start.3 = (bf16[128,256]{1,0:T(8,128)(2,1)S(1)}, bf16[128,256]{1,0:T(8,128)(2,1)S(1)}, u32[]{:S(2)}, u32[]{:S(2)}) collective-permute-start(bf16[128,256]{1,0:T(8,128)(2,1)S(1)} %collective-permute-done.2), channel_id=1, source_target_pairs={{0,8},{4,12},{8,0},{12,4},{16,24},{20,28},{24,16},{28,20},{1,9},{5... | collective-permute-start | bytes 196616 | tf_op jit(solution)/shard_map/ppermute | solution.py:279
  12.4 19.4 %collective-permute-start.8 = (bf16[256,256]{1,0:T(8,128)(2,1)S(1)}, bf16[256,256]{1,0:T(8,128)(2,1)S(1)}, u32[]{:S(2)}, u32[]{:S(2)}) collective-permute-start(bf16[256,256]{1,0:T(8,128)(2,1)S(1)} %pad_maximum_fusion.2), channel_id=1, source_target_pairs={{0,4},{4,0},{8,12},{12,8},{16,20},{20,16},{24,28},{28,24},{1,5},{5... | collective-permute-start | bytes 393224 | tf_op jit(solution)/shard_map/ppermute | solution.py:279
  15.3 16.5 %collective-permute-start.4 = (bf16[256,256]{1,0:T(8,128)(2,1)S(1)}, bf16[256,256]{1,0:T(8,128)(2,1)S(1)}, u32[]{:S(2)}, u32[]{:S(2)}) collective-permute-start(bf16[256,256]{1,0:T(8,128)(2,1)S(1)} %pad_maximum_fusion.1), channel_id=1, source_target_pairs={{0,4},{4,0},{8,12},{12,8},{16,20},{20,16},{24,28},{28,24},{1,5},{5... | collective-permute-start | bytes 393224 | tf_op jit(solution)/shard_map/ppermute | solution.py:279
  17.3 5.8 %collective-permute-start.7 = (bf16[256,256]{1,0:T(8,128)(2,1)S(1)}, bf16[256,256]{1,0:T(8,128)(2,1)S(1)}, u32[]{:S(2)}, u32[]{:S(2)}) collective-permute-start(bf16[256,256]{1,0:T(8,128)(2,1)S(1)} %collective-permute-done.6.qa_ref), channel_id=1, source_target_pairs={{0,4},{4,0},{8,12},{12,8},{16,20},{20,16},{24,28},{28,24},{1,5},{5... | collective-permute-start | bytes 393224 | tf_op jit(solution)/shard_map/ppermute | solution.py:279
  23.1 2.3 %copy-start = (bf16[4096,256]{1,0:T(8,128)(2,1)S(1)}, bf16[4096,256]{1,0:T(8,128)(2,1)}, u32[]{:S(2)}) copy-start(bf16[4096,256]{1,0:T(8,128)(2,1)} %k_ref.9) | copy-start | bytes 6291460
  23.1 2.3 %copy-start.2 = (s32[128]{0:T(128)S(1)}, s32[128]{0:T(128)}, u32[]{:S(2)}) copy-start(s32[128]{0:T(128)} %param.13) | copy-start | bytes 1540
  23.1 15.3 %collective-permute-start.12 = (bf16[640,256]{1,0:T(8,128)(2,1)S(1)}, bf16[640,256]{1,0:T(8,128)(2,1)S(1)}, u32[]{:S(2)}, u32[]{:S(2)}) collective-permute-start(bf16[640,256]{1,0:T(8,128)(2,1)S(1)} %constant_dynamic-update-slice_fusion.refs_0_), channel_id=1, source_target_pairs={{0,2},{1,3},{2,0},{3,1},{4,6},{5,7},{6,4},{7,5},{8,10},{9,11},{10,... | collective-permute-start | bytes 983048 | tf_op jit(solution)/shard_map/ppermute | solution.py:279
  31.9 27.4 %collective-permute-start.15 = (bf16[384,256]{1,0:T(8,128)(2,1)S(1)}, bf16[384,256]{1,0:T(8,128)(2,1)}, u32[]{:S(2)}, u32[]{:S(2)}) collective-permute-start(bf16[384,256]{1,0:T(8,128)(2,1)S(1)} %pad_maximum_fusion.refs_0_), channel_id=1, source_target_pairs={{0,2},{1,3},{2,0},{3,1},{4,6},{5,7},{6,4},{7,5},{8,10},{9,11},{10,... | collective-permute-start | bytes 589832 | tf_op jit(solution)/shard_map/ppermute | solution.py:279
  38.3 37.0 %copy-start.1 = (s32[32]{0:T(128)S(1)}, s32[32]{0:T(128)}, u32[]{:S(2)}) copy-start(s32[32]{0:T(128)} %block_order.3) | copy-start | bytes 388
  38.4 37.0 %collective-permute-start.13 = (bf16[640,256]{1,0:T(8,128)(2,1)S(1)}, bf16[640,256]{1,0:T(8,128)(2,1)S(1)}, u32[]{:S(2)}, u32[]{:S(2)}) collective-permute-start(bf16[640,256]{1,0:T(8,128)(2,1)S(1)} %constant_dynamic-update-slice_fusion.refs_0_), channel_id=1, source_target_pairs={{0,1},{1,0},{2,3},{3,2},{4,5},{5,4},{6,7},{7,6},{8,9},{9,8},{10,11... | collective-permute-start | bytes 983048 | tf_op jit(solution)/shard_map/ppermute | solution.py:279
  38.4 36.9 %collective-permute-start.14 = (bf16[640,256]{1,0:T(8,128)(2,1)S(1)}, bf16[640,256]{1,0:T(8,128)(2,1)}, u32[]{:S(2)}, u32[]{:S(2)}) collective-permute-start(bf16[640,256]{1,0:T(8,128)(2,1)S(1)} %collective-permute-done.12.refs_1_), channel_id=1, source_target_pairs={{0,1},{1,0},{2,3},{3,2},{4,5},{5,4},{6,7},{7,6},{8,9},{9,8},{10,11... | collective-permute-start | bytes 983048 | tf_op jit(solution)/shard_map/ppermute | solution.py:279
  52.4 14.2 %all-to-all-start = ((f32[8,32,128]{2,1,0:T(8,128)}), f32[8,32,128]{2,1,0:T(8,128)S(1)}, u32[]{:S(2)}, u32[]{:S(2)}) async-start(f32[8,32,128]{2,1,0:T(8,128)} %shard_map.98), calls=%async_computation | async-start | bytes 262144 | tf_op jit(solution)/shard_map/all_to_all | solution.py:365
  59.2 18.8 %collective-permute-start.16 = (bf16[384,256]{1,0:T(8,128)(2,1)S(1)}, bf16[384,256]{1,0:T(8,128)(2,1)}, u32[]{:S(2)}, u32[]{:S(2)}) collective-permute-start(bf16[384,256]{1,0:T(8,128)(2,1)S(1)} %pad_maximum_fusion.refs_0_), channel_id=1, source_target_pairs={{0,1},{1,0},{2,3},{3,2},{4,5},{5,4},{6,7},{7,6},{8,9},{9,8},{10,11... | collective-permute-start | bytes 589832 | tf_op jit(solution)/shard_map/ppermute | solution.py:279
  59.2 18.8 %collective-permute-start.17 = (bf16[384,256]{1,0:T(8,128)(2,1)}, bf16[384,256]{1,0:T(8,128)(2,1)}, u32[]{:S(2)}, u32[]{:S(2)}) collective-permute-start(bf16[384,256]{1,0:T(8,128)(2,1)} %collective-permute-done.15.refs_1_), channel_id=1, source_target_pairs={{0,1},{1,0},{2,3},{3,2},{4,5},{5,4},{6,7},{7,6},{8,9},{9,8},{10,11... | collective-permute-start | bytes 589832 | tf_op jit(solution)/shard_map/ppermute | solution.py:279
  67.1 1.2 %collective-permute-start.11 = (f32[1,128]{1,0:T(1,128)S(1)}, f32[1,128]{1,0:T(1,128)S(1)}, u32[]{:S(2)}, u32[]{:S(2)}) collective-permute-start(f32[1,128]{1,0:T(1,128)S(1)} %get-tuple-element.10.refs_0_), channel_id=1, source_target_pairs={{0,1},{1,0},{2,3},{3,2},{4,5},{5,4},{6,7},{7,6},{8,9},{9,8},{10,11... | collective-permute-start | bytes 1544 | tf_op jit(solution)/shard_map/ppermute | solution.py:279
  68.3 3.6 %collective-permute-start.10 = (f32[1,128]{1,0:T(1,128)S(1)}, f32[1,128]{1,0:T(1,128)S(1)}, u32[]{:S(2)}, u32[]{:S(2)}) collective-permute-start(f32[1,128]{1,0:T(1,128)S(1)} %get-tuple-element.10.refs_0_), channel_id=1, source_target_pairs={{0,2},{1,3},{2,0},{3,1},{4,6},{5,7},{6,4},{7,5},{8,10},{9,11},{10,... | collective-permute-start | bytes 1544 | tf_op jit(solution)/shard_map/ppermute | solution.py:279
  71.9 3.0 %collective-permute-start.9 = (f32[1,128]{1,0:T(1,128)S(1)}, f32[1,128]{1,0:T(1,128)S(1)}, u32[]{:S(2)}, u32[]{:S(2)}) collective-permute-start(f32[1,128]{1,0:T(1,128)S(1)} %get-tuple-element.10.refs_0_), channel_id=1, source_target_pairs={{0,3},{1,2},{2,1},{3,0},{4,7},{5,6},{6,5},{7,4},{8,11},{9,10},{10,... | collective-permute-start | bytes 1544 | tf_op jit(solution)/shard_map/ppermute | solution.py:279

commit v4 on v2

--- a/solution.py
+++ b/solution.py
@@ -33,9 +33,9 @@
     o_ref[2:3, :] = jnp.sum(w * a, axis=0, keepdims=True)
 
 
-def accumulate(log_scale, q, k_ref, o_ref):
+def accumulate(rate_ref, q, k_ref, o_ref):
     count, tiles = q.shape[0], k_ref.shape[0] // TILE
-    c = jnp.exp(jnp.broadcast_to(log_scale, (8, count))) * LOG2E
+    c = jnp.concatenate([rate_ref[...]] * (count // rate_ref.shape[1]), axis=1) * LOG2E
     d = scores_of(k_ref, q, 0)
     m = jnp.max(d, axis=0)
     e = jnp.exp2((d - m[None]) * c[None])
@@ -70,57 +70,62 @@
     o_ref[...] = jnp.zeros_like(o_ref)
 
 
-def first_kernel(_, ls_ref, index_ref, qa_ref, qb_ref, k_ref, o_ref, pos_ref):
+def first_kernel(_, rate_ref, index_ref, qa_ref, qb_ref, k_ref, o_ref, pos_ref):
     tok = qa_ref.shape[0] // 2
     scores = dot_t(qa_ref[tok:, :], qa_ref[:tok, :])
     rows = lax.broadcasted_iota(jnp.int32, scores.shape, 0)
     pos_ref[...] = jnp.sum(jnp.where(rows == index_ref[...], scores, 0.0), axis=0, keepdims=True)
-    accumulate(ls_ref[...], both(qa_ref, qb_ref, tok), k_ref, o_ref)
-
-
-def middle_kernel(ls_ref, qa_ref, qb_ref, k_ref, o_ref):
-    accumulate(ls_ref[...], both(qa_ref, qb_ref, o_ref.shape[1] // 2), k_ref, o_ref)
-
-
-def last_kernel(ls_ref, qa_ref, qb_ref, k_ref, pos_ref, *refs):
-    *parts, o_ref, hold, own = refs
-    n, tok = o_ref.shape[0], o_ref.shape[2]
+    accumulate(rate_ref, both(qa_ref, qb_ref, tok), k_ref, o_ref)
+
+
+def middle_kernel(rate_ref, qa_ref, qb_ref, k_ref, o_ref):
+    accumulate(rate_ref, both(qa_ref, qb_ref, o_ref.shape[1] // 2), k_ref, o_ref)
+
+
+def last_kernel(pairs, rate_ref, qa_ref, qb_ref, k_ref, pos_ref, *refs):
+    *parts, o_ref, own = refs
+    n, tok = o_ref.shape[0] // 4, o_ref.shape[1]
     me = lax.axis_index("queue")
-    hold[3 * n : 3 * n + 1, :] = pos_ref[...]
-    for k in range(n - 2):
-        at = jnp.bitwise_xor(me, k)
-        for i in range(3):
-            hold[pl.ds(i * n + at, 1), :] = parts[k // 2][i : i + 1, (k % 2) * tok : (k % 2 + 1) * tok]
-    accumulate(ls_ref[...], both(qa_ref, qb_ref, tok), k_ref, own)
-    for k in range(n - 2, n):
-        at = jnp.bitwise_xor(me, k)
-        for i in range(3):
-            hold[pl.ds(i * n + at, 1), :] = own[i : i + 1, (k % 2) * tok : (k % 2 + 1) * tok]
-    sent = hold[...]
-    for i in range(n):
-        o_ref[i] = sent
-
-
-def base_kernel(_, ptr_ref, order_ref, k_ref, base_ref, sem):
+    o_ref[3 * n :, :] = jnp.zeros((n, tok), jnp.float32)
+    o_ref[pl.ds(3 * n + me, 1), :] = pos_ref[...]
+
+    def lay(pair, part):
+        for j, k in enumerate(pair):
+            at = jnp.bitwise_xor(me, k)
+            for i in range(3):
+                o_ref[pl.ds(i * n + at, 1), :] = part[i : i + 1, j * tok : (j + 1) * tok]
+
+    for pair, part in zip(pairs, parts):
+        lay(pair, part)
+    accumulate(rate_ref, both(qa_ref, qb_ref, tok), k_ref, own)
+    lay(pairs[-1], own)
+
+
+def merge_kernel(rate_ref, a_ref, b_ref, o_ref):
+    n, tok = o_ref.shape[0] // 4, o_ref.shape[1]
+    scale = jnp.broadcast_to(rate_ref[0:1, :], (n, tok))
+    ours, theirs = a_ref[0:n, :], b_ref[0:n, :]
+    level = jnp.maximum(ours, theirs)
+    f, g = jnp.exp(scale * (ours - level)), jnp.exp(scale * (theirs - level))
+    o_ref[0:n, :] = level
+    o_ref[n : 2 * n, :] = a_ref[n : 2 * n, :] * f + b_ref[n : 2 * n, :] * g
+    o_ref[2 * n : 3 * n, :] = a_ref[2 * n : 3 * n, :] * f + b_ref[2 * n : 3 * n, :] * g
+    o_ref[3 * n :, :] = a_ref[3 * n :, :] + b_ref[3 * n :, :]
+
+
+def base_kernel(_, k_ref, base_ref, sem):
     copy = pltpu.make_async_copy(k_ref, base_ref, sem)
     copy.start()
     copy.wait()
 
 
-def final_kernel(ls_ref, back_ref, loss_ref, term_ref, hold_ref):
-    n, tok = back_ref.shape[0], back_ref.shape[2]
-    scale = jnp.exp(jnp.broadcast_to(ls_ref[...], (n, tok)))
-    pos = scale * back_ref[:, 3 * n, :]
-    peak = back_ref[0, 0:n, :]
-    for i in range(1, n):
-        peak = jnp.maximum(peak, back_ref[i, 0:n, :])
-    total = jnp.zeros((n, tok), jnp.float32)
-    weighted = jnp.zeros((n, tok), jnp.float32)
-    for i in range(n):
-        factor = jnp.exp(scale * (back_ref[i, 0:n, :] - peak))
-        total += back_ref[i, n : 2 * n, :] * factor
-        weighted += back_ref[i, 2 * n : 3 * n, :] * factor
-    peak = scale * peak
+def final_kernel(rate_ref, stats_ref, loss_ref, term_ref, hold_ref):
+    n, tok = stats_ref.shape[0] // 4, stats_ref.shape[1]
+    scale = jnp.broadcast_to(rate_ref[0:1, :], (n, tok))
+    peak = scale * stats_ref[0:n, :]
+    total = stats_ref[n : 2 * n, :]
+    weighted = stats_ref[2 * n : 3 * n, :]
+    pos = scale * stats_ref[3 * n :, :]
     highest = jnp.maximum(peak, pos)
     factor = jnp.exp(peak - highest)
     own = jnp.exp(pos - highest)
@@ -138,7 +143,7 @@
     o_ref[...] = sum((x[0:1, 0:1] for x in terms[1:]), terms[0][0:1, 0:1])
 
 
-def enqueue_kernel(n_queue, n_batch, order, ptr, block_order, base_ref, *refs):
+def enqueue_kernel(n_queue, n_batch, split, held, ptr, block_order, base_ref, *refs):
     *pieces, out_ref, sem = refs
     per_dev = out_ref.shape[0] // BLOCK
     total = per_dev * n_queue
@@ -162,9 +167,10 @@
         def _():
             dev = c // each
             dq, db = jnp.bitwise_xor(dev // n_batch, me_q), jnp.bitwise_xor(dev % n_batch, me_b)
-            at = jnp.where(dq < 4, dq, dq - 4) * each + c % each
-            for (b, p), piece in zip(order, pieces):
-                @pl.when((db == b) & (dq >= 4 if p else dq < 4))
+            late = dq >= split
+            at = jnp.where(late, dq - split, dq) * each + c % each
+            for (b, p), piece in zip(held, pieces):
+                @pl.when((db == b) & (late if p else jnp.logical_not(late)))
                 def _():
                     pltpu.make_async_copy(piece.at[rows(at)], out_ref.at[rows(slot)], sem.at[slot]).start()
 
@@ -181,8 +187,8 @@
 
     @pl.when((offset < per_dev) | (offset + count > total))
     def _():
-        lax.fori_loop(0, count, start, 0, unroll=4)
-        lax.fori_loop(0, count, finish, 0, unroll=4)
+        lax.fori_loop(0, count, start, 0)
+        lax.fori_loop(0, count, finish, 0)
 
 
 def kernel_call(kernel, operands, specs, shapes, out_specs, scratch=(), cost=None, **more):
@@ -202,6 +208,11 @@
     return sorted(range(2, n, 2), key=lambda k: (bin(k).count("1"), -k))
 
 
+def pairs_of(n):
+    early, late = range(4, n, 2), range(5, n, 2)
+    return [(0, 1), *zip(early[::2], early[1::2]), (2, 3), *zip(late[::2], late[1::2])]
+
+
 def per_device(n_queue, n_batch, queries, keys, queue_keys, log_scale, write_pointer, block_order, pos_index):
     tok, width = queries.shape
 
@@ -219,8 +230,9 @@
         bytes_accessed=queue_keys.size * 2,
         transcendentals=2 * tok * queue_keys.shape[0],
     )
-    ls = log_scale.reshape(1, 1)
-    opened = kernel_call(open_kernel, (), [], jax.ShapeDtypeStruct((8, 128), jnp.float32), VMEM, cost=cost)
+    rate = jnp.broadcast_to(jnp.exp(log_scale), (8, tok))
+    wait = pl.CostEstimate(flops=64 * cost.flops, bytes_accessed=4096, transcendentals=0)
+    opened = kernel_call(open_kernel, (), [], jax.ShapeDtypeStruct((8, 128), jnp.float32), VMEM, cost=wait)
 
     got = [None] * n_queue
     far = [k for k in evens(n_queue) if k > 2]
@@ -239,52 +251,55 @@
         got[k + 1] = across(jnp.concatenate([got[k], far_keys[k]], axis=0), 1)
         far_keys[k + 1] = got[k + 1][tok:]
 
-    pieces = {(0, 0): jnp.concatenate([x[tok:] for x in got[:4]], axis=0)}
-    if far:
-        pieces[0, 1] = jnp.concatenate([far_keys[k] for k in sorted(far_keys)], axis=0)
+    far_keys.update((k, x[tok:]) for k, x in enumerate(got[:4]))
+    split = max(5 * n_queue // 8, 1)
+    pieces = {(0, 0): jnp.concatenate([far_keys[k] for k in range(split)], axis=0)}
+    pieces[0, 1] = jnp.concatenate([far_keys[k] for k in range(split, n_queue)], axis=0)
     step = n_batch // 2
     while step:
         for (b, p), x in list(pieces.items()):
-            pieces[b ^ step, p] = beside(x, step)
+            k = step if p else step | 1
+            pieces[b ^ k, p] = beside(x, k)
         step //= 2
-    order = list(pieces)
-
+
+    pairs = pairs_of(n_queue)
     part_shape = jax.ShapeDtypeStruct((3, 2 * tok), jnp.float32)
     queue_shape = jax.ShapeDtypeStruct(queue_keys.shape, queue_keys.dtype)
     first, pos = kernel_call(
         first_kernel,
-        (opened, ls, pos_index.reshape(1, tok), got[0], got[1], queue_keys),
+        (opened, rate, pos_index.reshape(1, tok), got[0], got[1], queue_keys),
         [VMEM] * 6,
         (part_shape, jax.ShapeDtypeStruct((1, tok), jnp.float32)),
         (VMEM, VMEM),
         cost=cost,
     )
     parts = [first]
-    for k in range(2, n_queue - 2, 2):
+    for a, b in pairs[1:-1]:
         parts.append(
-            kernel_call(
-                middle_kernel, (ls, got[k], got[k + 1], queue_keys), [VMEM] + [VMEM] * 3, part_shape, VMEM, cost=cost
-            )
+            kernel_call(middle_kernel, (rate, got[a], got[b], queue_keys), [VMEM] * 4, part_shape, VMEM, cost=cost)
         )
-    sent = kernel_call(
-        last_kernel,
-        (ls, got[n_queue - 2], got[n_queue - 1], queue_keys, pos, *parts),
+    stats_shape = jax.ShapeDtypeStruct((4 * n_queue, tok), jnp.float32)
+    stats = kernel_call(
+        functools.partial(last_kernel, pairs),
+        (rate, got[pairs[-1][0]], got[pairs[-1][1]], queue_keys, pos, *parts),
         [VMEM] + [VMEM] * (4 + len(parts)),
-        jax.ShapeDtypeStruct((n_queue, 3 * n_queue + 8, tok), jnp.float32),
+        stats_shape,
         VMEM,
-        [
-            pltpu.VMEM((3 * n_queue + 8, tok), jnp.float32),
-            pltpu.VMEM((3, 2 * tok), jnp.float32),
-        ],
+        [pltpu.VMEM((3, 2 * tok), jnp.float32)],
         cost=cost,
     )
+    per_dev = queue_keys.shape[0] // BLOCK
     base = kernel_call(
-        base_kernel, (first, write_pointer, block_order, queue_keys), [HBM, SMEM, SMEM, VMEM], queue_shape, HBM, [pltpu.SemaphoreType.DMA], cost=cost
-    )
-    back = lax.all_to_all(sent, "queue", split_axis=0, concat_axis=0, tiled=True)
+        base_kernel, (first, queue_keys), [HBM, VMEM], queue_shape, HBM, [pltpu.SemaphoreType.DMA], cost=cost
+    )
+    k = 1
+    while k < n_queue:
+        came = across(stats, k)
+        stats = kernel_call(merge_kernel, (rate, stats, came), [VMEM] * 3, stats_shape, VMEM)
+        k *= 2
     loss, term = kernel_call(
         final_kernel,
-        (ls, back),
+        (rate, stats),
         [VMEM, VMEM],
         (jax.ShapeDtypeStruct((1, tok), jnp.float32), jax.ShapeDtypeStruct((1, tok), jnp.float32)),
         (VMEM, VMEM),
@@ -293,12 +308,12 @@
     terms = [term] + [beside(term, k) for k in range(n_batch - 1, 0, -1)]
     temp_grad = kernel_call(grad_kernel, terms, [VMEM] * n_batch, jax.ShapeDtypeStruct((1, 1), jnp.float32), VMEM)
     new_queue = kernel_call(
-        functools.partial(enqueue_kernel, n_queue, n_batch, order),
+        functools.partial(enqueue_kernel, n_queue, n_batch, split, list(pieces)),
         (write_pointer, block_order, base, *pieces.values()),
         [SMEM, SMEM, HBM] + [VMEM] * len(pieces),
         queue_shape,
         HBM,
-        [pltpu.SemaphoreType.DMA((queue_keys.shape[0] // BLOCK,))],
+        [pltpu.SemaphoreType.DMA((per_dev,))],
         input_output_aliases={2: 0},
     )
     return (loss.reshape(tok), temp_grad.reshape(1), new_queue)

time: 74.3 us -> 79.4 us (1.069)
  waiting for transfers between devices: 15.9 us -> 26.5 us
  starting transfers between devices: 24.3 us -> 20.6 us
  Pallas kernels: 30.7 us -> 28.9 us
    ppermute x18 -> x21, waiting for transfers between devices: 9.58 us -> 26.5 us  [hop(): return lax.ppermute(x, axis, [(i, i ^ k) for i in range(n)])]
    all_to_all x1 -> x0, waiting for transfers between devices: 6.31 us -> none  [per_device(): lax.all_to_all(sent, 'queue', split_axis=0, concat_axis=0, tiled=True)]
    all_to_all x1 -> x0, starting transfers between devices: 5.49 us -> none  [per_device(): lax.all_to_all(sent, 'queue', split_axis=0, concat_axis=0, tiled=True)]
    ppermute x18 -> x21, starting transfers between devices: 18.8 us -> 20.6 us  [hop(): return lax.ppermute(x, axis, [(i, i ^ k) for i in range(n)])]
    pallas_call x9 -> x12, Pallas kernels: 30.7 us -> 28.9 us  [kernel_call(): pl.pallas_call(kernel, out_shape=shapes, in_specs=specs, out_specs=out_sp...]
  transfers between devices with their start and end apart: 19 -> 21, of which waited for: 8 -> 10; matrix products, arithmetic and copies ran while one was open for 1% -> 1% of each run, Pallas kernels for 40% -> 35%
where the time goes in v4:
time: 79.4 us; the launch traced here: 79.2 us
  Pallas kernels  28.9 us (36%)
  waiting for transfers between devices  26.5 us (33%)
  starting transfers between devices  20.6 us (26%)
  between operations  2.19 us (3%)
  other arithmetic  1.01 us (1%)
    pallas_call x12, Pallas kernels, kernel_call(): pl.pallas_call(kernel, out_shape=shapes, in_specs=specs, out_specs=out_sp...  28.9 us
    ppermute x21, waiting for transfers between devices, hop(): return lax.ppermute(x, axis, [(i, i ^ k) for i in range(n)])  26.5 us
    ppermute x21, starting transfers between devices, hop(): return lax.ppermute(x, axis, [(i, i ^ k) for i in range(n)])  20.6 us
  transfers between devices with their start and end apart: 21, of which 10 were waited for; matrix products, arithmetic and copies ran while one was open for 1% of the time, Pallas kernels for 35%

profile of v4, /device:TPU:0, one launch (start us, length us, event | category | flops | bytes accessed | tf_op | source)
XLA Modules:
  0.0 79.2 jit_solution(7706959399341318245)
XLA Ops:
  0.6 4.1 %collective-permute-start = (bf16[128,256]{1,0:T(8,128)(2,1)}, bf16[128,256]{1,0:T(8,128)(2,1)S(1)}, u32[]{:S(2)}, u32[]{:S(2)}) collective-permute-start(bf16[128,256]{1,0:T(8,128)(2,1)} %param.7), channel_id=1, source_target_pairs={{0,16},{4,20},{8,24},{12,28},{16,0},{20,4},{24,8},{28,12},{1,17},{... | collective-permute-start | bytes 196616 | tf_op jit(solution)/shard_map/ppermute | solution.py:220
  4.8 1.0 %pad_select_fusion.qa_ref = bf16[256,256]{1,0:T(8,128)(2,1)S(1)} fusion(bf16[128,256]{1,0:T(8,128)(2,1)} %param.8, bf16[128,256]{1,0:T(8,128)(2,1)} %param.7, pred[256]{0:T(512)(128)(4,1)S(1)} %iota_compare_fusion), kind=kLoop, calls=%fused_computation.3 | loop fusion | flops 65536 | bytes 262400 | tf_op jit(solution)/shard_map/jit(_where)/select_n | solution.py:243
  5.8 1.9 %collective-permute-start.7 = (bf16[256,256]{1,0:T(8,128)(2,1)S(1)}, bf16[256,256]{1,0:T(8,128)(2,1)S(1)}, u32[]{:S(2)}, u32[]{:S(2)}) collective-permute-start(bf16[256,256]{1,0:T(8,128)(2,1)S(1)} %pad_select_fusion.qa_ref), channel_id=1, source_target_pairs={{0,8},{4,12},{8,0},{12,4},{16,24},{20,28},{24,16},{28,20},{1,9},{5... | collective-permute-start | bytes 393224 | tf_op jit(solution)/shard_map/ppermute | solution.py:220
  7.7 1.5 %collective-permute-start.6 = (bf16[256,256]{1,0:T(8,128)(2,1)S(1)}, bf16[256,256]{1,0:T(8,128)(2,1)S(1)}, u32[]{:S(2)}, u32[]{:S(2)}) collective-permute-start(bf16[256,256]{1,0:T(8,128)(2,1)S(1)} %pad_select_fusion.qa_ref), channel_id=1, source_target_pairs={{0,4},{4,0},{8,12},{12,8},{16,20},{20,16},{24,28},{28,24},{1,5},{5... | collective-permute-start | bytes 393224 | tf_op jit(solution)/shard_map/ppermute | solution.py:220
  9.3 1.8 %collective-permute-done.1 = bf16[128,256]{1,0:T(8,128)(2,1)S(1)} collective-permute-done((bf16[128,256]{1,0:T(8,128)(2,1)}, bf16[128,256]{1,0:T(8,128)(2,1)S(1)}, u32[]{:S(2)}, u32[]{:S(2)}) %collective-permute-start.1) | collective-permute-done | bytes 65568 | tf_op jit(solution)/shard_map/ppermute | solution.py:220
  11.0 2.0 %collective-permute-start.2 = (bf16[256,256]{1,0:T(8,128)(2,1)S(1)}, bf16[256,256]{1,0:T(8,128)(2,1)S(1)}, u32[]{:S(2)}, u32[]{:S(2)}) collective-permute-start(bf16[256,256]{1,0:T(8,128)(2,1)S(1)} %pad_maximum_fusion.1), channel_id=1, source_target_pairs={{0,4},{4,0},{8,12},{12,8},{16,20},{20,16},{24,28},{28,24},{1,5},{5... | collective-permute-start | bytes 393224 | tf_op jit(solution)/shard_map/ppermute | solution.py:220
  13.0 1.0 %collective-permute-start.3 = (bf16[128,256]{1,0:T(8,128)(2,1)S(1)}, bf16[128,256]{1,0:T(8,128)(2,1)S(1)}, u32[]{:S(2)}, u32[]{:S(2)}) collective-permute-start(bf16[128,256]{1,0:T(8,128)(2,1)S(1)} %collective-permute-done.qa_ref), channel_id=1, source_target_pairs={{0,8},{4,12},{8,0},{12,4},{16,24},{20,28},{24,16},{28,20},{1,9},{5... | collective-permute-start | bytes 196616 | tf_op jit(solution)/shard_map/ppermute | solution.py:220
  14.0 1.0 %collective-permute-start.4 = (bf16[128,256]{1,0:T(8,128)(2,1)S(1)}, bf16[128,256]{1,0:T(8,128)(2,1)S(1)}, u32[]{:S(2)}, u32[]{:S(2)}) collective-permute-start(bf16[128,256]{1,0:T(8,128)(2,1)S(1)} %collective-permute-done.1), channel_id=1, source_target_pairs={{0,8},{4,12},{8,0},{12,4},{16,24},{20,28},{24,16},{28,20},{1,9},{5... | collective-permute-start | bytes 196616 | tf_op jit(solution)/shard_map/ppermute | solution.py:220
  15.2 4.8 %collective-permute-done.8.qb_ref = bf16[256,256]{1,0:T(8,128)(2,1)S(1)} collective-permute-done((bf16[256,256]{1,0:T(8,128)(2,1)S(1)}, bf16[256,256]{1,0:T(8,128)(2,1)S(1)}, u32[]{:S(2)}, u32[]{:S(2)}) %collective-permute-start.8) | collective-permute-done | bytes 131104 | tf_op jit(solution)/shard_map/ppermute | solution.py:220
  20.1 0.9 %collective-permute-start.5 = (bf16[256,256]{1,0:T(8,128)(2,1)S(1)}, bf16[256,256]{1,0:T(8,128)(2,1)S(1)}, u32[]{:S(2)}, u32[]{:S(2)}) collective-permute-start(bf16[256,256]{1,0:T(8,128)(2,1)S(1)} %pad_maximum_fusion.2), channel_id=1, source_target_pairs={{0,4},{4,0},{8,12},{12,8},{16,20},{20,16},{24,28},{28,24},{1,5},{5... | collective-permute-start | bytes 393224 | tf_op jit(solution)/shard_map/ppermute | solution.py:220
  21.0 1.3 %collective-permute-start.17 = (bf16[640,256]{1,0:T(8,128)(2,1)S(1)}, bf16[640,256]{1,0:T(8,128)(2,1)S(1)}, u32[]{:S(2)}, u32[]{:S(2)}) collective-permute-start(bf16[640,256]{1,0:T(8,128)(2,1)S(1)} %constant_dynamic-update-slice_fusion.refs_0_), channel_id=1, source_target_pairs={{0,1},{1,0},{2,3},{3,2},{4,5},{5,4},{6,7},{7,6},{8,9},{9,8},{10,11... | collective-permute-start | bytes 983048 | tf_op jit(solution)/shard_map/ppermute | solution.py:220
  22.4 3.6 %collective-permute-done.5.qb_ref = bf16[256,256]{1,0:T(8,128)(2,1)S(1)} collective-permute-done((bf16[256,256]{1,0:T(8,128)(2,1)S(1)}, bf16[256,256]{1,0:T(8,128)(2,1)S(1)}, u32[]{:S(2)}, u32[]{:S(2)}) %collective-permute-start.5) | collective-permute-done | bytes 131104 | tf_op jit(solution)/shard_map/ppermute | solution.py:220
  26.0 1.8 %collective-permute-start.16 = (bf16[384,256]{1,0:T(8,128)(2,1)S(1)}, bf16[384,256]{1,0:T(8,128)(2,1)S(1)}, u32[]{:S(2)}, u32[]{:S(2)}) collective-permute-start(bf16[384,256]{1,0:T(8,128)(2,1)S(1)} %pad_maximum_fusion.refs_1_), channel_id=1, source_target_pairs={{0,2},{1,3},{2,0},{3,1},{4,6},{5,7},{6,4},{7,5},{8,10},{9,11},{10,... | collective-permute-start | bytes 589832 | tf_op jit(solution)/shard_map/ppermute | solution.py:220
  27.8 2.2 %collective-permute-done.15.refs_2_ = bf16[640,256]{1,0:T(8,128)(2,1)S(1)} collective-permute-done((bf16[640,256]{1,0:T(8,128)(2,1)S(1)}, bf16[640,256]{1,0:T(8,128)(2,1)S(1)}, u32[]{:S(2)}, u32[]{:S(2)}) %collective-permute-start.15) | collective-permute-done | bytes 327712 | tf_op jit(solution)/shard_map/ppermute | solution.py:220
  30.9 6.4 %shard_map.96.refs_1_ = f32[3,256]{1,0:T(4,128)S(1)} custom-call(f32[8,128]{1,0:T(8,128)S(1)} %broadcast_in_dim.2.rate_ref, bf16[128,256]{1,0:T(8,128)(2,1)S(1)} %collective-permute-done.qa_ref, bf16[128,256]{1,0:T(8,128)(2,1)S(1)} %collective-permute-done.3.qb_ref, bf16[4096,256]{1,0:T(8,128)(2,1)S(1)} %copy-done), custom_call_target="tpu_custom_call" | custom-call | flops 536870912 | bytes 2097152 | tf_op jit(solution)/shard_map/pallas_call | solution.py:195
  37.3 6.4 %shard_map.95 = (f32[3,256]{1,0:T(4,128)S(1)}, f32[1,128]{1,0:T(1,128)S(1)}) custom-call(f32[8,128]{1,0:T(8,128)S(1)} %shard_map.94._, f32[8,128]{1,0:T(8,128)S(1)} %broadcast_in_dim.2.rate_ref, s32[1,128]{1,0:T(1,128)S(1)} %bitcast.4, bf16[256,256]{1,0:T(8,128)(2,1)S(1)} %pad_select_fusion.qa_ref, bf16[256,256]{1,0:T(8,128)(2,1)S(1)} %collective-permute-done.6.qb_ref, ...), custom_call_target="tpu_custom_call" | custom-call | flops 536870912 | bytes 2097152 | tf_op jit(solution)/shard_map/pallas_call | solution.py:195
  43.9 0.5 collective-permute-start.20
  44.3 6.4 %shard_map.97.refs_2_ = f32[3,256]{1,0:T(4,128)S(1)} custom-call(f32[8,128]{1,0:T(8,128)S(1)} %broadcast_in_dim.2.rate_ref, bf16[256,256]{1,0:T(8,128)(2,1)S(1)} %collective-permute-done.7.qa_ref, bf16[256,256]{1,0:T(8,128)(2,1)S(1)} %collective-permute-done.8.qb_ref, bf16[4096,256]{1,0:T(8,128)(2,1)S(1)} %copy-done), custom_call_target="tpu_custom_call" | custom-call | flops 536870912 | bytes 2097152 | tf_op jit(solution)/shard_map/pallas_call | solution.py:195
  50.8 6.4 %shard_map.98.a_ref = f32[32,128]{1,0:T(8,128)S(1)} custom-call(f32[8,128]{1,0:T(8,128)S(1)} %broadcast_in_dim.2.rate_ref, bf16[256,256]{1,0:T(8,128)(2,1)S(1)} %collective-permute-done.2.qa_ref, bf16[256,256]{1,0:T(8,128)(2,1)S(1)} %collective-permute-done.5.qb_ref, bf16[4096,256]{1,0:T(8,128)(2,1)S(1)} %copy-done, f32[1,128]{1,0:T(1,128)S(1)} %get-tuple-element.7.pos_ref, ...), custom_call_target="tpu_custom_call" | custom-call | flops 536870912 | bytes 2097152 | tf_op jit(solution)/shard_map/pallas_call | solution.py:195
  57.2 0.8 %collective-permute-start.9 = (f32[32,128]{1,0:T(8,128)S(1)}, f32[32,128]{1,0:T(8,128)S(1)}, u32[]{:S(2)}, u32[]{:S(2)}) collective-permute-start(f32[32,128]{1,0:T(8,128)S(1)} %shard_map.98.a_ref), channel_id=1, source_target_pairs={{0,4},{4,0},{8,12},{12,8},{16,20},{20,16},{24,28},{28,24},{1,5},{5... | collective-permute-start | bytes 49160 | tf_op jit(solution)/shard_map/ppermute | solution.py:220
  58.0 3.0 %collective-permute-done.9.b_ref = f32[32,128]{1,0:T(8,128)S(1)} collective-permute-done((f32[32,128]{1,0:T(8,128)S(1)}, f32[32,128]{1,0:T(8,128)S(1)}, u32[]{:S(2)}, u32[]{:S(2)}) %collective-permute-start.9) | collective-permute-done | bytes 16416 | tf_op jit(solution)/shard_map/ppermute | solution.py:220
  61.0 1.1 %collective-permute-start.10 = (f32[32,128]{1,0:T(8,128)S(1)}, f32[32,128]{1,0:T(8,128)S(1)}, u32[]{:S(2)}, u32[]{:S(2)}) collective-permute-start(f32[32,128]{1,0:T(8,128)S(1)} %shard_map.99.a_ref), channel_id=1, source_target_pairs={{0,8},{4,12},{8,0},{12,4},{16,24},{20,28},{24,16},{28,20},{1,9},{5... | collective-permute-start | bytes 49160 | tf_op jit(solution)/shard_map/ppermute | solution.py:220
  62.1 2.7 %collective-permute-done.10.b_ref = f32[32,128]{1,0:T(8,128)S(1)} collective-permute-done((f32[32,128]{1,0:T(8,128)S(1)}, f32[32,128]{1,0:T(8,128)S(1)}, u32[]{:S(2)}, u32[]{:S(2)}) %collective-permute-start.10) | collective-permute-done | bytes 16416 | tf_op jit(solution)/shard_map/ppermute | solution.py:220
  64.8 2.1 %collective-permute-start.11 = (f32[32,128]{1,0:T(8,128)S(1)}, f32[32,128]{1,0:T(8,128)S(1)}, u32[]{:S(2)}, u32[]{:S(2)}) collective-permute-start(f32[32,128]{1,0:T(8,128)S(1)} %shard_map.100.a_ref), channel_id=1, source_target_pairs={{0,16},{4,20},{8,24},{12,28},{16,0},{20,4},{24,8},{28,12},{1,17},{... | collective-permute-start | bytes 49160 | tf_op jit(solution)/shard_map/ppermute | solution.py:220
  67.0 2.6 %collective-permute-done.11.b_ref = f32[32,128]{1,0:T(8,128)S(1)} collective-permute-done((f32[32,128]{1,0:T(8,128)S(1)}, f32[32,128]{1,0:T(8,128)S(1)}, u32[]{:S(2)}, u32[]{:S(2)}) %collective-permute-start.11) | collective-permute-done | bytes 16416 | tf_op jit(solution)/shard_map/ppermute | solution.py:220
  69.5 0.5 shard_map.102
  70.1 1.2 %collective-permute-done.14.refs_3_ = f32[1,128]{1,0:T(1,128)S(1)} collective-permute-done((f32[1,128]{1,0:T(1,128)S(1)}, f32[1,128]{1,0:T(1,128)S(1)}, u32[]{:S(2)}, u32[]{:S(2)}) %collective-permute-start.14) | collective-permute-done | bytes 544 | tf_op jit(solution)/shard_map/ppermute | solution.py:220
  71.9 2.9 %collective-permute-done.13.refs_2_ = f32[1,128]{1,0:T(1,128)S(1)} collective-permute-done((f32[1,128]{1,0:T(1,128)S(1)}, f32[1,128]{1,0:T(1,128)S(1)}, u32[]{:S(2)}, u32[]{:S(2)}) %collective-permute-start.13) | collective-permute-done | bytes 544 | tf_op jit(solution)/shard_map/ppermute | solution.py:220
  74.8 1.3 %shard_map.104.base_ref = bf16[4096,256]{1,0:T(8,128)(2,1)} custom-call(f32[3,256]{1,0:T(4,128)S(1)} %get-tuple-element.8.refs_0_._, bf16[4096,256]{1,0:T(8,128)(2,1)S(1)} %copy-done), custom_call_target="tpu_custom_call" | custom-call | flops 536870912 | bytes 2097152 | tf_op jit(solution)/shard_map/pallas_call | solution.py:195
  76.2 1.7 %collective-permute-done.12.refs_1_ = f32[1,128]{1,0:T(1,128)S(1)} collective-permute-done((f32[1,128]{1,0:T(1,128)S(1)}, f32[1,128]{1,0:T(1,128)S(1)}, u32[]{:S(2)}, u32[]{:S(2)}) %collective-permute-start.12) | collective-permute-done | bytes 544 | tf_op jit(solution)/shard_map/ppermute | solution.py:220
  77.8 0.5 shard_map.103
  78.4 0.9 %shard_map.105 = bf16[4096,256]{1,0:T(8,128)(2,1)} custom-call(s32[1]{0:T(128)S(6)} %copy.17.ptr, s32[32]{0:T(128)S(1)} %copy-done.2, bf16[4096,256]{1,0:T(8,128)(2,1)} %shard_map.104.base_ref, bf16[640,256]{1,0:T(8,128)(2,1)S(1)} %constant_dynamic-update-slice_fusion.refs_0_, ...), custom_call_target="tpu_custom_call", output_to_operand_aliasing={{}: (2, {})} | custom-call | tf_op jit(solution)/shard_map/pallas_call | solution.py:195
  (41 shorter events, 0.6 us)
Async XLA Ops:
  0.6 8.6 %collective-permute-start = (bf16[128,256]{1,0:T(8,128)(2,1)}, bf16[128,256]{1,0:T(8,128)(2,1)S(1)}, u32[]{:S(2)}, u32[]{:S(2)}) collective-permute-start(bf16[128,256]{1,0:T(8,128)(2,1)} %param.7), channel_id=1, source_target_pairs={{0,16},{4,20},{8,24},{12,28},{16,0},{20,4},{24,8},{28,12},{1,17},{... | collective-permute-start | bytes 196616 | tf_op jit(solution)/shard_map/ppermute | solution.py:220
  4.8 6.2 %collective-permute-start.1 = (bf16[128,256]{1,0:T(8,128)(2,1)}, bf16[128,256]{1,0:T(8,128)(2,1)S(1)}, u32[]{:S(2)}, u32[]{:S(2)}) collective-permute-start(bf16[128,256]{1,0:T(8,128)(2,1)} %param.8), channel_id=1, source_target_pairs={{0,16},{4,20},{8,24},{12,28},{16,0},{20,4},{24,8},{28,12},{1,17},{... | collective-permute-start | bytes 196616 | tf_op jit(solution)/shard_map/ppermute | solution.py:220
  5.8 9.2 %collective-permute-start.7 = (bf16[256,256]{1,0:T(8,128)(2,1)S(1)}, bf16[256,256]{1,0:T(8,128)(2,1)S(1)}, u32[]{:S(2)}, u32[]{:S(2)}) collective-permute-start(bf16[256,256]{1,0:T(8,128)(2,1)S(1)} %pad_select_fusion.qa_ref), channel_id=1, source_target_pairs={{0,8},{4,12},{8,0},{12,4},{16,24},{20,28},{24,16},{28,20},{1,9},{5... | collective-permute-start | bytes 393224 | tf_op jit(solution)/shard_map/ppermute | solution.py:220
  7.7 7.4 %collective-permute-start.6 = (bf16[256,256]{1,0:T(8,128)(2,1)S(1)}, bf16[256,256]{1,0:T(8,128)(2,1)S(1)}, u32[]{:S(2)}, u32[]{:S(2)}) collective-permute-start(bf16[256,256]{1,0:T(8,128)(2,1)S(1)} %pad_select_fusion.qa_ref), channel_id=1, source_target_pairs={{0,4},{4,0},{8,12},{12,8},{16,20},{20,16},{24,28},{28,24},{1,5},{5... | collective-permute-start | bytes 393224 | tf_op jit(solution)/shard_map/ppermute | solution.py:220
  11.0 10.0 %collective-permute-start.2 = (bf16[256,256]{1,0:T(8,128)(2,1)S(1)}, bf16[256,256]{1,0:T(8,128)(2,1)S(1)}, u32[]{:S(2)}, u32[]{:S(2)}) collective-permute-start(bf16[256,256]{1,0:T(8,128)(2,1)S(1)} %pad_maximum_fusion.1), channel_id=1, source_target_pairs={{0,4},{4,0},{8,12},{12,8},{16,20},{20,16},{24,28},{28,24},{1,5},{5... | collective-permute-start | bytes 393224 | tf_op jit(solution)/shard_map/ppermute | solution.py:220
  13.0 7.1 %collective-permute-start.3 = (bf16[128,256]{1,0:T(8,128)(2,1)S(1)}, bf16[128,256]{1,0:T(8,128)(2,1)S(1)}, u32[]{:S(2)}, u32[]{:S(2)}) collective-permute-start(bf16[128,256]{1,0:T(8,128)(2,1)S(1)} %collective-permute-done.qa_ref), channel_id=1, source_target_pairs={{0,8},{4,12},{8,0},{12,4},{16,24},{20,28},{24,16},{28,20},{1,9},{5... | collective-permute-start | bytes 196616 | tf_op jit(solution)/shard_map/ppermute | solution.py:220
  14.0 6.1 %collective-permute-start.4 = (bf16[128,256]{1,0:T(8,128)(2,1)S(1)}, bf16[128,256]{1,0:T(8,128)(2,1)S(1)}, u32[]{:S(2)}, u32[]{:S(2)}) collective-permute-start(bf16[128,256]{1,0:T(8,128)(2,1)S(1)} %collective-permute-done.1), channel_id=1, source_target_pairs={{0,8},{4,12},{8,0},{12,4},{16,24},{20,28},{24,16},{28,20},{1,9},{5... | collective-permute-start | bytes 196616 | tf_op jit(solution)/shard_map/ppermute | solution.py:220
  15.0 5.0 %collective-permute-start.8 = (bf16[256,256]{1,0:T(8,128)(2,1)S(1)}, bf16[256,256]{1,0:T(8,128)(2,1)S(1)}, u32[]{:S(2)}, u32[]{:S(2)}) collective-permute-start(bf16[256,256]{1,0:T(8,128)(2,1)S(1)} %collective-permute-done.7.qa_ref), channel_id=1, source_target_pairs={{0,4},{4,0},{8,12},{12,8},{16,20},{20,16},{24,28},{28,24},{1,5},{5... | collective-permute-start | bytes 393224 | tf_op jit(solution)/shard_map/ppermute | solution.py:220
  20.0 10.0 %collective-permute-start.15 = (bf16[640,256]{1,0:T(8,128)(2,1)S(1)}, bf16[640,256]{1,0:T(8,128)(2,1)S(1)}, u32[]{:S(2)}, u32[]{:S(2)}) collective-permute-start(bf16[640,256]{1,0:T(8,128)(2,1)S(1)} %constant_dynamic-update-slice_fusion.refs_0_), channel_id=1, source_target_pairs={{0,3},{1,2},{2,1},{3,0},{4,7},{5,6},{6,5},{7,4},{8,11},{9,10},{10,... | collective-permute-start | bytes 983048 | tf_op jit(solution)/shard_map/ppermute | solution.py:220
  20.1 5.8 %collective-permute-start.5 = (bf16[256,256]{1,0:T(8,128)(2,1)S(1)}, bf16[256,256]{1,0:T(8,128)(2,1)S(1)}, u32[]{:S(2)}, u32[]{:S(2)}) collective-permute-start(bf16[256,256]{1,0:T(8,128)(2,1)S(1)} %pad_maximum_fusion.2), channel_id=1, source_target_pairs={{0,4},{4,0},{8,12},{12,8},{16,20},{20,16},{24,28},{28,24},{1,5},{5... | collective-permute-start | bytes 393224 | tf_op jit(solution)/shard_map/ppermute | solution.py:220
  21.0 57.3 %collective-permute-start.17 = (bf16[640,256]{1,0:T(8,128)(2,1)S(1)}, bf16[640,256]{1,0:T(8,128)(2,1)S(1)}, u32[]{:S(2)}, u32[]{:S(2)}) collective-permute-start(bf16[640,256]{1,0:T(8,128)(2,1)S(1)} %constant_dynamic-update-slice_fusion.refs_0_), channel_id=1, source_target_pairs={{0,1},{1,0},{2,3},{3,2},{4,5},{5,4},{6,7},{7,6},{8,9},{9,8},{10,11... | collective-permute-start | bytes 983048 | tf_op jit(solution)/shard_map/ppermute | solution.py:220
  26.0 4.9 %copy-start = (bf16[4096,256]{1,0:T(8,128)(2,1)S(1)}, bf16[4096,256]{1,0:T(8,128)(2,1)}, u32[]{:S(2)}) copy-start(bf16[4096,256]{1,0:T(8,128)(2,1)} %k_ref.9) | copy-start | bytes 6291460
  26.0 17.8 %collective-permute-start.16 = (bf16[384,256]{1,0:T(8,128)(2,1)S(1)}, bf16[384,256]{1,0:T(8,128)(2,1)S(1)}, u32[]{:S(2)}, u32[]{:S(2)}) collective-permute-start(bf16[384,256]{1,0:T(8,128)(2,1)S(1)} %pad_maximum_fusion.refs_1_), channel_id=1, source_target_pairs={{0,2},{1,3},{2,0},{3,1},{4,6},{5,7},{6,4},{7,5},{8,10},{9,11},{10,... | collective-permute-start | bytes 589832 | tf_op jit(solution)/shard_map/ppermute | solution.py:220
  30.1 48.3 %collective-permute-start.19 = (bf16[640,256]{1,0:T(8,128)(2,1)S(1)}, bf16[640,256]{1,0:T(8,128)(2,1)S(1)}, u32[]{:S(2)}, u32[]{:S(2)}) collective-permute-start(bf16[640,256]{1,0:T(8,128)(2,1)S(1)} %collective-permute-done.15.refs_2_), channel_id=1, source_target_pairs={{0,1},{1,0},{2,3},{3,2},{4,5},{5,4},{6,7},{7,6},{8,9},{9,8},{10,11... | collective-permute-start | bytes 983048 | tf_op jit(solution)/shard_map/ppermute | solution.py:220
  30.2 7.2 %copy-start.1 = (s32[128]{0:T(128)S(1)}, s32[128]{0:T(128)}, u32[]{:S(2)}) copy-start(s32[128]{0:T(128)} %param.13) | copy-start | bytes 1540
  43.8 34.6 %collective-permute-start.18 = (bf16[384,256]{1,0:T(8,128)(2,1)S(1)}, bf16[384,256]{1,0:T(8,128)(2,1)S(1)}, u32[]{:S(2)}, u32[]{:S(2)}) collective-permute-start(bf16[384,256]{1,0:T(8,128)(2,1)S(1)} %pad_maximum_fusion.refs_1_), channel_id=1, source_target_pairs={{0,1},{1,0},{2,3},{3,2},{4,5},{5,4},{6,7},{7,6},{8,9},{9,8},{10,11... | collective-permute-start | bytes 589832 | tf_op jit(solution)/shard_map/ppermute | solution.py:220
  43.9 34.5 %collective-permute-start.20 = (bf16[384,256]{1,0:T(8,128)(2,1)S(1)}, bf16[384,256]{1,0:T(8,128)(2,1)S(1)}, u32[]{:S(2)}, u32[]{:S(2)}) collective-permute-start(bf16[384,256]{1,0:T(8,128)(2,1)S(1)} %collective-permute-done.16.refs_3_), channel_id=1, source_target_pairs={{0,1},{1,0},{2,3},{3,2},{4,5},{5,4},{6,7},{7,6},{8,9},{9,8},{10,11... | collective-permute-start | bytes 589832 | tf_op jit(solution)/shard_map/ppermute | solution.py:220
  57.2 3.8 %collective-permute-start.9 = (f32[32,128]{1,0:T(8,128)S(1)}, f32[32,128]{1,0:T(8,128)S(1)}, u32[]{:S(2)}, u32[]{:S(2)}) collective-permute-start(f32[32,128]{1,0:T(8,128)S(1)} %shard_map.98.a_ref), channel_id=1, source_target_pairs={{0,4},{4,0},{8,12},{12,8},{16,20},{20,16},{24,28},{28,24},{1,5},{5... | collective-permute-start | bytes 49160 | tf_op jit(solution)/shard_map/ppermute | solution.py:220
  61.0 3.8 %collective-permute-start.10 = (f32[32,128]{1,0:T(8,128)S(1)}, f32[32,128]{1,0:T(8,128)S(1)}, u32[]{:S(2)}, u32[]{:S(2)}) collective-permute-start(f32[32,128]{1,0:T(8,128)S(1)} %shard_map.99.a_ref), channel_id=1, source_target_pairs={{0,8},{4,12},{8,0},{12,4},{16,24},{20,28},{24,16},{28,20},{1,9},{5... | collective-permute-start | bytes 49160 | tf_op jit(solution)/shard_map/ppermute | solution.py:220
  64.8 4.7 %collective-permute-start.11 = (f32[32,128]{1,0:T(8,128)S(1)}, f32[32,128]{1,0:T(8,128)S(1)}, u32[]{:S(2)}, u32[]{:S(2)}) collective-permute-start(f32[32,128]{1,0:T(8,128)S(1)} %shard_map.100.a_ref), channel_id=1, source_target_pairs={{0,16},{4,20},{8,24},{12,28},{16,0},{20,4},{24,8},{28,12},{1,17},{... | collective-permute-start | bytes 49160 | tf_op jit(solution)/shard_map/ppermute | solution.py:220
  70.1 1.2 %collective-permute-start.14 = (f32[1,128]{1,0:T(1,128)S(1)}, f32[1,128]{1,0:T(1,128)S(1)}, u32[]{:S(2)}, u32[]{:S(2)}) collective-permute-start(f32[1,128]{1,0:T(1,128)S(1)} %get-tuple-element.10.refs_0_), channel_id=1, source_target_pairs={{0,1},{1,0},{2,3},{3,2},{4,5},{5,4},{6,7},{7,6},{8,9},{9,8},{10,11... | collective-permute-start | bytes 1544 | tf_op jit(solution)/shard_map/ppermute | solution.py:220
  71.3 3.6 %collective-permute-start.13 = (f32[1,128]{1,0:T(1,128)S(1)}, f32[1,128]{1,0:T(1,128)S(1)}, u32[]{:S(2)}, u32[]{:S(2)}) collective-permute-start(f32[1,128]{1,0:T(1,128)S(1)} %get-tuple-element.10.refs_0_), channel_id=1, source_target_pairs={{0,2},{1,3},{2,0},{3,1},{4,6},{5,7},{6,4},{7,5},{8,10},{9,11},{10,... | collective-permute-start | bytes 1544 | tf_op jit(solution)/shard_map/ppermute | solution.py:220
  71.9 6.4 %copy-start.2 = (s32[32]{0:T(128)S(1)}, s32[32]{0:T(128)}, u32[]{:S(2)}) copy-start(s32[32]{0:T(128)} %block_order.1) | copy-start | bytes 388
  74.8 3.0 %collective-permute-start.12 = (f32[1,128]{1,0:T(1,128)S(1)}, f32[1,128]{1,0:T(1,128)S(1)}, u32[]{:S(2)}, u32[]{:S(2)}) collective-permute-start(f32[1,128]{1,0:T(1,128)S(1)} %get-tuple-element.10.refs_0_), channel_id=1, source_target_pairs={{0,3},{1,2},{2,1},{3,0},{4,7},{5,6},{6,5},{7,4},{8,11},{9,10},{10,... | collective-permute-start | bytes 1544 | tf_op jit(solution)/shard_map/ppermute | solution.py:220

commit v5 on v4

--- a/solution.py
+++ b/solution.py
@@ -70,7 +70,7 @@
     o_ref[...] = jnp.zeros_like(o_ref)
 
 
-def first_kernel(_, rate_ref, index_ref, qa_ref, qb_ref, k_ref, o_ref, pos_ref):
+def first_kernel(_, __, rate_ref, index_ref, qa_ref, qb_ref, k_ref, o_ref, pos_ref):
     tok = qa_ref.shape[0] // 2
     scores = dot_t(qa_ref[tok:, :], qa_ref[:tok, :])
     rows = lax.broadcasted_iota(jnp.int32, scores.shape, 0)
@@ -113,7 +113,7 @@
     o_ref[3 * n :, :] = a_ref[3 * n :, :] + b_ref[3 * n :, :]
 
 
-def base_kernel(_, k_ref, base_ref, sem):
+def base_kernel(_, ptr_ref, k_ref, base_ref, sem):
     copy = pltpu.make_async_copy(k_ref, base_ref, sem)
     copy.start()
     copy.wait()
@@ -160,35 +160,27 @@
         at = offset + block_order[c]
         return jnp.where(at >= total, at - total, at)
 
-    def start(c, _):
-        slot = slot_of(c)
+    def start(b, p, piece, r, _):
+        dq = r // each + (split if p else 0)
+        dev = jnp.bitwise_xor(me_q, dq) * n_batch + jnp.bitwise_xor(me_b, b)
+        slot = slot_of(dev * each + r % each)
 
         @pl.when(slot < per_dev)
         def _():
-            dev = c // each
-            dq, db = jnp.bitwise_xor(dev // n_batch, me_q), jnp.bitwise_xor(dev % n_batch, me_b)
-            late = dq >= split
-            at = jnp.where(late, dq - split, dq) * each + c % each
-            for (b, p), piece in zip(held, pieces):
-                @pl.when((db == b) & (late if p else jnp.logical_not(late)))
-                def _():
-                    pltpu.make_async_copy(piece.at[rows(at)], out_ref.at[rows(slot)], sem.at[slot]).start()
+            pltpu.make_async_copy(piece.at[rows(r)], out_ref.at[rows(slot)], sem.at[slot]).start()
 
         return 0
 
-    def finish(c, _):
-        slot = slot_of(c)
-
-        @pl.when(slot < per_dev)
-        def _():
-            pltpu.make_async_copy(pieces[0].at[rows(0)], out_ref.at[rows(slot)], sem.at[slot]).wait()
-
+    def finish(slot, _):
+        pltpu.make_async_copy(pieces[0].at[rows(0)], out_ref.at[rows(slot)], sem.at[slot]).wait()
         return 0
 
     @pl.when((offset < per_dev) | (offset + count > total))
     def _():
-        lax.fori_loop(0, count, start, 0)
-        lax.fori_loop(0, count, finish, 0)
+        for (b, p), piece in zip(held, pieces):
+            lax.fori_loop(0, piece.shape[0] // BLOCK, functools.partial(start, b, p, piece), 0)
+        lax.fori_loop(jnp.minimum(offset, per_dev), jnp.minimum(offset + count, per_dev), finish, 0)
+        lax.fori_loop(0, jnp.maximum(offset + count - total, 0), finish, 0)
 
 
 def kernel_call(kernel, operands, specs, shapes, out_specs, scratch=(), cost=None, **more):
@@ -232,6 +224,7 @@
     )
     rate = jnp.broadcast_to(jnp.exp(log_scale), (8, tok))
     wait = pl.CostEstimate(flops=64 * cost.flops, bytes_accessed=4096, transcendentals=0)
+    gate = kernel_call(open_kernel, (), [], jax.ShapeDtypeStruct((8, 128), jnp.float32), VMEM)
     opened = kernel_call(open_kernel, (), [], jax.ShapeDtypeStruct((8, 128), jnp.float32), VMEM, cost=wait)
 
     got = [None] * n_queue
@@ -267,8 +260,8 @@
     queue_shape = jax.ShapeDtypeStruct(queue_keys.shape, queue_keys.dtype)
     first, pos = kernel_call(
         first_kernel,
-        (opened, rate, pos_index.reshape(1, tok), got[0], got[1], queue_keys),
-        [VMEM] * 6,
+        (opened, gate, rate, pos_index.reshape(1, tok), got[0], got[1], queue_keys),
+        [VMEM] * 7,
         (part_shape, jax.ShapeDtypeStruct((1, tok), jnp.float32)),
         (VMEM, VMEM),
         cost=cost,
@@ -290,7 +283,7 @@
     )
     per_dev = queue_keys.shape[0] // BLOCK
     base = kernel_call(
-        base_kernel, (first, queue_keys), [HBM, VMEM], queue_shape, HBM, [pltpu.SemaphoreType.DMA], cost=cost
+        base_kernel, (first, write_pointer, queue_keys), [HBM, SMEM, VMEM], queue_shape, HBM, [pltpu.SemaphoreType.DMA], cost=cost
     )
     k = 1
     while k < n_queue:

time: 79.4 us -> 79.4 us (level)
    pallas_call x12 -> x13, Pallas kernels: 28.9 us -> 28.9 us  [kernel_call(): pl.pallas_call(kernel, out_shape=shapes, in_specs=specs, out_specs=out_sp...]
where the time goes in v5:
time: 79.4 us; the launch traced here: 79.2 us
  Pallas kernels  28.9 us (36%)
  waiting for transfers between devices  26.5 us (33%)
  starting transfers between devices  20.6 us (26%)
  between operations  2.19 us (3%)
  other arithmetic  1.01 us (1%)
    pallas_call x13, Pallas kernels, kernel_call(): pl.pallas_call(kernel, out_shape=shapes, in_specs=specs, out_specs=out_sp...  28.9 us
    ppermute x21, waiting for transfers between devices, hop(): return lax.ppermute(x, axis, [(i, i ^ k) for i in range(n)])  26.5 us
    ppermute x21, starting transfers between devices, hop(): return lax.ppermute(x, axis, [(i, i ^ k) for i in range(n)])  20.6 us
  transfers between devices with their start and end apart: 21, of which 10 were waited for; matrix products, arithmetic and copies ran while one was open for 1% of the time, Pallas kernels for 35%

profile of v5, /device:TPU:0, one launch (start us, length us, event | category | flops | bytes accessed | tf_op | source)
XLA Modules:
  0.0 79.2 jit_solution(9488338106932026843)
XLA Ops:
  0.6 4.1 %collective-permute-start = (bf16[128,256]{1,0:T(8,128)(2,1)}, bf16[128,256]{1,0:T(8,128)(2,1)S(1)}, u32[]{:S(2)}, u32[]{:S(2)}) collective-permute-start(bf16[128,256]{1,0:T(8,128)(2,1)} %param.7), channel_id=1, source_target_pairs={{0,16},{4,20},{8,24},{12,28},{16,0},{20,4},{24,8},{28,12},{1,17},{... | collective-permute-start | bytes 196616 | tf_op jit(solution)/shard_map/ppermute | solution.py:212
  4.8 1.0 %pad_select_fusion.qa_ref = bf16[256,256]{1,0:T(8,128)(2,1)S(1)} fusion(bf16[128,256]{1,0:T(8,128)(2,1)} %param.8, bf16[128,256]{1,0:T(8,128)(2,1)} %param.7, pred[256]{0:T(512)(128)(4,1)S(1)} %iota_compare_fusion), kind=kLoop, calls=%fused_computation.3 | loop fusion | flops 65536 | bytes 262400 | tf_op jit(solution)/shard_map/jit(_where)/select_n | solution.py:236
  5.8 1.9 %collective-permute-start.7 = (bf16[256,256]{1,0:T(8,128)(2,1)S(1)}, bf16[256,256]{1,0:T(8,128)(2,1)S(1)}, u32[]{:S(2)}, u32[]{:S(2)}) collective-permute-start(bf16[256,256]{1,0:T(8,128)(2,1)S(1)} %pad_select_fusion.qa_ref), channel_id=1, source_target_pairs={{0,8},{4,12},{8,0},{12,4},{16,24},{20,28},{24,16},{28,20},{1,9},{5... | collective-permute-start | bytes 393224 | tf_op jit(solution)/shard_map/ppermute | solution.py:212
  7.7 1.5 %collective-permute-start.6 = (bf16[256,256]{1,0:T(8,128)(2,1)S(1)}, bf16[256,256]{1,0:T(8,128)(2,1)S(1)}, u32[]{:S(2)}, u32[]{:S(2)}) collective-permute-start(bf16[256,256]{1,0:T(8,128)(2,1)S(1)} %pad_select_fusion.qa_ref), channel_id=1, source_target_pairs={{0,4},{4,0},{8,12},{12,8},{16,20},{20,16},{24,28},{28,24},{1,5},{5... | collective-permute-start | bytes 393224 | tf_op jit(solution)/shard_map/ppermute | solution.py:212
  9.3 1.8 %collective-permute-done.1 = bf16[128,256]{1,0:T(8,128)(2,1)S(1)} collective-permute-done((bf16[128,256]{1,0:T(8,128)(2,1)}, bf16[128,256]{1,0:T(8,128)(2,1)S(1)}, u32[]{:S(2)}, u32[]{:S(2)}) %collective-permute-start.1) | collective-permute-done | bytes 65568 | tf_op jit(solution)/shard_map/ppermute | solution.py:212
  11.0 2.0 %collective-permute-start.2 = (bf16[256,256]{1,0:T(8,128)(2,1)S(1)}, bf16[256,256]{1,0:T(8,128)(2,1)S(1)}, u32[]{:S(2)}, u32[]{:S(2)}) collective-permute-start(bf16[256,256]{1,0:T(8,128)(2,1)S(1)} %pad_maximum_fusion.1), channel_id=1, source_target_pairs={{0,4},{4,0},{8,12},{12,8},{16,20},{20,16},{24,28},{28,24},{1,5},{5... | collective-permute-start | bytes 393224 | tf_op jit(solution)/shard_map/ppermute | solution.py:212
  13.0 1.0 %collective-permute-start.3 = (bf16[128,256]{1,0:T(8,128)(2,1)S(1)}, bf16[128,256]{1,0:T(8,128)(2,1)S(1)}, u32[]{:S(2)}, u32[]{:S(2)}) collective-permute-start(bf16[128,256]{1,0:T(8,128)(2,1)S(1)} %collective-permute-done.qa_ref), channel_id=1, source_target_pairs={{0,8},{4,12},{8,0},{12,4},{16,24},{20,28},{24,16},{28,20},{1,9},{5... | collective-permute-start | bytes 196616 | tf_op jit(solution)/shard_map/ppermute | solution.py:212
  14.0 1.0 %collective-permute-start.4 = (bf16[128,256]{1,0:T(8,128)(2,1)S(1)}, bf16[128,256]{1,0:T(8,128)(2,1)S(1)}, u32[]{:S(2)}, u32[]{:S(2)}) collective-permute-start(bf16[128,256]{1,0:T(8,128)(2,1)S(1)} %collective-permute-done.1), channel_id=1, source_target_pairs={{0,8},{4,12},{8,0},{12,4},{16,24},{20,28},{24,16},{28,20},{1,9},{5... | collective-permute-start | bytes 196616 | tf_op jit(solution)/shard_map/ppermute | solution.py:212
  15.2 4.8 %collective-permute-done.8.qb_ref = bf16[256,256]{1,0:T(8,128)(2,1)S(1)} collective-permute-done((bf16[256,256]{1,0:T(8,128)(2,1)S(1)}, bf16[256,256]{1,0:T(8,128)(2,1)S(1)}, u32[]{:S(2)}, u32[]{:S(2)}) %collective-permute-start.8) | collective-permute-done | bytes 131104 | tf_op jit(solution)/shard_map/ppermute | solution.py:212
  20.1 0.9 %collective-permute-start.5 = (bf16[256,256]{1,0:T(8,128)(2,1)S(1)}, bf16[256,256]{1,0:T(8,128)(2,1)S(1)}, u32[]{:S(2)}, u32[]{:S(2)}) collective-permute-start(bf16[256,256]{1,0:T(8,128)(2,1)S(1)} %pad_maximum_fusion.2), channel_id=1, source_target_pairs={{0,4},{4,0},{8,12},{12,8},{16,20},{20,16},{24,28},{28,24},{1,5},{5... | collective-permute-start | bytes 393224 | tf_op jit(solution)/shard_map/ppermute | solution.py:212
  21.0 1.3 %collective-permute-start.17 = (bf16[640,256]{1,0:T(8,128)(2,1)S(1)}, bf16[640,256]{1,0:T(8,128)(2,1)S(1)}, u32[]{:S(2)}, u32[]{:S(2)}) collective-permute-start(bf16[640,256]{1,0:T(8,128)(2,1)S(1)} %constant_dynamic-update-slice_fusion.refs_0_), channel_id=1, source_target_pairs={{0,1},{1,0},{2,3},{3,2},{4,5},{5,4},{6,7},{7,6},{8,9},{9,8},{10,11... | collective-permute-start | bytes 983048 | tf_op jit(solution)/shard_map/ppermute | solution.py:212
  22.4 3.6 %collective-permute-done.5.qb_ref = bf16[256,256]{1,0:T(8,128)(2,1)S(1)} collective-permute-done((bf16[256,256]{1,0:T(8,128)(2,1)S(1)}, bf16[256,256]{1,0:T(8,128)(2,1)S(1)}, u32[]{:S(2)}, u32[]{:S(2)}) %collective-permute-start.5) | collective-permute-done | bytes 131104 | tf_op jit(solution)/shard_map/ppermute | solution.py:212
  26.0 1.8 %collective-permute-start.16 = (bf16[384,256]{1,0:T(8,128)(2,1)S(1)}, bf16[384,256]{1,0:T(8,128)(2,1)S(1)}, u32[]{:S(2)}, u32[]{:S(2)}) collective-permute-start(bf16[384,256]{1,0:T(8,128)(2,1)S(1)} %pad_maximum_fusion.refs_1_), channel_id=1, source_target_pairs={{0,2},{1,3},{2,0},{3,1},{4,6},{5,7},{6,4},{7,5},{8,10},{9,11},{10,... | collective-permute-start | bytes 589832 | tf_op jit(solution)/shard_map/ppermute | solution.py:212
  27.8 2.2 %collective-permute-done.15.refs_2_ = bf16[640,256]{1,0:T(8,128)(2,1)S(1)} collective-permute-done((bf16[640,256]{1,0:T(8,128)(2,1)S(1)}, bf16[640,256]{1,0:T(8,128)(2,1)S(1)}, u32[]{:S(2)}, u32[]{:S(2)}) %collective-permute-start.15) | collective-permute-done | bytes 327712 | tf_op jit(solution)/shard_map/ppermute | solution.py:212
  30.9 6.4 %shard_map.97.refs_1_ = f32[3,256]{1,0:T(4,128)S(1)} custom-call(f32[8,128]{1,0:T(8,128)S(1)} %broadcast_in_dim.2.rate_ref, bf16[128,256]{1,0:T(8,128)(2,1)S(1)} %collective-permute-done.qa_ref, bf16[128,256]{1,0:T(8,128)(2,1)S(1)} %collective-permute-done.3.qb_ref, bf16[4096,256]{1,0:T(8,128)(2,1)S(1)} %copy-done), custom_call_target="tpu_custom_call" | custom-call | flops 536870912 | bytes 2097152 | tf_op jit(solution)/shard_map/pallas_call | solution.py:187
  37.3 6.4 %shard_map.96 = (f32[3,256]{1,0:T(4,128)S(1)}, f32[1,128]{1,0:T(1,128)S(1)}) custom-call(f32[8,128]{1,0:T(8,128)S(1)} %shard_map.94._, f32[8,128]{1,0:T(8,128)S(1)} %shard_map.95.__, f32[8,128]{1,0:T(8,128)S(1)} %broadcast_in_dim.2.rate_ref, s32[1,128]{1,0:T(1,128)S(1)} %bitcast.4, bf16[256,256]{1,0:T(8,128)(2,1)S(1)} %pad_select_fusion.qa_ref, ...), custom_call_target="tpu_custom_call" | custom-call | flops 536870912 | bytes 2097152 | tf_op jit(solution)/shard_map/pallas_call | solution.py:187
  43.9 0.5 collective-permute-start.20
  44.3 6.4 %shard_map.98.refs_2_ = f32[3,256]{1,0:T(4,128)S(1)} custom-call(f32[8,128]{1,0:T(8,128)S(1)} %broadcast_in_dim.2.rate_ref, bf16[256,256]{1,0:T(8,128)(2,1)S(1)} %collective-permute-done.7.qa_ref, bf16[256,256]{1,0:T(8,128)(2,1)S(1)} %collective-permute-done.8.qb_ref, bf16[4096,256]{1,0:T(8,128)(2,1)S(1)} %copy-done), custom_call_target="tpu_custom_call" | custom-call | flops 536870912 | bytes 2097152 | tf_op jit(solution)/shard_map/pallas_call | solution.py:187
  50.8 6.4 %shard_map.99.a_ref = f32[32,128]{1,0:T(8,128)S(1)} custom-call(f32[8,128]{1,0:T(8,128)S(1)} %broadcast_in_dim.2.rate_ref, bf16[256,256]{1,0:T(8,128)(2,1)S(1)} %collective-permute-done.2.qa_ref, bf16[256,256]{1,0:T(8,128)(2,1)S(1)} %collective-permute-done.5.qb_ref, bf16[4096,256]{1,0:T(8,128)(2,1)S(1)} %copy-done, f32[1,128]{1,0:T(1,128)S(1)} %get-tuple-element.7.pos_ref, ...), custom_call_target="tpu_custom_call" | custom-call | flops 536870912 | bytes 2097152 | tf_op jit(solution)/shard_map/pallas_call | solution.py:187
  57.2 0.8 %collective-permute-start.9 = (f32[32,128]{1,0:T(8,128)S(1)}, f32[32,128]{1,0:T(8,128)S(1)}, u32[]{:S(2)}, u32[]{:S(2)}) collective-permute-start(f32[32,128]{1,0:T(8,128)S(1)} %shard_map.99.a_ref), channel_id=1, source_target_pairs={{0,4},{4,0},{8,12},{12,8},{16,20},{20,16},{24,28},{28,24},{1,5},{5... | collective-permute-start | bytes 49160 | tf_op jit(solution)/shard_map/ppermute | solution.py:212
  58.0 3.0 %collective-permute-done.9.b_ref = f32[32,128]{1,0:T(8,128)S(1)} collective-permute-done((f32[32,128]{1,0:T(8,128)S(1)}, f32[32,128]{1,0:T(8,128)S(1)}, u32[]{:S(2)}, u32[]{:S(2)}) %collective-permute-start.9) | collective-permute-done | bytes 16416 | tf_op jit(solution)/shard_map/ppermute | solution.py:212
  61.0 1.1 %collective-permute-start.10 = (f32[32,128]{1,0:T(8,128)S(1)}, f32[32,128]{1,0:T(8,128)S(1)}, u32[]{:S(2)}, u32[]{:S(2)}) collective-permute-start(f32[32,128]{1,0:T(8,128)S(1)} %shard_map.100.a_ref), channel_id=1, source_target_pairs={{0,8},{4,12},{8,0},{12,4},{16,24},{20,28},{24,16},{28,20},{1,9},{5... | collective-permute-start | bytes 49160 | tf_op jit(solution)/shard_map/ppermute | solution.py:212
  62.1 2.7 %collective-permute-done.10.b_ref = f32[32,128]{1,0:T(8,128)S(1)} collective-permute-done((f32[32,128]{1,0:T(8,128)S(1)}, f32[32,128]{1,0:T(8,128)S(1)}, u32[]{:S(2)}, u32[]{:S(2)}) %collective-permute-start.10) | collective-permute-done | bytes 16416 | tf_op jit(solution)/shard_map/ppermute | solution.py:212
  64.8 2.1 %collective-permute-start.11 = (f32[32,128]{1,0:T(8,128)S(1)}, f32[32,128]{1,0:T(8,128)S(1)}, u32[]{:S(2)}, u32[]{:S(2)}) collective-permute-start(f32[32,128]{1,0:T(8,128)S(1)} %shard_map.101.a_ref), channel_id=1, source_target_pairs={{0,16},{4,20},{8,24},{12,28},{16,0},{20,4},{24,8},{28,12},{1,17},{... | collective-permute-start | bytes 49160 | tf_op jit(solution)/shard_map/ppermute | solution.py:212
  66.9 2.6 %collective-permute-done.11.b_ref = f32[32,128]{1,0:T(8,128)S(1)} collective-permute-done((f32[32,128]{1,0:T(8,128)S(1)}, f32[32,128]{1,0:T(8,128)S(1)}, u32[]{:S(2)}, u32[]{:S(2)}) %collective-permute-start.11) | collective-permute-done | bytes 16416 | tf_op jit(solution)/shard_map/ppermute | solution.py:212
  69.5 0.5 shard_map.103
  70.1 1.2 %collective-permute-done.14.refs_3_ = f32[1,128]{1,0:T(1,128)S(1)} collective-permute-done((f32[1,128]{1,0:T(1,128)S(1)}, f32[1,128]{1,0:T(1,128)S(1)}, u32[]{:S(2)}, u32[]{:S(2)}) %collective-permute-start.14) | collective-permute-done | bytes 544 | tf_op jit(solution)/shard_map/ppermute | solution.py:212
  71.9 2.9 %collective-permute-done.13.refs_2_ = f32[1,128]{1,0:T(1,128)S(1)} collective-permute-done((f32[1,128]{1,0:T(1,128)S(1)}, f32[1,128]{1,0:T(1,128)S(1)}, u32[]{:S(2)}, u32[]{:S(2)}) %collective-permute-start.13) | collective-permute-done | bytes 544 | tf_op jit(solution)/shard_map/ppermute | solution.py:212
  74.8 1.3 %shard_map.105.base_ref = bf16[4096,256]{1,0:T(8,128)(2,1)} custom-call(f32[3,256]{1,0:T(4,128)S(1)} %get-tuple-element.8.refs_0_._, s32[1]{0:T(128)S(6)} %copy.17.ptr_ref.ptr, bf16[4096,256]{1,0:T(8,128)(2,1)S(1)} %copy-done), custom_call_target="tpu_custom_call" | custom-call | flops 536870912 | bytes 2097152 | tf_op jit(solution)/shard_map/pallas_call | solution.py:187
  76.1 1.7 %collective-permute-done.12.refs_1_ = f32[1,128]{1,0:T(1,128)S(1)} collective-permute-done((f32[1,128]{1,0:T(1,128)S(1)}, f32[1,128]{1,0:T(1,128)S(1)}, u32[]{:S(2)}, u32[]{:S(2)}) %collective-permute-start.12) | collective-permute-done | bytes 544 | tf_op jit(solution)/shard_map/ppermute | solution.py:212
  77.8 0.5 shard_map.104
  78.4 0.9 %shard_map.106 = bf16[4096,256]{1,0:T(8,128)(2,1)} custom-call(s32[1]{0:T(128)S(6)} %copy.17.ptr_ref.ptr, s32[32]{0:T(128)S(1)} %copy-done.2, bf16[4096,256]{1,0:T(8,128)(2,1)} %shard_map.105.base_ref, bf16[640,256]{1,0:T(8,128)(2,1)S(1)} %constant_dynamic-update-slice_fusion.refs_0_, ...), custom_call_target="tpu_custom_call", output_to_operand_aliasing={{}: (2, {})} | custom-call | tf_op jit(solution)/shard_map/pallas_call | solution.py:187
  (42 shorter events, 0.6 us)
Async XLA Ops:
  0.6 8.6 %collective-permute-start = (bf16[128,256]{1,0:T(8,128)(2,1)}, bf16[128,256]{1,0:T(8,128)(2,1)S(1)}, u32[]{:S(2)}, u32[]{:S(2)}) collective-permute-start(bf16[128,256]{1,0:T(8,128)(2,1)} %param.7), channel_id=1, source_target_pairs={{0,16},{4,20},{8,24},{12,28},{16,0},{20,4},{24,8},{28,12},{1,17},{... | collective-permute-start | bytes 196616 | tf_op jit(solution)/shard_map/ppermute | solution.py:212
  4.8 6.2 %collective-permute-start.1 = (bf16[128,256]{1,0:T(8,128)(2,1)}, bf16[128,256]{1,0:T(8,128)(2,1)S(1)}, u32[]{:S(2)}, u32[]{:S(2)}) collective-permute-start(bf16[128,256]{1,0:T(8,128)(2,1)} %param.8), channel_id=1, source_target_pairs={{0,16},{4,20},{8,24},{12,28},{16,0},{20,4},{24,8},{28,12},{1,17},{... | collective-permute-start | bytes 196616 | tf_op jit(solution)/shard_map/ppermute | solution.py:212
  5.8 9.2 %collective-permute-start.7 = (bf16[256,256]{1,0:T(8,128)(2,1)S(1)}, bf16[256,256]{1,0:T(8,128)(2,1)S(1)}, u32[]{:S(2)}, u32[]{:S(2)}) collective-permute-start(bf16[256,256]{1,0:T(8,128)(2,1)S(1)} %pad_select_fusion.qa_ref), channel_id=1, source_target_pairs={{0,8},{4,12},{8,0},{12,4},{16,24},{20,28},{24,16},{28,20},{1,9},{5... | collective-permute-start | bytes 393224 | tf_op jit(solution)/shard_map/ppermute | solution.py:212
  7.7 7.4 %collective-permute-start.6 = (bf16[256,256]{1,0:T(8,128)(2,1)S(1)}, bf16[256,256]{1,0:T(8,128)(2,1)S(1)}, u32[]{:S(2)}, u32[]{:S(2)}) collective-permute-start(bf16[256,256]{1,0:T(8,128)(2,1)S(1)} %pad_select_fusion.qa_ref), channel_id=1, source_target_pairs={{0,4},{4,0},{8,12},{12,8},{16,20},{20,16},{24,28},{28,24},{1,5},{5... | collective-permute-start | bytes 393224 | tf_op jit(solution)/shard_map/ppermute | solution.py:212
  11.0 10.0 %collective-permute-start.2 = (bf16[256,256]{1,0:T(8,128)(2,1)S(1)}, bf16[256,256]{1,0:T(8,128)(2,1)S(1)}, u32[]{:S(2)}, u32[]{:S(2)}) collective-permute-start(bf16[256,256]{1,0:T(8,128)(2,1)S(1)} %pad_maximum_fusion.1), channel_id=1, source_target_pairs={{0,4},{4,0},{8,12},{12,8},{16,20},{20,16},{24,28},{28,24},{1,5},{5... | collective-permute-start | bytes 393224 | tf_op jit(solution)/shard_map/ppermute | solution.py:212
  13.0 7.1 %collective-permute-start.3 = (bf16[128,256]{1,0:T(8,128)(2,1)S(1)}, bf16[128,256]{1,0:T(8,128)(2,1)S(1)}, u32[]{:S(2)}, u32[]{:S(2)}) collective-permute-start(bf16[128,256]{1,0:T(8,128)(2,1)S(1)} %collective-permute-done.qa_ref), channel_id=1, source_target_pairs={{0,8},{4,12},{8,0},{12,4},{16,24},{20,28},{24,16},{28,20},{1,9},{5... | collective-permute-start | bytes 196616 | tf_op jit(solution)/shard_map/ppermute | solution.py:212
  14.0 6.1 %collective-permute-start.4 = (bf16[128,256]{1,0:T(8,128)(2,1)S(1)}, bf16[128,256]{1,0:T(8,128)(2,1)S(1)}, u32[]{:S(2)}, u32[]{:S(2)}) collective-permute-start(bf16[128,256]{1,0:T(8,128)(2,1)S(1)} %collective-permute-done.1), channel_id=1, source_target_pairs={{0,8},{4,12},{8,0},{12,4},{16,24},{20,28},{24,16},{28,20},{1,9},{5... | collective-permute-start | bytes 196616 | tf_op jit(solution)/shard_map/ppermute | solution.py:212
  15.0 5.0 %collective-permute-start.8 = (bf16[256,256]{1,0:T(8,128)(2,1)S(1)}, bf16[256,256]{1,0:T(8,128)(2,1)S(1)}, u32[]{:S(2)}, u32[]{:S(2)}) collective-permute-start(bf16[256,256]{1,0:T(8,128)(2,1)S(1)} %collective-permute-done.7.qa_ref), channel_id=1, source_target_pairs={{0,4},{4,0},{8,12},{12,8},{16,20},{20,16},{24,28},{28,24},{1,5},{5... | collective-permute-start | bytes 393224 | tf_op jit(solution)/shard_map/ppermute | solution.py:212
  20.0 10.0 %collective-permute-start.15 = (bf16[640,256]{1,0:T(8,128)(2,1)S(1)}, bf16[640,256]{1,0:T(8,128)(2,1)S(1)}, u32[]{:S(2)}, u32[]{:S(2)}) collective-permute-start(bf16[640,256]{1,0:T(8,128)(2,1)S(1)} %constant_dynamic-update-slice_fusion.refs_0_), channel_id=1, source_target_pairs={{0,3},{1,2},{2,1},{3,0},{4,7},{5,6},{6,5},{7,4},{8,11},{9,10},{10,... | collective-permute-start | bytes 983048 | tf_op jit(solution)/shard_map/ppermute | solution.py:212
  20.1 5.8 %collective-permute-start.5 = (bf16[256,256]{1,0:T(8,128)(2,1)S(1)}, bf16[256,256]{1,0:T(8,128)(2,1)S(1)}, u32[]{:S(2)}, u32[]{:S(2)}) collective-permute-start(bf16[256,256]{1,0:T(8,128)(2,1)S(1)} %pad_maximum_fusion.2), channel_id=1, source_target_pairs={{0,4},{4,0},{8,12},{12,8},{16,20},{20,16},{24,28},{28,24},{1,5},{5... | collective-permute-start | bytes 393224 | tf_op jit(solution)/shard_map/ppermute | solution.py:212
  21.0 57.3 %collective-permute-start.17 = (bf16[640,256]{1,0:T(8,128)(2,1)S(1)}, bf16[640,256]{1,0:T(8,128)(2,1)S(1)}, u32[]{:S(2)}, u32[]{:S(2)}) collective-permute-start(bf16[640,256]{1,0:T(8,128)(2,1)S(1)} %constant_dynamic-update-slice_fusion.refs_0_), channel_id=1, source_target_pairs={{0,1},{1,0},{2,3},{3,2},{4,5},{5,4},{6,7},{7,6},{8,9},{9,8},{10,11... | collective-permute-start | bytes 983048 | tf_op jit(solution)/shard_map/ppermute | solution.py:212
  26.0 4.9 %copy-start = (bf16[4096,256]{1,0:T(8,128)(2,1)S(1)}, bf16[4096,256]{1,0:T(8,128)(2,1)}, u32[]{:S(2)}) copy-start(bf16[4096,256]{1,0:T(8,128)(2,1)} %k_ref.9) | copy-start | bytes 6291460
  26.0 17.8 %collective-permute-start.16 = (bf16[384,256]{1,0:T(8,128)(2,1)S(1)}, bf16[384,256]{1,0:T(8,128)(2,1)S(1)}, u32[]{:S(2)}, u32[]{:S(2)}) collective-permute-start(bf16[384,256]{1,0:T(8,128)(2,1)S(1)} %pad_maximum_fusion.refs_1_), channel_id=1, source_target_pairs={{0,2},{1,3},{2,0},{3,1},{4,6},{5,7},{6,4},{7,5},{8,10},{9,11},{10,... | collective-permute-start | bytes 589832 | tf_op jit(solution)/shard_map/ppermute | solution.py:212
  30.1 48.3 %collective-permute-start.19 = (bf16[640,256]{1,0:T(8,128)(2,1)S(1)}, bf16[640,256]{1,0:T(8,128)(2,1)S(1)}, u32[]{:S(2)}, u32[]{:S(2)}) collective-permute-start(bf16[640,256]{1,0:T(8,128)(2,1)S(1)} %collective-permute-done.15.refs_2_), channel_id=1, source_target_pairs={{0,1},{1,0},{2,3},{3,2},{4,5},{5,4},{6,7},{7,6},{8,9},{9,8},{10,11... | collective-permute-start | bytes 983048 | tf_op jit(solution)/shard_map/ppermute | solution.py:212
  30.2 7.2 %copy-start.1 = (s32[128]{0:T(128)S(1)}, s32[128]{0:T(128)}, u32[]{:S(2)}) copy-start(s32[128]{0:T(128)} %param.13) | copy-start | bytes 1540
  43.8 34.6 %collective-permute-start.18 = (bf16[384,256]{1,0:T(8,128)(2,1)S(1)}, bf16[384,256]{1,0:T(8,128)(2,1)S(1)}, u32[]{:S(2)}, u32[]{:S(2)}) collective-permute-start(bf16[384,256]{1,0:T(8,128)(2,1)S(1)} %pad_maximum_fusion.refs_1_), channel_id=1, source_target_pairs={{0,1},{1,0},{2,3},{3,2},{4,5},{5,4},{6,7},{7,6},{8,9},{9,8},{10,11... | collective-permute-start | bytes 589832 | tf_op jit(solution)/shard_map/ppermute | solution.py:212
  43.9 34.5 %collective-permute-start.20 = (bf16[384,256]{1,0:T(8,128)(2,1)S(1)}, bf16[384,256]{1,0:T(8,128)(2,1)S(1)}, u32[]{:S(2)}, u32[]{:S(2)}) collective-permute-start(bf16[384,256]{1,0:T(8,128)(2,1)S(1)} %collective-permute-done.16.refs_3_), channel_id=1, source_target_pairs={{0,1},{1,0},{2,3},{3,2},{4,5},{5,4},{6,7},{7,6},{8,9},{9,8},{10,11... | collective-permute-start | bytes 589832 | tf_op jit(solution)/shard_map/ppermute | solution.py:212
  57.2 3.8 %collective-permute-start.9 = (f32[32,128]{1,0:T(8,128)S(1)}, f32[32,128]{1,0:T(8,128)S(1)}, u32[]{:S(2)}, u32[]{:S(2)}) collective-permute-start(f32[32,128]{1,0:T(8,128)S(1)} %shard_map.99.a_ref), channel_id=1, source_target_pairs={{0,4},{4,0},{8,12},{12,8},{16,20},{20,16},{24,28},{28,24},{1,5},{5... | collective-permute-start | bytes 49160 | tf_op jit(solution)/shard_map/ppermute | solution.py:212
  61.0 3.8 %collective-permute-start.10 = (f32[32,128]{1,0:T(8,128)S(1)}, f32[32,128]{1,0:T(8,128)S(1)}, u32[]{:S(2)}, u32[]{:S(2)}) collective-permute-start(f32[32,128]{1,0:T(8,128)S(1)} %shard_map.100.a_ref), channel_id=1, source_target_pairs={{0,8},{4,12},{8,0},{12,4},{16,24},{20,28},{24,16},{28,20},{1,9},{5... | collective-permute-start | bytes 49160 | tf_op jit(solution)/shard_map/ppermute | solution.py:212
  64.8 4.7 %collective-permute-start.11 = (f32[32,128]{1,0:T(8,128)S(1)}, f32[32,128]{1,0:T(8,128)S(1)}, u32[]{:S(2)}, u32[]{:S(2)}) collective-permute-start(f32[32,128]{1,0:T(8,128)S(1)} %shard_map.101.a_ref), channel_id=1, source_target_pairs={{0,16},{4,20},{8,24},{12,28},{16,0},{20,4},{24,8},{28,12},{1,17},{... | collective-permute-start | bytes 49160 | tf_op jit(solution)/shard_map/ppermute | solution.py:212
  70.1 1.2 %collective-permute-start.14 = (f32[1,128]{1,0:T(1,128)S(1)}, f32[1,128]{1,0:T(1,128)S(1)}, u32[]{:S(2)}, u32[]{:S(2)}) collective-permute-start(f32[1,128]{1,0:T(1,128)S(1)} %get-tuple-element.10.refs_0_), channel_id=1, source_target_pairs={{0,1},{1,0},{2,3},{3,2},{4,5},{5,4},{6,7},{7,6},{8,9},{9,8},{10,11... | collective-permute-start | bytes 1544 | tf_op jit(solution)/shard_map/ppermute | solution.py:212
  71.2 3.6 %collective-permute-start.13 = (f32[1,128]{1,0:T(1,128)S(1)}, f32[1,128]{1,0:T(1,128)S(1)}, u32[]{:S(2)}, u32[]{:S(2)}) collective-permute-start(f32[1,128]{1,0:T(1,128)S(1)} %get-tuple-element.10.refs_0_), channel_id=1, source_target_pairs={{0,2},{1,3},{2,0},{3,1},{4,6},{5,7},{6,4},{7,5},{8,10},{9,11},{10,... | collective-permute-start | bytes 1544 | tf_op jit(solution)/shard_map/ppermute | solution.py:212
  71.9 6.4 %copy-start.2 = (s32[32]{0:T(128)S(1)}, s32[32]{0:T(128)}, u32[]{:S(2)}) copy-start(s32[32]{0:T(128)} %block_order.1) | copy-start | bytes 388
  74.8 3.0 %collective-permute-start.12 = (f32[1,128]{1,0:T(1,128)S(1)}, f32[1,128]{1,0:T(1,128)S(1)}, u32[]{:S(2)}, u32[]{:S(2)}) collective-permute-start(f32[1,128]{1,0:T(1,128)S(1)} %get-tuple-element.10.refs_0_), channel_id=1, source_target_pairs={{0,3},{1,2},{2,1},{3,0},{4,7},{5,6},{6,5},{7,4},{8,11},{9,10},{10,... | collective-permute-start | bytes 1544 | tf_op jit(solution)/shard_map/ppermute | solution.py:212

commit v6 on v5

--- a/solution.py
+++ b/solution.py
@@ -241,8 +241,10 @@
     for k in far:
         low = k & -k
         far_keys[k] = across(far_keys[k - low] if k > low else keys, low)
-        got[k + 1] = across(jnp.concatenate([got[k], far_keys[k]], axis=0), 1)
-        far_keys[k + 1] = got[k + 1][tok:]
+        got[k + 1] = across(got[k], 1)
+    if far:
+        odd = across(jnp.concatenate([far_keys[k] for k in far], axis=0), 1)
+        far_keys.update((k + 1, odd[i * tok : (i + 1) * tok]) for i, k in enumerate(far))
 
     far_keys.update((k, x[tok:]) for k, x in enumerate(got[:4]))
     split = max(5 * n_queue // 8, 1)

time: 79.4 us -> 84.5 us (1.064)
  waiting for transfers between devices: 26.5 us -> 29.4 us
  starting transfers between devices: 20.6 us -> 22.7 us
    ppermute x21 -> x22, waiting for transfers between devices: 26.5 us -> 29.4 us  [hop(): return lax.ppermute(x, axis, [(i, i ^ k) for i in range(n)])]
    ppermute x21 -> x22, starting transfers between devices: 20.6 us -> 22.7 us  [hop(): return lax.ppermute(x, axis, [(i, i ^ k) for i in range(n)])]
  transfers between devices with their start and end apart: 21 -> 22, of which waited for: 10 -> 10; matrix products, arithmetic and copies ran while one was open for 1% -> 1% of each run, Pallas kernels for 35% -> 33%
where the time goes in v6:
time: 84.5 us; the launch traced here: 84.3 us
  waiting for transfers between devices  29.4 us (35%)
  Pallas kernels  29 us (34%)
  starting transfers between devices  22.7 us (27%)
  between operations  2.17 us (3%)
  other arithmetic  1 us (1%)
    ppermute x22, waiting for transfers between devices, hop(): return lax.ppermute(x, axis, [(i, i ^ k) for i in range(n)])  29.4 us
    pallas_call x13, Pallas kernels, kernel_call(): pl.pallas_call(kernel, out_shape=shapes, in_specs=specs, out_specs=out_sp...  29 us
    ppermute x22, starting transfers between devices, hop(): return lax.ppermute(x, axis, [(i, i ^ k) for i in range(n)])  22.7 us
  transfers between devices with their start and end apart: 22, of which 10 were waited for; matrix products, arithmetic and copies ran while one was open for 1% of the time, Pallas kernels for 33%

profile of v6, /device:TPU:0, one launch (start us, length us, event | category | flops | bytes accessed | tf_op | source)
XLA Modules:
  0.0 84.3 jit_solution(2029374040171158705)
XLA Ops:
  0.6 4.1 %collective-permute-start = (bf16[128,256]{1,0:T(8,128)(2,1)}, bf16[128,256]{1,0:T(8,128)(2,1)S(1)}, u32[]{:S(2)}, u32[]{:S(2)}) collective-permute-start(bf16[128,256]{1,0:T(8,128)(2,1)} %param.7), channel_id=1, source_target_pairs={{0,16},{4,20},{8,24},{12,28},{16,0},{20,4},{24,8},{28,12},{1,17},{... | collective-permute-start | bytes 196616 | tf_op jit(solution)/shard_map/ppermute | solution.py:212
  4.8 1.0 %pad_select_fusion.qa_ref = bf16[256,256]{1,0:T(8,128)(2,1)S(1)} fusion(bf16[128,256]{1,0:T(8,128)(2,1)} %param.8, bf16[128,256]{1,0:T(8,128)(2,1)} %param.7, pred[256]{0:T(512)(128)(4,1)S(1)} %iota_compare_fusion), kind=kLoop, calls=%fused_computation.2 | loop fusion | flops 65536 | bytes 262400 | tf_op jit(solution)/shard_map/jit(_where)/select_n | solution.py:236
  5.8 1.9 %collective-permute-start.5 = (bf16[256,256]{1,0:T(8,128)(2,1)S(1)}, bf16[256,256]{1,0:T(8,128)(2,1)S(1)}, u32[]{:S(2)}, u32[]{:S(2)}) collective-permute-start(bf16[256,256]{1,0:T(8,128)(2,1)S(1)} %pad_select_fusion.qa_ref), channel_id=1, source_target_pairs={{0,8},{4,12},{8,0},{12,4},{16,24},{20,28},{24,16},{28,20},{1,9},{5... | collective-permute-start | bytes 393224 | tf_op jit(solution)/shard_map/ppermute | solution.py:212
  7.7 1.5 %collective-permute-start.4 = (bf16[256,256]{1,0:T(8,128)(2,1)S(1)}, bf16[256,256]{1,0:T(8,128)(2,1)S(1)}, u32[]{:S(2)}, u32[]{:S(2)}) collective-permute-start(bf16[256,256]{1,0:T(8,128)(2,1)S(1)} %pad_select_fusion.qa_ref), channel_id=1, source_target_pairs={{0,4},{4,0},{8,12},{12,8},{16,20},{20,16},{24,28},{28,24},{1,5},{5... | collective-permute-start | bytes 393224 | tf_op jit(solution)/shard_map/ppermute | solution.py:212
  9.2 1.8 %collective-permute-done.13 = bf16[128,256]{1,0:T(8,128)(2,1)S(1)} collective-permute-done((bf16[128,256]{1,0:T(8,128)(2,1)}, bf16[128,256]{1,0:T(8,128)(2,1)S(1)}, u32[]{:S(2)}, u32[]{:S(2)}) %collective-permute-start.13) | collective-permute-done | bytes 65568 | tf_op jit(solution)/shard_map/ppermute | solution.py:212
  11.0 1.4 %collective-permute-start.14 = (bf16[128,256]{1,0:T(8,128)(2,1)S(1)}, bf16[128,256]{1,0:T(8,128)(2,1)S(1)}, u32[]{:S(2)}, u32[]{:S(2)}) collective-permute-start(bf16[128,256]{1,0:T(8,128)(2,1)S(1)} %collective-permute-done.13), channel_id=1, source_target_pairs={{0,8},{4,12},{8,0},{12,4},{16,24},{20,28},{24,16},{28,20},{1,9},{5... | collective-permute-start | bytes 196616 | tf_op jit(solution)/shard_map/ppermute | solution.py:212
  12.4 0.7 collective-permute-start.2
  13.1 2.9 %collective-permute-done.14 = bf16[128,256]{1,0:T(8,128)(2,1)S(1)} collective-permute-done((bf16[128,256]{1,0:T(8,128)(2,1)S(1)}, bf16[128,256]{1,0:T(8,128)(2,1)S(1)}, u32[]{:S(2)}, u32[]{:S(2)}) %collective-permute-start.14) | collective-permute-done | bytes 65568 | tf_op jit(solution)/shard_map/ppermute | solution.py:212
  16.0 1.6 %collective-permute-start.15 = (bf16[256,256]{1,0:T(8,128)(2,1)S(1)}, bf16[256,256]{1,0:T(8,128)(2,1)S(1)}, u32[]{:S(2)}, u32[]{:S(2)}) collective-permute-start(bf16[256,256]{1,0:T(8,128)(2,1)S(1)} %pad_maximum_fusion.1), channel_id=1, source_target_pairs={{0,4},{4,0},{8,12},{12,8},{16,20},{20,16},{24,28},{28,24},{1,5},{5... | collective-permute-start | bytes 393224 | tf_op jit(solution)/shard_map/ppermute | solution.py:212
  18.1 4.4 %collective-permute-done.6.qb_ref = bf16[256,256]{1,0:T(8,128)(2,1)S(1)} collective-permute-done((bf16[256,256]{1,0:T(8,128)(2,1)S(1)}, bf16[256,256]{1,0:T(8,128)(2,1)S(1)}, u32[]{:S(2)}, u32[]{:S(2)}) %collective-permute-start.6) | collective-permute-done | bytes 131104 | tf_op jit(solution)/shard_map/ppermute | solution.py:212
  22.6 1.6 %collective-permute-start.16 = (bf16[640,256]{1,0:T(8,128)(2,1)S(1)}, bf16[640,256]{1,0:T(8,128)(2,1)S(1)}, u32[]{:S(2)}, u32[]{:S(2)}) collective-permute-start(bf16[640,256]{1,0:T(8,128)(2,1)S(1)} %constant_dynamic-update-slice_fusion.refs_0_), channel_id=1, source_target_pairs={{0,3},{1,2},{2,1},{3,0},{4,7},{5,6},{6,5},{7,4},{8,11},{9,10},{10,... | collective-permute-start | bytes 983048 | tf_op jit(solution)/shard_map/ppermute | solution.py:212
  24.3 0.6 collective-permute-start.17
  24.9 7.4 %collective-permute-done.16.refs_2_ = bf16[640,256]{1,0:T(8,128)(2,1)S(1)} collective-permute-done((bf16[640,256]{1,0:T(8,128)(2,1)S(1)}, bf16[640,256]{1,0:T(8,128)(2,1)S(1)}, u32[]{:S(2)}, u32[]{:S(2)}) %collective-permute-start.16) | collective-permute-done | bytes 327712 | tf_op jit(solution)/shard_map/ppermute | solution.py:212
  32.3 0.8 collective-permute-start.20
  33.8 1.5 %collective-permute-start.1 = (bf16[128,256]{1,0:T(8,128)(2,1)S(1)}, bf16[128,256]{1,0:T(8,128)(2,1)S(1)}, u32[]{:S(2)}, u32[]{:S(2)}) collective-permute-start(bf16[128,256]{1,0:T(8,128)(2,1)S(1)} %collective-permute-done.qa_ref), channel_id=1, source_target_pairs={{0,4},{4,0},{8,12},{12,8},{16,20},{20,16},{24,28},{28,24},{1,5},{5... | collective-permute-start | bytes 196616 | tf_op jit(solution)/shard_map/ppermute | solution.py:212
  35.3 0.6 collective-permute-start.3
  35.9 6.4 %shard_map.97.refs_1_ = f32[3,256]{1,0:T(4,128)S(1)} custom-call(f32[8,128]{1,0:T(8,128)S(1)} %broadcast_in_dim.2.rate_ref, bf16[128,256]{1,0:T(8,128)(2,1)S(1)} %collective-permute-done.qa_ref, bf16[128,256]{1,0:T(8,128)(2,1)S(1)} %collective-permute-done.2.qb_ref, bf16[4096,256]{1,0:T(8,128)(2,1)S(1)} %copy-done), custom_call_target="tpu_custom_call" | custom-call | flops 536870912 | bytes 2097152 | tf_op jit(solution)/shard_map/pallas_call | solution.py:187
  42.4 6.4 %shard_map.96 = (f32[3,256]{1,0:T(4,128)S(1)}, f32[1,128]{1,0:T(1,128)S(1)}) custom-call(f32[8,128]{1,0:T(8,128)S(1)} %shard_map.94._, f32[8,128]{1,0:T(8,128)S(1)} %shard_map.95.__, f32[8,128]{1,0:T(8,128)S(1)} %broadcast_in_dim.2.rate_ref, s32[1,128]{1,0:T(1,128)S(1)} %bitcast.4, bf16[256,256]{1,0:T(8,128)(2,1)S(1)} %pad_select_fusion.qa_ref, ...), custom_call_target="tpu_custom_call" | custom-call | flops 536870912 | bytes 2097152 | tf_op jit(solution)/shard_map/pallas_call | solution.py:187
  49.4 6.4 %shard_map.98.refs_2_ = f32[3,256]{1,0:T(4,128)S(1)} custom-call(f32[8,128]{1,0:T(8,128)S(1)} %broadcast_in_dim.2.rate_ref, bf16[256,256]{1,0:T(8,128)(2,1)S(1)} %collective-permute-done.5.qa_ref, bf16[256,256]{1,0:T(8,128)(2,1)S(1)} %collective-permute-done.6.qb_ref, bf16[4096,256]{1,0:T(8,128)(2,1)S(1)} %copy-done), custom_call_target="tpu_custom_call" | custom-call | flops 536870912 | bytes 2097152 | tf_op jit(solution)/shard_map/pallas_call | solution.py:187
  55.9 6.4 %shard_map.99.a_ref = f32[32,128]{1,0:T(8,128)S(1)} custom-call(f32[8,128]{1,0:T(8,128)S(1)} %broadcast_in_dim.2.rate_ref, bf16[128,256]{1,0:T(8,128)(2,1)S(1)} %collective-permute-done.1.qa_ref, bf16[128,256]{1,0:T(8,128)(2,1)S(1)} %collective-permute-done.3.qb_ref, bf16[4096,256]{1,0:T(8,128)(2,1)S(1)} %copy-done, f32[1,128]{1,0:T(1,128)S(1)} %get-tuple-element.7.pos_ref, ...), custom_call_target="tpu_custom_call" | custom-call | flops 536870912 | bytes 2097152 | tf_op jit(solution)/shard_map/pallas_call | solution.py:187
  62.3 1.5 %collective-permute-start.7 = (f32[32,128]{1,0:T(8,128)S(1)}, f32[32,128]{1,0:T(8,128)S(1)}, u32[]{:S(2)}, u32[]{:S(2)}) collective-permute-start(f32[32,128]{1,0:T(8,128)S(1)} %shard_map.99.a_ref), channel_id=1, source_target_pairs={{0,4},{4,0},{8,12},{12,8},{16,20},{20,16},{24,28},{28,24},{1,5},{5... | collective-permute-start | bytes 49160 | tf_op jit(solution)/shard_map/ppermute | solution.py:212
  63.8 2.3 %collective-permute-done.7.b_ref = f32[32,128]{1,0:T(8,128)S(1)} collective-permute-done((f32[32,128]{1,0:T(8,128)S(1)}, f32[32,128]{1,0:T(8,128)S(1)}, u32[]{:S(2)}, u32[]{:S(2)}) %collective-permute-start.7) | collective-permute-done | bytes 16416 | tf_op jit(solution)/shard_map/ppermute | solution.py:212
  66.1 1.1 %collective-permute-start.8 = (f32[32,128]{1,0:T(8,128)S(1)}, f32[32,128]{1,0:T(8,128)S(1)}, u32[]{:S(2)}, u32[]{:S(2)}) collective-permute-start(f32[32,128]{1,0:T(8,128)S(1)} %shard_map.100.a_ref), channel_id=1, source_target_pairs={{0,8},{4,12},{8,0},{12,4},{16,24},{20,28},{24,16},{28,20},{1,9},{5... | collective-permute-start | bytes 49160 | tf_op jit(solution)/shard_map/ppermute | solution.py:212
  67.2 2.7 %collective-permute-done.8.b_ref = f32[32,128]{1,0:T(8,128)S(1)} collective-permute-done((f32[32,128]{1,0:T(8,128)S(1)}, f32[32,128]{1,0:T(8,128)S(1)}, u32[]{:S(2)}, u32[]{:S(2)}) %collective-permute-start.8) | collective-permute-done | bytes 16416 | tf_op jit(solution)/shard_map/ppermute | solution.py:212
  69.9 2.6 %collective-permute-start.9 = (f32[32,128]{1,0:T(8,128)S(1)}, f32[32,128]{1,0:T(8,128)S(1)}, u32[]{:S(2)}, u32[]{:S(2)}) collective-permute-start(f32[32,128]{1,0:T(8,128)S(1)} %shard_map.101.a_ref), channel_id=1, source_target_pairs={{0,16},{4,20},{8,24},{12,28},{16,0},{20,4},{24,8},{28,12},{1,17},{... | collective-permute-start | bytes 49160 | tf_op jit(solution)/shard_map/ppermute | solution.py:212
  72.6 2.1 %collective-permute-done.9.b_ref = f32[32,128]{1,0:T(8,128)S(1)} collective-permute-done((f32[32,128]{1,0:T(8,128)S(1)}, f32[32,128]{1,0:T(8,128)S(1)}, u32[]{:S(2)}, u32[]{:S(2)}) %collective-permute-start.9) | collective-permute-done | bytes 16416 | tf_op jit(solution)/shard_map/ppermute | solution.py:212
  74.6 0.5 shard_map.103
  75.2 1.2 %collective-permute-done.12.refs_3_ = f32[1,128]{1,0:T(1,128)S(1)} collective-permute-done((f32[1,128]{1,0:T(1,128)S(1)}, f32[1,128]{1,0:T(1,128)S(1)}, u32[]{:S(2)}, u32[]{:S(2)}) %collective-permute-start.12) | collective-permute-done | bytes 544 | tf_op jit(solution)/shard_map/ppermute | solution.py:212
  77.0 2.9 %collective-permute-done.11.refs_2_ = f32[1,128]{1,0:T(1,128)S(1)} collective-permute-done((f32[1,128]{1,0:T(1,128)S(1)}, f32[1,128]{1,0:T(1,128)S(1)}, u32[]{:S(2)}, u32[]{:S(2)}) %collective-permute-start.11) | collective-permute-done | bytes 544 | tf_op jit(solution)/shard_map/ppermute | solution.py:212
  79.9 1.3 %shard_map.105.base_ref = bf16[4096,256]{1,0:T(8,128)(2,1)} custom-call(f32[3,256]{1,0:T(4,128)S(1)} %get-tuple-element.8.refs_0_._, s32[1]{0:T(128)S(6)} %copy.17.ptr_ref.ptr, bf16[4096,256]{1,0:T(8,128)(2,1)S(1)} %copy-done), custom_call_target="tpu_custom_call" | custom-call | flops 536870912 | bytes 2097152 | tf_op jit(solution)/shard_map/pallas_call | solution.py:187
  81.3 1.7 %collective-permute-done.10.refs_1_ = f32[1,128]{1,0:T(1,128)S(1)} collective-permute-done((f32[1,128]{1,0:T(1,128)S(1)}, f32[1,128]{1,0:T(1,128)S(1)}, u32[]{:S(2)}, u32[]{:S(2)}) %collective-permute-start.10) | collective-permute-done | bytes 544 | tf_op jit(solution)/shard_map/ppermute | solution.py:212
  83.5 0.9 %shard_map.106 = bf16[4096,256]{1,0:T(8,128)(2,1)} custom-call(s32[1]{0:T(128)S(6)} %copy.17.ptr_ref.ptr, s32[32]{0:T(128)S(1)} %copy-done.2, bf16[4096,256]{1,0:T(8,128)(2,1)} %shard_map.105.base_ref, bf16[640,256]{1,0:T(8,128)(2,1)S(1)} %constant_dynamic-update-slice_fusion.refs_0_, ...), custom_call_target="tpu_custom_call", output_to_operand_aliasing={{}: (2, {})} | custom-call | tf_op jit(solution)/shard_map/pallas_call | solution.py:187
  (42 shorter events, 1.9 us)
Async XLA Ops:
  0.6 11.8 %collective-permute-start = (bf16[128,256]{1,0:T(8,128)(2,1)}, bf16[128,256]{1,0:T(8,128)(2,1)S(1)}, u32[]{:S(2)}, u32[]{:S(2)}) collective-permute-start(bf16[128,256]{1,0:T(8,128)(2,1)} %param.7), channel_id=1, source_target_pairs={{0,16},{4,20},{8,24},{12,28},{16,0},{20,4},{24,8},{28,12},{1,17},{... | collective-permute-start | bytes 196616 | tf_op jit(solution)/shard_map/ppermute | solution.py:212
  4.8 6.2 %collective-permute-start.13 = (bf16[128,256]{1,0:T(8,128)(2,1)}, bf16[128,256]{1,0:T(8,128)(2,1)S(1)}, u32[]{:S(2)}, u32[]{:S(2)}) collective-permute-start(bf16[128,256]{1,0:T(8,128)(2,1)} %param.8), channel_id=1, source_target_pairs={{0,16},{4,20},{8,24},{12,28},{16,0},{20,4},{24,8},{28,12},{1,17},{... | collective-permute-start | bytes 196616 | tf_op jit(solution)/shard_map/ppermute | solution.py:212
  5.8 11.7 %collective-permute-start.5 = (bf16[256,256]{1,0:T(8,128)(2,1)S(1)}, bf16[256,256]{1,0:T(8,128)(2,1)S(1)}, u32[]{:S(2)}, u32[]{:S(2)}) collective-permute-start(bf16[256,256]{1,0:T(8,128)(2,1)S(1)} %pad_select_fusion.qa_ref), channel_id=1, source_target_pairs={{0,8},{4,12},{8,0},{12,4},{16,24},{20,28},{24,16},{28,20},{1,9},{5... | collective-permute-start | bytes 393224 | tf_op jit(solution)/shard_map/ppermute | solution.py:212
  7.7 10.4 %collective-permute-start.4 = (bf16[256,256]{1,0:T(8,128)(2,1)S(1)}, bf16[256,256]{1,0:T(8,128)(2,1)S(1)}, u32[]{:S(2)}, u32[]{:S(2)}) collective-permute-start(bf16[256,256]{1,0:T(8,128)(2,1)S(1)} %pad_select_fusion.qa_ref), channel_id=1, source_target_pairs={{0,4},{4,0},{8,12},{12,8},{16,20},{20,16},{24,28},{28,24},{1,5},{5... | collective-permute-start | bytes 393224 | tf_op jit(solution)/shard_map/ppermute | solution.py:212
  11.0 5.0 %collective-permute-start.14 = (bf16[128,256]{1,0:T(8,128)(2,1)S(1)}, bf16[128,256]{1,0:T(8,128)(2,1)S(1)}, u32[]{:S(2)}, u32[]{:S(2)}) collective-permute-start(bf16[128,256]{1,0:T(8,128)(2,1)S(1)} %collective-permute-done.13), channel_id=1, source_target_pairs={{0,8},{4,12},{8,0},{12,4},{16,24},{20,28},{24,16},{28,20},{1,9},{5... | collective-permute-start | bytes 196616 | tf_op jit(solution)/shard_map/ppermute | solution.py:212
  12.4 22.9 %collective-permute-start.2 = (bf16[128,256]{1,0:T(8,128)(2,1)S(1)}, bf16[128,256]{1,0:T(8,128)(2,1)S(1)}, u32[]{:S(2)}, u32[]{:S(2)}) collective-permute-start(bf16[128,256]{1,0:T(8,128)(2,1)S(1)} %collective-permute-done.qa_ref), channel_id=1, source_target_pairs={{0,8},{4,12},{8,0},{12,4},{16,24},{20,28},{24,16},{28,20},{1,9},{5... | collective-permute-start | bytes 196616 | tf_op jit(solution)/shard_map/ppermute | solution.py:212
  16.0 8.2 %collective-permute-start.15 = (bf16[256,256]{1,0:T(8,128)(2,1)S(1)}, bf16[256,256]{1,0:T(8,128)(2,1)S(1)}, u32[]{:S(2)}, u32[]{:S(2)}) collective-permute-start(bf16[256,256]{1,0:T(8,128)(2,1)S(1)} %pad_maximum_fusion.1), channel_id=1, source_target_pairs={{0,4},{4,0},{8,12},{12,8},{16,20},{20,16},{24,28},{28,24},{1,5},{5... | collective-permute-start | bytes 393224 | tf_op jit(solution)/shard_map/ppermute | solution.py:212
  17.6 5.0 %collective-permute-start.6 = (bf16[256,256]{1,0:T(8,128)(2,1)S(1)}, bf16[256,256]{1,0:T(8,128)(2,1)S(1)}, u32[]{:S(2)}, u32[]{:S(2)}) collective-permute-start(bf16[256,256]{1,0:T(8,128)(2,1)S(1)} %collective-permute-done.5.qa_ref), channel_id=1, source_target_pairs={{0,4},{4,0},{8,12},{12,8},{16,20},{20,16},{24,28},{28,24},{1,5},{5... | collective-permute-start | bytes 393224 | tf_op jit(solution)/shard_map/ppermute | solution.py:212
  22.5 60.9 %collective-permute-start.18 = (bf16[640,256]{1,0:T(8,128)(2,1)S(1)}, bf16[640,256]{1,0:T(8,128)(2,1)S(1)}, u32[]{:S(2)}, u32[]{:S(2)}) collective-permute-start(bf16[640,256]{1,0:T(8,128)(2,1)S(1)} %constant_dynamic-update-slice_fusion.refs_0_), channel_id=1, source_target_pairs={{0,1},{1,0},{2,3},{3,2},{4,5},{5,4},{6,7},{7,6},{8,9},{9,8},{10,11... | collective-permute-start | bytes 983048 | tf_op jit(solution)/shard_map/ppermute | solution.py:212
  22.6 9.7 %collective-permute-start.16 = (bf16[640,256]{1,0:T(8,128)(2,1)S(1)}, bf16[640,256]{1,0:T(8,128)(2,1)S(1)}, u32[]{:S(2)}, u32[]{:S(2)}) collective-permute-start(bf16[640,256]{1,0:T(8,128)(2,1)S(1)} %constant_dynamic-update-slice_fusion.refs_0_), channel_id=1, source_target_pairs={{0,3},{1,2},{2,1},{3,0},{4,7},{5,6},{6,5},{7,4},{8,11},{9,10},{10,... | collective-permute-start | bytes 983048 | tf_op jit(solution)/shard_map/ppermute | solution.py:212
  24.3 11.7 %copy-start = (bf16[4096,256]{1,0:T(8,128)(2,1)S(1)}, bf16[4096,256]{1,0:T(8,128)(2,1)}, u32[]{:S(2)}) copy-start(bf16[4096,256]{1,0:T(8,128)(2,1)} %k_ref.9) | copy-start | bytes 6291460
  24.3 24.6 %collective-permute-start.17 = (bf16[384,256]{1,0:T(8,128)(2,1)S(1)}, bf16[384,256]{1,0:T(8,128)(2,1)S(1)}, u32[]{:S(2)}, u32[]{:S(2)}) collective-permute-start(bf16[384,256]{1,0:T(8,128)(2,1)S(1)} %pad_maximum_fusion.refs_1_), channel_id=1, source_target_pairs={{0,2},{1,3},{2,0},{3,1},{4,6},{5,7},{6,4},{7,5},{8,10},{9,11},{10,... | collective-permute-start | bytes 589832 | tf_op jit(solution)/shard_map/ppermute | solution.py:212
  32.3 51.1 %collective-permute-start.20 = (bf16[640,256]{1,0:T(8,128)(2,1)S(1)}, bf16[640,256]{1,0:T(8,128)(2,1)S(1)}, u32[]{:S(2)}, u32[]{:S(2)}) collective-permute-start(bf16[640,256]{1,0:T(8,128)(2,1)S(1)} %collective-permute-done.16.refs_2_), channel_id=1, source_target_pairs={{0,1},{1,0},{2,3},{3,2},{4,5},{5,4},{6,7},{7,6},{8,9},{9,8},{10,11... | collective-permute-start | bytes 983048 | tf_op jit(solution)/shard_map/ppermute | solution.py:212
  33.1 9.2 %copy-start.1 = (s32[128]{0:T(128)S(1)}, s32[128]{0:T(128)}, u32[]{:S(2)}) copy-start(s32[128]{0:T(128)} %param.13) | copy-start | bytes 1540
  33.8 15.0 %collective-permute-start.1 = (bf16[128,256]{1,0:T(8,128)(2,1)S(1)}, bf16[128,256]{1,0:T(8,128)(2,1)S(1)}, u32[]{:S(2)}, u32[]{:S(2)}) collective-permute-start(bf16[128,256]{1,0:T(8,128)(2,1)S(1)} %collective-permute-done.qa_ref), channel_id=1, source_target_pairs={{0,4},{4,0},{8,12},{12,8},{16,20},{20,16},{24,28},{28,24},{1,5},{5... | collective-permute-start | bytes 196616 | tf_op jit(solution)/shard_map/ppermute | solution.py:212
  35.3 20.5 %collective-permute-start.3 = (bf16[128,256]{1,0:T(8,128)(2,1)S(1)}, bf16[128,256]{1,0:T(8,128)(2,1)S(1)}, u32[]{:S(2)}, u32[]{:S(2)}) collective-permute-start(bf16[128,256]{1,0:T(8,128)(2,1)S(1)} %collective-permute-done.2.qb_ref), channel_id=1, source_target_pairs={{0,4},{4,0},{8,12},{12,8},{16,20},{20,16},{24,28},{28,24},{1,5},{5... | collective-permute-start | bytes 196616 | tf_op jit(solution)/shard_map/ppermute | solution.py:212
  48.8 34.6 %collective-permute-start.19 = (bf16[384,256]{1,0:T(8,128)(2,1)S(1)}, bf16[384,256]{1,0:T(8,128)(2,1)S(1)}, u32[]{:S(2)}, u32[]{:S(2)}) collective-permute-start(bf16[384,256]{1,0:T(8,128)(2,1)S(1)} %pad_maximum_fusion.refs_1_), channel_id=1, source_target_pairs={{0,1},{1,0},{2,3},{3,2},{4,5},{5,4},{6,7},{7,6},{8,9},{9,8},{10,11... | collective-permute-start | bytes 589832 | tf_op jit(solution)/shard_map/ppermute | solution.py:212
  48.9 34.5 %collective-permute-start.21 = (bf16[384,256]{1,0:T(8,128)(2,1)S(1)}, bf16[384,256]{1,0:T(8,128)(2,1)S(1)}, u32[]{:S(2)}, u32[]{:S(2)}) collective-permute-start(bf16[384,256]{1,0:T(8,128)(2,1)S(1)} %collective-permute-done.17.refs_3_), channel_id=1, source_target_pairs={{0,1},{1,0},{2,3},{3,2},{4,5},{5,4},{6,7},{7,6},{8,9},{9,8},{10,11... | collective-permute-start | bytes 589832 | tf_op jit(solution)/shard_map/ppermute | solution.py:212
  62.3 3.8 %collective-permute-start.7 = (f32[32,128]{1,0:T(8,128)S(1)}, f32[32,128]{1,0:T(8,128)S(1)}, u32[]{:S(2)}, u32[]{:S(2)}) collective-permute-start(f32[32,128]{1,0:T(8,128)S(1)} %shard_map.99.a_ref), channel_id=1, source_target_pairs={{0,4},{4,0},{8,12},{12,8},{16,20},{20,16},{24,28},{28,24},{1,5},{5... | collective-permute-start | bytes 49160 | tf_op jit(solution)/shard_map/ppermute | solution.py:212
  66.1 3.8 %collective-permute-start.8 = (f32[32,128]{1,0:T(8,128)S(1)}, f32[32,128]{1,0:T(8,128)S(1)}, u32[]{:S(2)}, u32[]{:S(2)}) collective-permute-start(f32[32,128]{1,0:T(8,128)S(1)} %shard_map.100.a_ref), channel_id=1, source_target_pairs={{0,8},{4,12},{8,0},{12,4},{16,24},{20,28},{24,16},{28,20},{1,9},{5... | collective-permute-start | bytes 49160 | tf_op jit(solution)/shard_map/ppermute | solution.py:212
  69.9 4.7 %collective-permute-start.9 = (f32[32,128]{1,0:T(8,128)S(1)}, f32[32,128]{1,0:T(8,128)S(1)}, u32[]{:S(2)}, u32[]{:S(2)}) collective-permute-start(f32[32,128]{1,0:T(8,128)S(1)} %shard_map.101.a_ref), channel_id=1, source_target_pairs={{0,16},{4,20},{8,24},{12,28},{16,0},{20,4},{24,8},{28,12},{1,17},{... | collective-permute-start | bytes 49160 | tf_op jit(solution)/shard_map/ppermute | solution.py:212
  75.2 1.2 %collective-permute-start.12 = (f32[1,128]{1,0:T(1,128)S(1)}, f32[1,128]{1,0:T(1,128)S(1)}, u32[]{:S(2)}, u32[]{:S(2)}) collective-permute-start(f32[1,128]{1,0:T(1,128)S(1)} %get-tuple-element.10.refs_0_), channel_id=1, source_target_pairs={{0,1},{1,0},{2,3},{3,2},{4,5},{5,4},{6,7},{7,6},{8,9},{9,8},{10,11... | collective-permute-start | bytes 1544 | tf_op jit(solution)/shard_map/ppermute | solution.py:212
  76.4 3.6 %collective-permute-start.11 = (f32[1,128]{1,0:T(1,128)S(1)}, f32[1,128]{1,0:T(1,128)S(1)}, u32[]{:S(2)}, u32[]{:S(2)}) collective-permute-start(f32[1,128]{1,0:T(1,128)S(1)} %get-tuple-element.10.refs_0_), channel_id=1, source_target_pairs={{0,2},{1,3},{2,0},{3,1},{4,6},{5,7},{6,4},{7,5},{8,10},{9,11},{10,... | collective-permute-start | bytes 1544 | tf_op jit(solution)/shard_map/ppermute | solution.py:212
  77.0 6.4 %copy-start.2 = (s32[32]{0:T(128)S(1)}, s32[32]{0:T(128)}, u32[]{:S(2)}) copy-start(s32[32]{0:T(128)} %block_order.1) | copy-start | bytes 388
  79.9 3.0 %collective-permute-start.10 = (f32[1,128]{1,0:T(1,128)S(1)}, f32[1,128]{1,0:T(1,128)S(1)}, u32[]{:S(2)}, u32[]{:S(2)}) collective-permute-start(f32[1,128]{1,0:T(1,128)S(1)} %get-tuple-element.10.refs_0_), channel_id=1, source_target_pairs={{0,3},{1,2},{2,1},{3,0},{4,7},{5,6},{6,5},{7,4},{8,11},{9,10},{10,... | collective-permute-start | bytes 1544 | tf_op jit(solution)/shard_map/ppermute | solution.py:212
